TPU v7x, 16 devices: a whole 2x2x2 slice. The times are simulated.
16 devices in a mesh: dp: 4 (over z, y), ep: 4 (over x, core).
Axes of the slice: x: 2, y: 2, z: 2, core: 2. Of those that a mesh axis runs over, the one named last changes fastest.
Arguments:
- hidden: bfloat16 [32768, 2304], P(('dp', 'ep')), parts along dimension 0
- ln_gamma: float32 [2304], replicated
- ln_beta: float32 [2304], replicated
- w_router: bfloat16 [2304, 8], replicated
- w_gate: bfloat16 [8, 2304, 5760], P('ep')
- w_up: bfloat16 [8, 2304, 5760], P('ep')
- w_down: bfloat16 [8, 5760, 2304], P('ep')
- choice: int32 [32768, 2], P(('dp', 'ep')), parts along dimension 0
- mask_first: int32 [32768, 8], P(('dp', 'ep')), parts along dimension 0
- mask_second: int32 [32768, 8], P(('dp', 'ep')), parts along dimension 0
Outputs:
- output: bfloat16 [32768, 2304], P(('dp', 'ep')), parts along dimension 0
There are 4 independent parts. A program takes and returns all parts, laid end to end along the dimension named above; an argument that names none is the same for every part.
All inputs are finite; a program needn't handle non-finite values.
Results may differ from a plain program's by a relative error of at most 0.001.
Values are sent between devices in bfloat16 or wider.
A program may use at most 1 GiB of HBM per device.

v0:
```python
import jax
import jax.numpy as jnp
from jax import lax
from jax.sharding import PartitionSpec as P

LN_EPS = 1e-5


def layer_norm(token_rows, ln_gamma, ln_beta):
    values = token_rows.astype(jnp.float32)
    centred = values - jnp.mean(values, axis=-1, keepdims=True)
    variance = jnp.mean(centred * centred, axis=-1, keepdims=True)
    return (centred * lax.rsqrt(variance + LN_EPS) * ln_gamma + ln_beta).astype(jnp.bfloat16)


def sparse_gates(normed, w_router, choice, mask_first, mask_second):
    scores = jnp.dot(normed, w_router, preferred_element_type=jnp.float32)
    expert_ids = jnp.arange(w_router.shape[1], dtype=jnp.int32)
    mask_pair = jnp.stack([mask_first, mask_second], axis=1) > 0
    soft_probs = jax.nn.softmax(jnp.where(mask_pair, scores[:, None, :], -jnp.inf), axis=-1)
    return jnp.sum(jnp.where(choice[:, :, None] == expert_ids, soft_probs, 0.0), axis=-1)


def copy_slots(choice, experts, capacity):
    expert_ids = jnp.arange(experts, dtype=jnp.int32)
    hit_count = (choice[..., None] == expert_ids).astype(jnp.int32)
    per_token = jnp.sum(hit_count, axis=-2)
    before = jnp.cumsum(per_token, axis=-2) - per_token
    position = jnp.sum(hit_count * before[..., None, :], axis=-1)
    return position, position < capacity


def expert_mlp(expert_in, w_gate, w_up, w_down):
    gate_proj = jnp.einsum("secd,edf->secf", expert_in, w_gate, preferred_element_type=jnp.float32)
    up_proj = jnp.einsum("secd,edf->secf", expert_in, w_up, preferred_element_type=jnp.float32)
    inner_act = (jax.nn.silu(gate_proj) * up_proj).astype(jnp.bfloat16)
    return jnp.einsum("secf,efd->secd", inner_act, w_down, preferred_element_type=jnp.float32).astype(jnp.bfloat16)


def solution(mesh):
    group_size = mesh.shape["ep"]
    rows_spec = P(("dp", "ep"))

    def device_step(hidden, ln_gamma, ln_beta, w_router, w_gate, w_up, w_down, choice, mask_first, mask_second):
        tokens, row_width = hidden.shape
        local_experts = w_gate.shape[0]
        experts = local_experts * group_size
        capacity = (10 * tokens + 4 * experts - 1) // (4 * experts)
        slot_count = experts * capacity
        normed = layer_norm(hidden, ln_gamma, ln_beta)
        gate_vals = sparse_gates(normed, w_router, choice, mask_first, mask_second)
        position, kept_copy = copy_slots(choice, experts, capacity)
        flat_slot = jnp.where(kept_copy, choice * capacity + position, slot_count)
        token_ids = jnp.broadcast_to(jnp.arange(tokens, dtype=jnp.int32)[:, None], (tokens, 2))
        source_row = jnp.full((slot_count,), tokens, jnp.int32).at[flat_slot.reshape(-1)].set(token_ids.reshape(-1), mode="drop")
        send_rows = jnp.take(normed, source_row, axis=0, mode="fill", fill_value=0)
        recv_rows = lax.all_to_all(send_rows, "ep", 0, 0, tiled=True)
        expert_out = expert_mlp(recv_rows.reshape(group_size, local_experts, capacity, row_width), w_gate, w_up, w_down)
        back_rows = lax.all_to_all(expert_out.reshape(slot_count, row_width), "ep", 0, 0, tiled=True)
        picked = jnp.take(back_rows, flat_slot, axis=0, mode="fill", fill_value=0)
        mixed_out = hidden.astype(jnp.float32) + jnp.sum(gate_vals[:, :, None] * picked.astype(jnp.float32), axis=1)
        return mixed_out.astype(jnp.bfloat16)

    return jax.shard_map(device_step, mesh=mesh,
                         in_specs=(rows_spec, P(), P(), P(), P("ep"), P("ep"), P("ep"), rows_spec, rows_spec, rows_spec),
                         out_specs=rows_spec, check_vma=False)
```

profile of v0, /device:TPU:0, one launch (start us, length us, event | category | flops | bytes accessed | tf_op | source)
XLA Modules:
  0.0 1429.2 jit_solution(9633672971434301196)
XLA Ops:
  0.0 0.8 convert_reduce_fusion.1
  0.8 2.3 reduce-window.6
  3.7 0.8 select_reduce_fusion.1
  4.5 1.3 compare_and_fusion
  6.2 0.6 reshape.92
  7.4 15.5 %scatter_custom_fusion = s32[5120]{0:T(1024)S(1)} fusion(s32[4096]{0:T(1024)S(1)} %bitcast.90, s32[4096]{0:T(1024)S(1)} %reshape.115, s32[]{:T(128)} %constant.52.clone.1), kind=kCustom, calls=%fused_computation.58 | custom fusion | bytes 20484 | tf_op jit(solution)/shard_map/scatter | solution.py:55
  23.0 5.0 convert_reduce_fusion
  28.0 6.3 fusion.20
  34.3 10.9 fusion.23
  45.2 48.5 %gather_fusion = bf16[5120,2304]{1,0:T(8,128)(2,1)} fusion(bf16[2048,2304]{1,0:T(8,128)(2,1)} %fusion.23, s32[5120]{0:T(1024)S(1)} %fusion.41), kind=kCustom, calls=%fused_computation | custom fusion | bytes 47206400 | tf_op jit(solution)/shard_map/jit(_take)/gather | solution.py:56
  93.7 12.3 broadcast_select_fusion.1
  106.0 261.9 %all_to_all.18 = bf16[4,1280,2304]{2,1,0:T(8,128)(2,1)} all-to-all(bf16[4,1280,2304]{2,1,0:T(8,128)(2,1)S(1)} %broadcast_select_fusion.1), channel_id=1, replica_groups=mesh['dp'=4,'ep'=4] {'ep'}, dimensions={0} | all-to-all | bytes 47185920 | tf_op jit(solution)/shard_map/all_to_all | solution.py:57
  367.9 158.0 %fusion.13 = f32[2,4,640,5760]{3,2,1,0:T(8,128)} fusion(bf16[2,2304,5760]{2,1,0:T(8,128)(2,1)} %param.14, bf16[4,2,640,2304]{3,2,1,0:T(8,128)(2,1)} %bitcast.85), kind=kOutput, calls=%fused_computation.16 | convolution fusion | flops 135895449600 | bytes 194641920 | tf_op jit(solution)/shard_map/secd,edf->secf/dot_general | solution.py:34
  526.0 178.7 %fusion.65 = bf16[4,2,640,5760]{3,2,0,1:T(8,128)(2,1)} fusion(f32[2,4,640,5760]{3,2,1,0:T(8,128)} %fusion.13, bf16[2,2304,5760]{2,1,0:T(8,128)(2,1)} %param.15, bf16[4,2,640,2304]{3,2,1,0:T(8,128)(2,1)} %bitcast.86), kind=kOutput, calls=%fused_computation.6.clone.clone.clone.clone.1 | convolution fusion | flops 136072396800 | bytes 253624320 | tf_op jit(solution)/shard_map/secd,edf->secf/dot_general | solution.py:35
  704.7 152.6 %convert_bitcast_fusion = bf16[4,2,640,2304]{3,2,0,1:T(8,128)(2,1)} fusion(bf16[2,5760,2304]{2,1,0:T(8,128)(2,1)} %param.16, bf16[4,2,640,5760]{3,2,0,1:T(8,128)(2,1)} %fusion.65), kind=kOutput, calls=%fused_computation.23 | convolution fusion | flops 135907246080 | bytes 135659520 | tf_op jit(solution)/shard_map/secf,efd->secd/dot_general | solution.py:37
  857.2 19.7 %copy.22 = bf16[4,2,640,2304]{3,2,1,0:T(8,128)(2,1)} copy(bf16[4,2,640,2304]{3,2,0,1:T(8,128)(2,1)} %convert_bitcast_fusion) | data formatting | bytes 47185920 | tf_op jit(solution)/shard_map/convert_element_type | solution.py:37
  877.0 8.7 all-to-all-start.1
  885.7 0.5 copy.18
  887.0 6.2 fusion.53
  893.8 247.6 %all-to-all-done.1 = bf16[4,1280,2304]{2,1,0:T(8,128)(2,1)} async-done(((bf16[4,1280,2304]{2,1,0:T(8,128)(2,1)}), bf16[4,1280,2304]{2,1,0:T(8,128)(2,1)}, u32[]{:S(2)}, u32[]{:S(2)}) %all-to-all-start.1) | async-done | bytes 23592992 | tf_op jit(solution)/shard_map/all_to_all | solution.py:59
  1141.4 45.9 %gather_fusion.1 = bf16[4096,2304]{1,0:T(8,128)(2,1)} fusion(bf16[5120,2304]{1,0:T(8,128)(2,1)} %bitcast.17, s32[4096]{0:T(1024)S(1)} %broadcast_clamp_fusion), kind=kCustom, calls=%fused_computation.1 | custom fusion | bytes 37765120 | tf_op jit(solution)/shard_map/jit(_take)/gather | solution.py:60
  1187.3 36.4 %reshape.104 = bf16[2048,2,2304]{2,1,0:T(2,128)(2,1)} reshape(bf16[4096,2304]{1,0:T(8,128)(2,1)} %gather_fusion.1) | data formatting | bytes 37748736 | tf_op jit(solution)/shard_map/jit(_take)/gather | solution.py:60
  1223.6 195.5 %multiply_reduce_fusion = f32[2048,2304]{1,0:T(8,128)S(1)} fusion(bf16[2048,2,2304]{2,1,0:T(2,128)(2,1)} %reshape.104, pred[2048,2]{1,0:T(8,128)(4,1)S(1)} %copy.18, f32[2048,2]{1,0:T(8,128)S(1)} %copy.17), kind=kLoop, calls=%fused_computation.18 | loop fusion | flops 33030144 | bytes 37769216 | tf_op jit(solution)/shard_map/reduce_sum | solution.py:61
  1419.1 9.9 fusion.24
  (38 shorter events, 3.0 us)
Async XLA Ops:
  0.0 887.0 %copy-start = (bf16[2304,8]{0,1:T(8,128)(2,1)S(1)}, bf16[2304,8]{0,1:T(8,128)(2,1)}, u32[]{:S(2)}) copy-start(bf16[2304,8]{0,1:T(8,128)(2,1)} %param.13) | copy-start | bytes 110596
  0.0 34.2 %copy-start.5 = (f32[2304]{0:T(1024)S(1)}, f32[2304]{0:T(1024)}, u32[]{:S(2)}) copy-start(f32[2304]{0:T(1024)} %param.12) | copy-start | bytes 27652
  0.0 34.3 %copy-start.6 = (f32[2304]{0:T(1024)S(1)}, f32[2304]{0:T(1024)}, u32[]{:S(2)}) copy-start(f32[2304]{0:T(1024)} %param.11) | copy-start | bytes 27652
  5.8 87.8 %copy-start.1 = (s32[2048,2]{0,1:T(2,128)}, s32[2048,2]{0,1:T(2,128)S(1)}, u32[]{:S(2)}) copy-start(s32[2048,2]{0,1:T(2,128)S(1)} %get-tuple-element.6) | copy-start | bytes 49156
  877.0 8.7 copy-start.4
  877.0 9.2 copy-start.2
  877.0 16.3 %copy-start.3 = (s32[2048,2]{0,1:T(2,128)S(1)}, s32[2048,2]{0,1:T(2,128)}, u32[]{:S(2)}) copy-start(s32[2048,2]{0,1:T(2,128)} %param.17) | copy-start | bytes 49156
  877.0 16.3 %copy-start.7 = (s32[2048,8]{0,1:T(8,128)S(1)}, s32[2048,8]{0,1:T(8,128)}, u32[]{:S(2)}) copy-start(s32[2048,8]{0,1:T(8,128)} %param.19) | copy-start | bytes 196612
  877.0 16.3 %copy-start.8 = (s32[2048,8]{0,1:T(8,128)S(1)}, s32[2048,8]{0,1:T(8,128)}, u32[]{:S(2)}) copy-start(s32[2048,8]{0,1:T(8,128)} %param.18) | copy-start | bytes 196612
  877.0 264.4 %all-to-all-start.1 = ((bf16[4,1280,2304]{2,1,0:T(8,128)(2,1)}), bf16[4,1280,2304]{2,1,0:T(8,128)(2,1)}, u32[]{:S(2)}, u32[]{:S(2)}) async-start(bf16[4,1280,2304]{2,1,0:T(8,128)(2,1)} %bitcast.84), calls=%async_computation.1 | async-start | bytes 47185920 | tf_op jit(solution)/shard_map/all_to_all | solution.py:59
where the time goes:
time: 1440 us; the launch traced here: 1430 us
  matrix products  495 us (34%)
  blocking collectives  262 us (18%)
  waiting for transfers between devices  248 us (17%)
  other arithmetic  246 us (17%)
  local copies, waits for them, and re-layouts  170 us (12%)
    all_to_all x1, blocking collectives, device_step(): recv_rows = lax.all_to_all(send_rows, 'ep', 0, 0, tiled=True)  262 us
    all_to_all x1, waiting for transfers between devices, device_step(): lax.all_to_all(expert_out.reshape(slot_count, row_width), 'ep', 0, 0, til...  248 us
    reduce_sum x1, other arithmetic, device_step(): jnp.sum(gate_vals[:, :, None] * picked.astype(jnp.float32), axis=1)  195 us
    dot_general x1, matrix products, expert_mlp(): jnp.einsum('secd,edf->secf', expert_in, w_up, preferred_element_type=jnp....  179 us
    dot_general x1, matrix products, expert_mlp(): jnp.einsum('secd,edf->secf', expert_in, w_gate, preferred_element_type=jn...  158 us
    dot_general x1, matrix products, expert_mlp(): jnp.einsum('secf,efd->secd', inner_act, w_down, preferred_element_type=jn...  153 us
    gather x2, local copies, waits for them, and re-layouts, device_step(): picked = jnp.take(back_rows, flat_slot, axis=0, mode='fill', fill_value=0)  82.3 us
    gather x1, local copies, waits for them, and re-layouts, device_step(): send_rows = jnp.take(normed, source_row, axis=0, mode='fill', fill_value=0)  48.5 us
  transfers between devices with their start and end apart: 1, of which 1 were waited for; matrix products, arithmetic and copies ran while one was open for 1% of the time, Pallas kernels for 0%

commit v1 on v0

v1 whole, which is shorter than its diff:
```python
import functools

import jax
import jax.numpy as jnp
from jax import lax
from jax.experimental import pallas as pl
from jax.experimental.pallas import tpu as pltpu
from jax.sharding import PartitionSpec as P


LN_EPS = 1e-5
F32, BF16, I32 = jnp.float32, jnp.bfloat16, jnp.int32
VMEM_LIMIT = 66 * 1024 * 1024 - 2 * 1024 * 1024 - 128 * 1024
NORM_ROWS = 256
PACK_ROWS = 256
PACK_WIN = 128
TILE = 160
FF_BLOCK = 768
MIX_ROWS = 128
MIX_WIN = 256


def norm_kernel(x_ref, gamma_ref, beta_ref, router_ref, choice_ref, rel_ref, first_ref, second_ref, u_ref, gate_ref):
    values = x_ref[...].astype(F32)
    centred = values - jnp.mean(values, axis=-1, keepdims=True)
    variance = jnp.mean(centred * centred, axis=-1, keepdims=True)
    normed = (centred * lax.rsqrt(variance + LN_EPS) * gamma_ref[...] + beta_ref[...]).astype(BF16)
    u_ref[...] = normed
    scores = lax.dot_general(router_ref[...], normed, (((1,), (1,)), ((), ())), preferred_element_type=F32)
    expert_ids = lax.broadcasted_iota(I32, scores.shape, 0)
    gates = jnp.zeros_like(scores)
    for j, mask_ref in enumerate((first_ref, second_ref)):
        masked = jnp.where(mask_ref[...] > 0, scores, -jnp.inf)
        weights = jnp.exp(masked - jnp.max(masked, axis=0, keepdims=True))
        picked = jnp.where(expert_ids == choice_ref[j:j + 1, :], weights, 0.0)
        gate = jnp.sum(picked, axis=0, keepdims=True) / jnp.sum(weights, axis=0, keepdims=True)
        gates = gates + jnp.where(expert_ids == rel_ref[j:j + 1, :], gate, 0.0)
    gate_ref[...] = gates


def norm_call(part, parts, hidden, gamma, beta, router_t, choice_t, rel_t, first_t, second_t):
    tokens, width = hidden.shape
    experts = router_t.shape[0]
    rows = tokens // parts
    steps = rows // NORM_ROWS
    at = lambda i: i + part * steps
    lanes = lambda n: pl.BlockSpec((n, NORM_ROWS), lambda i: (0, at(i)))
    whole = lambda shape: pl.BlockSpec(shape, lambda i: (0, 0))
    return pl.pallas_call(
        norm_kernel,
        grid=(steps,),
        in_specs=[pl.BlockSpec((NORM_ROWS, width), lambda i: (at(i), 0)), whole((1, width)), whole((1, width)),
                  whole((experts, width)), lanes(2), lanes(2), lanes(experts), lanes(experts)],
        out_specs=[pl.BlockSpec((NORM_ROWS, width), lambda i: (i, 0)),
                   pl.BlockSpec((experts, NORM_ROWS), lambda i: (0, i))],
        out_shape=[jax.ShapeDtypeStruct((rows, width), BF16), jax.ShapeDtypeStruct((experts, rows), F32)],
        cost_estimate=pl.CostEstimate(flops=rows * width * 60, bytes_accessed=rows * width * 4, transcendentals=0),
        name="norm",
    )(hidden, gamma, beta, router_t, choice_t, rel_t, first_t, second_t)


def pack_kernel(half_steps, start_ref, pos_ref, low_ref, high_ref, rows_ref):
    step = pl.program_id(0)
    experts = rows_ref.shape[0]
    steps = 2 * half_steps

    @pl.when(step == 0)
    def _():
        rows_ref[...] = jnp.zeros_like(rows_ref)

    def pack(block_ref):
        for e in range(experts):
            begin = start_ref[e * (steps + 1) + step]
            end = start_ref[e * (steps + 1) + step + 1]
            base = (begin // 16) * 16
            windows = jnp.where(end > begin, (end - base + PACK_WIN - 1) // PACK_WIN, 0)
            slots = jnp.broadcast_to(pos_ref[e:e + 1, :], (PACK_WIN, PACK_ROWS))
            sublane = lax.broadcasted_iota(I32, (PACK_WIN, PACK_ROWS), 0)

            def window(w, carry):
                at = pl.multiple_of(base + w * PACK_WIN, 16)
                onehot = (slots - at == sublane).astype(F32).astype(BF16)
                picked = jnp.dot(onehot, block_ref[...], preferred_element_type=F32)
                held = rows_ref[e, pl.ds(at, PACK_WIN), :]
                rows_ref[e, pl.ds(at, PACK_WIN), :] = (held.astype(F32) + picked).astype(BF16)
                return carry

            lax.fori_loop(0, windows, window, 0)

    pl.when(step < half_steps)(lambda: pack(low_ref))
    pl.when(step >= half_steps)(lambda: pack(high_ref))


def pack_call(starts, pos, low, high, capacity):
    half, width = low.shape
    experts = pos.shape[0]
    half_steps = half // PACK_ROWS
    padded = (capacity + PACK_WIN - 1) // PACK_WIN * PACK_WIN + PACK_WIN
    return pl.pallas_call(
        functools.partial(pack_kernel, half_steps),
        grid_spec=pltpu.PrefetchScalarGridSpec(
            num_scalar_prefetch=1,
            grid=(2 * half_steps,),
            in_specs=[pl.BlockSpec((experts, PACK_ROWS), lambda i, s: (0, i)),
                      pl.BlockSpec((PACK_ROWS, width), lambda i, s: (jnp.minimum(i, half_steps - 1), 0)),
                      pl.BlockSpec((PACK_ROWS, width), lambda i, s: (jnp.maximum(i - half_steps, 0), 0))],
            out_specs=pl.BlockSpec((experts, padded, width), lambda i, s: (0, 0, 0)),
        ),
        out_shape=jax.ShapeDtypeStruct((experts, padded, width), BF16),
        compiler_params=pltpu.CompilerParams(vmem_limit_bytes=40 * 1024 * 1024),
        cost_estimate=pl.CostEstimate(flops=experts * 2 * half * PACK_ROWS * width, bytes_accessed=4 * half * width * 3,
                                      transcendentals=0),
        name="pack",
    )(starts, pos, low, high)


def mlp_kernel(full_steps, tail, tiles_ref, one_ref, two_ref, gate_ref, up_ref, down_ref, out_one_ref, out_two_ref, acc_ref):
    step = pl.program_id(0)
    tiles = tiles_ref[0]
    rows = out_one_ref.shape[0]

    @pl.when(step == 0)
    def _():
        acc_ref[...] = jnp.zeros_like(acc_ref)

    def accumulate(width):
        def tile(i, carry):
            at = pl.multiple_of(i * TILE, TILE)
            both = pl.multiple_of(i * 2 * TILE, 2 * TILE)
            tokens = jnp.concatenate([one_ref[0, pl.ds(at, TILE), :], two_ref[0, pl.ds(at, TILE), :]], axis=0)
            joined = jnp.concatenate([gate_ref[0, :, :width], up_ref[0, :, :width]], axis=1)
            proj = jnp.dot(tokens, joined, preferred_element_type=F32)
            inner = (jax.nn.silu(proj[:, :width]) * proj[:, width:]).astype(BF16)
            acc_ref[pl.ds(both, 2 * TILE), :] += jnp.dot(inner, down_ref[0, :width, :], preferred_element_type=F32)
            return carry

        lax.fori_loop(0, tiles, tile, 0)

    pl.when(step < full_steps)(lambda: accumulate(FF_BLOCK))

    @pl.when(step == full_steps)
    def _():
        accumulate(tail)
        for i in range(rows // TILE):
            out_one_ref[i * TILE:(i + 1) * TILE, :] = acc_ref[2 * i * TILE:(2 * i + 1) * TILE, :].astype(BF16)
            out_two_ref[i * TILE:(i + 1) * TILE, :] = acc_ref[(2 * i + 1) * TILE:(2 * i + 2) * TILE, :].astype(BF16)


def mlp_call(expert, chunk, rows, tiles, packed_one, packed_two, w_gate, w_up, w_down):
    width, ff = w_gate.shape[1:]
    full_steps, tail = divmod(ff, FF_BLOCK)
    once = pl.Buffered(1)
    packed_spec = pl.BlockSpec((1, rows, width), lambda f, t: (expert, chunk, 0), pipeline_mode=once)
    out_spec = pl.BlockSpec((rows, width), lambda f, t: (0, 0), pipeline_mode=once)
    in_spec = pl.BlockSpec((1, width, FF_BLOCK), lambda f, t: (expert, 0, f))
    out = jax.ShapeDtypeStruct((rows, width), BF16)
    return pl.pallas_call(
        functools.partial(mlp_kernel, full_steps, tail),
        grid_spec=pltpu.PrefetchScalarGridSpec(
            num_scalar_prefetch=1,
            grid=(full_steps + 1,),
            in_specs=[packed_spec, packed_spec, in_spec, in_spec,
                      pl.BlockSpec((1, FF_BLOCK, width), lambda f, t: (expert, f, 0))],
            out_specs=[out_spec, out_spec],
            scratch_shapes=[pltpu.VMEM((2 * rows, width), F32)],
        ),
        out_shape=[out, out],
        compiler_params=pltpu.CompilerParams(vmem_limit_bytes=VMEM_LIMIT),
        cost_estimate=pl.CostEstimate(flops=6 * 2 * rows * width * ff, bytes_accessed=6 * width * ff, transcendentals=0),
        name="mlp",
    )(tiles, packed_one, packed_two, w_gate, w_up, w_down)


def mix_kernel(columns, pieces, capacity, start_ref, base_ref, pos_ref, gate_ref, *rest):
    piece_refs, (out_ref, held_ref, sem) = rest[:-3], rest[-3:]
    step = pl.program_id(0)
    steps = pl.num_programs(0)

    @pl.when(step == 0)
    def _():
        copies = []
        for n, piece in enumerate(piece_refs):
            rows = piece.shape[0]
            copies.append(pltpu.make_async_copy(
                piece, held_ref.at[n // pieces, pl.ds((n % pieces) * rows, rows), :], sem.at[n]))
        for copy in copies:
            copy.start()
        for copy in copies:
            copy.wait()

    total = base_ref[...].astype(F32)
    lane = lax.broadcasted_iota(I32, (MIX_ROWS, MIX_WIN), 1)
    for n, column in enumerate(columns):
        begin = start_ref[column * (steps + 1) + step]
        base = pl.multiple_of(jnp.minimum((begin // 16) * 16, capacity - MIX_WIN), 16)
        onehot = (pos_ref[:, column:column + 1] - base == lane).astype(F32).astype(BF16)
        picked = jnp.dot(onehot, held_ref[n, pl.ds(base, MIX_WIN), :], preferred_element_type=F32)
        total = total + gate_ref[:, column:column + 1] * picked
    out_ref[...] = total.astype(out_ref.dtype)


def mix_call(columns, pieces, capacity, starts, base, pos, gates, rows, out_dtype):
    tokens, width = base.shape
    block = pl.BlockSpec((MIX_ROWS, width), lambda i, s: (i, 0))
    small = pl.BlockSpec((MIX_ROWS, pos.shape[1]), lambda i, s: (i, 0))
    return pl.pallas_call(
        functools.partial(mix_kernel, columns, pieces, capacity),
        grid_spec=pltpu.PrefetchScalarGridSpec(
            num_scalar_prefetch=1,
            grid=(tokens // MIX_ROWS,),
            in_specs=[block, small, small] + [pl.BlockSpec(memory_space=pl.ANY)] * len(rows),
            out_specs=block,
            scratch_shapes=[pltpu.VMEM((len(columns), capacity, width), BF16), pltpu.SemaphoreType.DMA((len(rows),))],
        ),
        out_shape=jax.ShapeDtypeStruct((tokens, width), out_dtype),
        compiler_params=pltpu.CompilerParams(vmem_limit_bytes=48 * 1024 * 1024),
        cost_estimate=pl.CostEstimate(flops=2 * tokens * MIX_WIN * width * len(columns),
                                      bytes_accessed=tokens * width * 10, transcendentals=0),
        name="mix",
    )(starts, base, pos, gates, *rows)


def solution(mesh):
    group_size = mesh.shape["ep"]
    rows_spec = P(("dp", "ep"))

    def swap(array, distance):
        return lax.ppermute(array, "ep", [(i, i ^ distance) for i in range(group_size)])

    def device_step(hidden, ln_gamma, ln_beta, w_router, w_gate, w_up, w_down, choice, mask_first, mask_second):
        tokens, _ = hidden.shape
        local = w_gate.shape[0]
        experts = local * group_size
        capacity = (10 * tokens + 4 * experts - 1) // (4 * experts)
        chunks = 2
        chunk_rows = capacity // chunks

        choice_t = choice.T
        rel_t = choice_t ^ (local * lax.axis_index("ep"))
        ids = lax.broadcasted_iota(I32, (experts, 1), 0)
        hit = ((rel_t[0:1] == ids) | (rel_t[1:2] == ids)).astype(I32)
        through = jnp.cumsum(hit, axis=1)
        before = through - hit
        pos = jnp.where((hit > 0) & (before < capacity), before, -1)
        starts = jnp.minimum(jnp.concatenate([before[:, ::MIX_ROWS], through[:, -1:]], axis=1), capacity)
        pack_starts = starts[:, ::PACK_ROWS // MIX_ROWS]
        marks = pack_starts.shape[1]
        meta = jnp.concatenate([pos, jnp.pad(pack_starts, ((0, 0), (0, 128 - marks)))], axis=1)
        metas = [meta[:local]] + [swap(meta[local * m:local * (m + 1)], m) for m in range(1, group_size)]

        halves, gates = [], []
        for part in range(2):
            u, g = norm_call(part, 2, hidden, ln_gamma[None], ln_beta[None], w_router.T, choice_t, rel_t,
                             mask_first.T, mask_second.T)
            halves.append(u)
            gates.append(g)
        gates_t = jnp.concatenate(gates, axis=1).T
        pos_t = pos.T

        sources = [halves, [swap(u, 1) for u in halves], [swap(u, 2) for u in halves]]
        sources.append([swap(u, 1) for u in sources[2]])

        def pack(m):
            return pack_call(metas[m][:, tokens:tokens + marks].reshape(-1), metas[m][:, :tokens], *sources[m], capacity)

        def counts(m):
            return metas[m][:, tokens + marks - 1]

        def run(m_one, m_two, expert, chunk, rows, packed):
            most = jnp.maximum(counts(m_one)[expert], counts(m_two)[expert])
            tiles = jnp.clip((most + TILE - 1) // TILE - chunk * (rows // TILE), 0, rows // TILE)
            return mlp_call(expert, chunk, rows, tiles[None], *packed, w_gate, w_up, w_down)

        near = [pack(0), pack(1)]
        near_rows = []
        for e in range(local):
            near_rows.append(run(0, 1, e, 0, capacity, near))
        mine = [one for one, _ in near_rows] + [swap(two, 1) for _, two in near_rows]

        far = [pack(2), pack(3)]
        far_two, far_three = [], []
        for e in range(local):
            for c in range(chunks):
                one, two = run(2, 3, e, c, chunk_rows, far)
                far_two.append(swap(one, 2))
                far_three.append(swap(two, 3))

        flat = starts.reshape(-1)
        total = mix_call(tuple(range(2 * local)), 1, capacity, flat, hidden, pos_t, gates_t, mine, F32)
        return mix_call(tuple(range(2 * local, experts)), chunks, capacity, flat, total, pos_t, gates_t,
                        far_two + far_three, BF16)

    return jax.shard_map(device_step, mesh=mesh,
                         in_specs=(rows_spec, P(), P(), P(), P("ep"), P("ep"), P("ep"), rows_spec, rows_spec, rows_spec),
                         out_specs=rows_spec, check_vma=False)
```

time: 1440 us -> 972 us (0.68)
  the two profiles are of different devices: /device:TPU:0 before, /device:TPU:5 now
where the time goes in v1:
time: 972 us; the launch traced here: 965 us
  Pallas kernels  574 us (59%)
  waiting for transfers between devices  292 us (30%)
  starting transfers between devices  70.7 us (7%)
  local copies, waits for them, and re-layouts  15.9 us (2%)
    pallas_call x6, Pallas kernels, mlp_call(): pl.pallas_call(functools.partial(mlp_kernel, full_steps, tail), grid_spec...  460 us
    ppermute x19, waiting for transfers between devices, swap(): lax.ppermute(array, 'ep', [(i, i ^ distance) for i in range(group_size)])  292 us
    ppermute x19, starting transfers between devices, swap(): lax.ppermute(array, 'ep', [(i, i ^ distance) for i in range(group_size)])  70.7 us
    pallas_call x2, Pallas kernels, mix_call(): pl.pallas_call(functools.partial(mix_kernel, columns, pieces, capacity),...  53 us
    pallas_call x4, Pallas kernels, pack_call(): pl.pallas_call(functools.partial(pack_kernel, half_steps), grid_spec=pltp...  47.3 us
  transfers between devices with their start and end apart: 19, of which 7 were waited for; matrix products, arithmetic and copies ran while one was open for 1% of the time, Pallas kernels for 56%

profile of v1, /device:TPU:5, one launch (start us, length us, event | category | flops | bytes accessed | tf_op | source)
XLA Modules:
  0.0 964.5 jit_solution(6086536221075590569)
XLA Ops:
  3.9 7.1 norm.3
  11.8 7.2 norm.2
  20.5 2.3 reduce-window.6
  28.4 2.3 copy-done.3
  30.8 2.3 copy-done.4
  33.1 9.4 pack.4.one_ref
  43.1 181.3 %collective-permute-done.6 = s32[2,2176]{1,0:T(2,128)S(1)} collective-permute-done((s32[2,2176]{1,0:T(2,128)S(1)}, s32[2,2176]{1,0:T(2,128)S(1)}, u32[]{:S(2)}, u32[]{:S(2)}) %collective-permute-start.6) | collective-permute-done | bytes 17440 | tf_op jit(solution)/shard_map/ppermute | solution.py:228
  233.5 12.6 %pack.5.two_ref = bf16[2,768,2304]{2,1,0:T(8,128)(2,1)} custom-call(s32[18]{0:T(128)S(1)} %reshape.106.start_ref, s32[2,2048]{1,0:T(2,128)S(1)} %slice.153.pos_ref, bf16[1024,2304]{1,0:T(8,128)(2,1)} %collective-permute-done.1.low_ref, bf16[1024,2304]{1,0:T(8,128)(2,1)} %collective-permute-done.2.high_ref), custom_call_target="tpu_custom_call" | custom-call | flops 2415919104 | bytes 28311552 | tf_op jit(solution)/shard_map/pack/pallas_call | solution.py:99
  246.1 97.8 %mlp.7 = (bf16[640,2304]{1,0:T(8,128)(2,1)}, bf16[640,2304]{1,0:T(8,128)(2,1)}) custom-call(s32[1]{0:T(128)} %bitcast.16.tiles_ref, bf16[2,768,2304]{2,1,0:T(8,128)(2,1)} %pack.4.one_ref, bf16[2,768,2304]{2,1,0:T(8,128)(2,1)} %pack.5.two_ref, bf16[2,2304,5760]{2,1,0:T(8,128)(2,1)} %gate_ref.11, bf16[2,2304,5760]{2,1,0:T(8,128)(2,1)} %up_ref.11, ...), custom_call_target="tpu_custom_call" | custom-call | flops 101921587200 | bytes 79626240 | tf_op jit(solution)/shard_map/mlp/pallas_call | solution.py:157
  344.7 126.6 %mlp.6 = (bf16[640,2304]{1,0:T(8,128)(2,1)}, bf16[640,2304]{1,0:T(8,128)(2,1)}) custom-call(s32[1]{0:T(128)} %bitcast.13.tiles_ref, bf16[2,768,2304]{2,1,0:T(8,128)(2,1)} %pack.4.one_ref, bf16[2,768,2304]{2,1,0:T(8,128)(2,1)} %pack.5.two_ref, bf16[2,2304,5760]{2,1,0:T(8,128)(2,1)} %gate_ref.11, bf16[2,2304,5760]{2,1,0:T(8,128)(2,1)} %up_ref.11, ...), custom_call_target="tpu_custom_call" | custom-call | flops 101921587200 | bytes 79626240 | tf_op jit(solution)/shard_map/mlp/pallas_call | solution.py:157
  471.8 12.7 %pack.6.one_ref = bf16[2,768,2304]{2,1,0:T(8,128)(2,1)} custom-call(s32[18]{0:T(128)S(1)} %reshape.107.start_ref, s32[2,2048]{1,0:T(2,128)S(1)} %slice.158.pos_ref, bf16[1024,2304]{1,0:T(8,128)(2,1)} %collective-permute-done.7.low_ref, bf16[1024,2304]{1,0:T(8,128)(2,1)} %collective-permute-done.8.high_ref), custom_call_target="tpu_custom_call" | custom-call | flops 2415919104 | bytes 28311552 | tf_op jit(solution)/shard_map/pack/pallas_call | solution.py:99
  484.5 12.6 %pack.7.two_ref = bf16[2,768,2304]{2,1,0:T(8,128)(2,1)} custom-call(s32[18]{0:T(128)S(1)} %reshape.108.start_ref, s32[2,2048]{1,0:T(2,128)S(1)} %slice.160.pos_ref, bf16[1024,2304]{1,0:T(8,128)(2,1)} %collective-permute-done.9.low_ref, bf16[1024,2304]{1,0:T(8,128)(2,1)} %collective-permute-done.10.high_ref), custom_call_target="tpu_custom_call" | custom-call | flops 2415919104 | bytes 28311552 | tf_op jit(solution)/shard_map/pack/pallas_call | solution.py:99
  497.1 37.7 %mlp.11 = (bf16[320,2304]{1,0:T(8,128)(2,1)}, bf16[320,2304]{1,0:T(8,128)(2,1)}) custom-call(s32[1]{0:T(128)} %bitcast.24.tiles_ref, bf16[2,768,2304]{2,1,0:T(8,128)(2,1)} %pack.6.one_ref, bf16[2,768,2304]{2,1,0:T(8,128)(2,1)} %pack.7.two_ref, bf16[2,2304,5760]{2,1,0:T(8,128)(2,1)} %gate_ref.11, bf16[2,2304,5760]{2,1,0:T(8,128)(2,1)} %up_ref.11, ...), custom_call_target="tpu_custom_call" | custom-call | flops 50960793600 | bytes 79626240 | tf_op jit(solution)/shard_map/mlp/pallas_call | solution.py:157
  534.9 30.1 %collective-permute-start.14 = (bf16[320,2304]{1,0:T(8,128)(2,1)}, bf16[320,2304]{1,0:T(8,128)(2,1)}, u32[]{:S(2)}, u32[]{:S(2)}) collective-permute-start(bf16[320,2304]{1,0:T(8,128)(2,1)} %get-tuple-element.32), channel_id=1, source_target_pairs={{0,2},{1,3},{2,0},{3,1},{4,6},{5,7},{6,4},{7,5},{8,10},{9,11},{10,... | collective-permute-start | bytes 4423688 | tf_op jit(solution)/shard_map/ppermute | solution.py:228
  565.0 28.2 %collective-permute-start.18 = (bf16[320,2304]{1,0:T(8,128)(2,1)}, bf16[320,2304]{1,0:T(8,128)(2,1)}, u32[]{:S(2)}, u32[]{:S(2)}) collective-permute-start(bf16[320,2304]{1,0:T(8,128)(2,1)} %get-tuple-element.36), channel_id=1, source_target_pairs={{0,3},{1,2},{2,1},{3,0},{4,7},{5,6},{6,5},{7,4},{8,11},{9,10},{10,... | collective-permute-start | bytes 4423688 | tf_op jit(solution)/shard_map/ppermute | solution.py:228
  593.1 65.8 %mlp.10 = (bf16[320,2304]{1,0:T(8,128)(2,1)}, bf16[320,2304]{1,0:T(8,128)(2,1)}) custom-call(s32[1]{0:T(128)} %bitcast.23.tiles_ref, bf16[2,768,2304]{2,1,0:T(8,128)(2,1)} %pack.6.one_ref, bf16[2,768,2304]{2,1,0:T(8,128)(2,1)} %pack.7.two_ref, bf16[2,2304,5760]{2,1,0:T(8,128)(2,1)} %gate_ref.11, bf16[2,2304,5760]{2,1,0:T(8,128)(2,1)} %up_ref.11, ...), custom_call_target="tpu_custom_call" | custom-call | flops 50960793600 | bytes 79626240 | tf_op jit(solution)/shard_map/mlp/pallas_call | solution.py:157
  660.7 66.1 %mlp.9 = (bf16[320,2304]{1,0:T(8,128)(2,1)}, bf16[320,2304]{1,0:T(8,128)(2,1)}) custom-call(s32[1]{0:T(128)} %bitcast.20.tiles_ref, bf16[2,768,2304]{2,1,0:T(8,128)(2,1)} %pack.6.one_ref, bf16[2,768,2304]{2,1,0:T(8,128)(2,1)} %pack.7.two_ref, bf16[2,2304,5760]{2,1,0:T(8,128)(2,1)} %gate_ref.11, bf16[2,2304,5760]{2,1,0:T(8,128)(2,1)} %up_ref.11, ...), custom_call_target="tpu_custom_call" | custom-call | flops 50960793600 | bytes 79626240 | tf_op jit(solution)/shard_map/mlp/pallas_call | solution.py:157
  726.8 65.8 %mlp.8 = (bf16[320,2304]{1,0:T(8,128)(2,1)}, bf16[320,2304]{1,0:T(8,128)(2,1)}) custom-call(s32[1]{0:T(128)} %bitcast.19.tiles_ref, bf16[2,768,2304]{2,1,0:T(8,128)(2,1)} %pack.6.one_ref, bf16[2,768,2304]{2,1,0:T(8,128)(2,1)} %pack.7.two_ref, bf16[2,2304,5760]{2,1,0:T(8,128)(2,1)} %gate_ref.11, bf16[2,2304,5760]{2,1,0:T(8,128)(2,1)} %up_ref.11, ...), custom_call_target="tpu_custom_call" | custom-call | flops 50960793600 | bytes 79626240 | tf_op jit(solution)/shard_map/mlp/pallas_call | solution.py:157
  800.6 26.5 %mix.2.base_ref = f32[2048,2304]{1,0:T(8,128)} custom-call(s32[136]{0:T(256)S(1)} %min.31.start_ref, bf16[2048,2304]{1,0:T(8,128)(2,1)} %base_ref.1, s32[2048,8]{1,0:T(8,128)S(1)} %bitcast.32, f32[2048,8]{1,0:T(8,128)S(1)} %bitcast.34, bf16[640,2304]{1,0:T(8,128)(2,1)S(1)} %copy-done.5, bf16[640,2304]{1,0:T(8,128)(2,1)} %get-tuple-element.26.rest_1_, ...), custom_call_target="tpu_custom_call" | custom-call | flops 9663676416 | bytes 47185920 | tf_op jit(solution)/shard_map/mix/pallas_call | solution.py:206
  827.7 26.5 %collective-permute-done.12.rest_1_ = bf16[320,2304]{1,0:T(8,128)(2,1)S(1)} collective-permute-done((bf16[320,2304]{1,0:T(8,128)(2,1)}, bf16[320,2304]{1,0:T(8,128)(2,1)S(1)}, u32[]{:S(2)}, u32[]{:S(2)}) %collective-permute-start.12) | collective-permute-done | bytes 1474592 | tf_op jit(solution)/shard_map/ppermute | solution.py:228
  854.2 36.7 %collective-permute-done.16.rest_5_ = bf16[320,2304]{1,0:T(8,128)(2,1)} collective-permute-done((bf16[320,2304]{1,0:T(8,128)(2,1)}, bf16[320,2304]{1,0:T(8,128)(2,1)}, u32[]{:S(2)}, u32[]{:S(2)}) %collective-permute-start.16) | collective-permute-done | bytes 1474592 | tf_op jit(solution)/shard_map/ppermute | solution.py:228
  890.9 26.5 %collective-permute-done.11.rest_0_ = bf16[320,2304]{1,0:T(8,128)(2,1)} collective-permute-done((bf16[320,2304]{1,0:T(8,128)(2,1)}, bf16[320,2304]{1,0:T(8,128)(2,1)}, u32[]{:S(2)}, u32[]{:S(2)}) %collective-permute-start.11) | collective-permute-done | bytes 1474592 | tf_op jit(solution)/shard_map/ppermute | solution.py:228
  917.4 20.1 %collective-permute-done.15.rest_4_ = bf16[320,2304]{1,0:T(8,128)(2,1)} collective-permute-done((bf16[320,2304]{1,0:T(8,128)(2,1)}, bf16[320,2304]{1,0:T(8,128)(2,1)}, u32[]{:S(2)}, u32[]{:S(2)}) %collective-permute-start.15) | collective-permute-done | bytes 1474592 | tf_op jit(solution)/shard_map/ppermute | solution.py:228
  937.5 26.5 %mix.3 = bf16[2048,2304]{1,0:T(8,128)(2,1)} custom-call(s32[136]{0:T(256)S(1)} %min.31.start_ref, f32[2048,2304]{1,0:T(8,128)} %mix.2.base_ref, s32[2048,8]{1,0:T(8,128)S(1)} %bitcast.33, f32[2048,8]{1,0:T(8,128)S(1)} %bitcast.35, bf16[320,2304]{1,0:T(8,128)(2,1)} %collective-permute-done.11.rest_0_, bf16[320,2304]{1,0:T(8,128)(2,1)S(1)} %collective-permute-done.12.rest_1_, ...), custom_call_target="tpu_custom_call" | custom-call | flops 9663676416 | bytes 47185920 | tf_op jit(solution)/shard_map/mix/pallas_call | solution.py:206
  (86 shorter events, 28.1 us)
Async XLA Ops:
  11.1 9.4 copy-start.6
  11.1 222.4 %collective-permute-start.2 = (bf16[1024,2304]{1,0:T(8,128)(2,1)}, bf16[1024,2304]{1,0:T(8,128)(2,1)}, u32[]{:S(2)}, u32[]{:S(2)}) collective-permute-start(bf16[1024,2304]{1,0:T(8,128)(2,1)} %get-tuple-element.24.high_ref), channel_id=1, source_target_pairs={{0,1},{1,0},{2,3},{3,2},{4,5},{5,4},{6,7},{7,6},{8,9},{9,8},{10,11... | collective-permute-start | bytes 14155784 | tf_op jit(solution)/shard_map/ppermute | solution.py:228
  19.0 214.5 %collective-permute-start.1 = (bf16[1024,2304]{1,0:T(8,128)(2,1)}, bf16[1024,2304]{1,0:T(8,128)(2,1)}, u32[]{:S(2)}, u32[]{:S(2)}) collective-permute-start(bf16[1024,2304]{1,0:T(8,128)(2,1)} %get-tuple-element.23.low_ref), channel_id=1, source_target_pairs={{0,1},{1,0},{2,3},{3,2},{4,5},{5,4},{6,7},{7,6},{8,9},{9,8},{10,11... | collective-permute-start | bytes 14155784 | tf_op jit(solution)/shard_map/ppermute | solution.py:228
  19.0 324.9 %collective-permute-start.8 = (bf16[1024,2304]{1,0:T(8,128)(2,1)}, bf16[1024,2304]{1,0:T(8,128)(2,1)}, u32[]{:S(2)}, u32[]{:S(2)}) collective-permute-start(bf16[1024,2304]{1,0:T(8,128)(2,1)} %get-tuple-element.24.high_ref), channel_id=1, source_target_pairs={{0,2},{1,3},{2,0},{3,1},{4,6},{5,7},{6,4},{7,5},{8,10},{9,11},{10,... | collective-permute-start | bytes 14155784 | tf_op jit(solution)/shard_map/ppermute | solution.py:228
  20.2 324.4 %collective-permute-start.7 = (bf16[1024,2304]{1,0:T(8,128)(2,1)}, bf16[1024,2304]{1,0:T(8,128)(2,1)}, u32[]{:S(2)}, u32[]{:S(2)}) collective-permute-start(bf16[1024,2304]{1,0:T(8,128)(2,1)} %get-tuple-element.23.low_ref), channel_id=1, source_target_pairs={{0,2},{1,3},{2,0},{3,1},{4,6},{5,7},{6,4},{7,5},{8,10},{9,11},{10,... | collective-permute-start | bytes 14155784 | tf_op jit(solution)/shard_map/ppermute | solution.py:228
  24.6 17.9 %copy-start = (s32[8,2048]{0,1:T(8,128)}, s32[8,2048]{0,1:T(8,128)S(1)}, u32[]{:S(2)}) copy-start(s32[8,2048]{0,1:T(8,128)S(1)} %get-tuple-element.37) | copy-start | bytes 196612
  25.9 198.6 %collective-permute-start.6 = (s32[2,2176]{1,0:T(2,128)S(1)}, s32[2,2176]{1,0:T(2,128)S(1)}, u32[]{:S(2)}, u32[]{:S(2)}) collective-permute-start(s32[2,2176]{1,0:T(2,128)S(1)} %get-tuple-element.39), channel_id=1, source_target_pairs={{0,3},{1,2},{2,1},{3,0},{4,7},{5,6},{6,5},{7,4},{8,11},{9,10},{10,... | collective-permute-start | bytes 52232 | tf_op jit(solution)/shard_map/ppermute | solution.py:228
  224.5 1.2 collective-permute-start
  225.6 4.4 collective-permute-start.5
  343.9 140.7 %collective-permute-start.10 = (bf16[1024,2304]{1,0:T(8,128)(2,1)}, bf16[1024,2304]{1,0:T(8,128)(2,1)}, u32[]{:S(2)}, u32[]{:S(2)}) collective-permute-start(bf16[1024,2304]{1,0:T(8,128)(2,1)} %collective-permute-done.8.high_ref), channel_id=1, source_target_pairs={{0,1},{1,0},{2,3},{3,2},{4,5},{5,4},{6,7},{7,6},{8,9},{9,8},{10,11... | collective-permute-start | bytes 14155784 | tf_op jit(solution)/shard_map/ppermute | solution.py:228
  344.7 139.9 %collective-permute-start.9 = (bf16[1024,2304]{1,0:T(8,128)(2,1)}, bf16[1024,2304]{1,0:T(8,128)(2,1)}, u32[]{:S(2)}, u32[]{:S(2)}) collective-permute-start(bf16[1024,2304]{1,0:T(8,128)(2,1)} %collective-permute-done.7.low_ref), channel_id=1, source_target_pairs={{0,1},{1,0},{2,3},{3,2},{4,5},{5,4},{6,7},{7,6},{8,9},{9,8},{10,11... | collective-permute-start | bytes 14155784 | tf_op jit(solution)/shard_map/ppermute | solution.py:228
  471.3 321.2 %collective-permute-start.4 = (bf16[640,2304]{1,0:T(8,128)(2,1)}, bf16[640,2304]{1,0:T(8,128)(2,1)}, u32[]{:S(2)}, u32[]{:S(2)}) collective-permute-start(bf16[640,2304]{1,0:T(8,128)(2,1)} %get-tuple-element.28), channel_id=1, source_target_pairs={{0,1},{1,0},{2,3},{3,2},{4,5},{5,4},{6,7},{7,6},{8,9},{9,8},{10,11... | collective-permute-start | bytes 8847368 | tf_op jit(solution)/shard_map/ppermute | solution.py:228
  471.3 321.2 %collective-permute-start.3 = (bf16[640,2304]{1,0:T(8,128)(2,1)}, bf16[640,2304]{1,0:T(8,128)(2,1)}, u32[]{:S(2)}, u32[]{:S(2)}) collective-permute-start(bf16[640,2304]{1,0:T(8,128)(2,1)} %get-tuple-element.27), channel_id=1, source_target_pairs={{0,1},{1,0},{2,3},{3,2},{4,5},{5,4},{6,7},{7,6},{8,9},{9,8},{10,11... | collective-permute-start | bytes 8847368 | tf_op jit(solution)/shard_map/ppermute | solution.py:228
  534.9 257.7 %collective-permute-start.14 = (bf16[320,2304]{1,0:T(8,128)(2,1)}, bf16[320,2304]{1,0:T(8,128)(2,1)}, u32[]{:S(2)}, u32[]{:S(2)}) collective-permute-start(bf16[320,2304]{1,0:T(8,128)(2,1)} %get-tuple-element.32), channel_id=1, source_target_pairs={{0,2},{1,3},{2,0},{3,1},{4,6},{5,7},{6,4},{7,5},{8,10},{9,11},{10,... | collective-permute-start | bytes 4423688 | tf_op jit(solution)/shard_map/ppermute | solution.py:228
  565.0 229.4 %collective-permute-start.18 = (bf16[320,2304]{1,0:T(8,128)(2,1)}, bf16[320,2304]{1,0:T(8,128)(2,1)}, u32[]{:S(2)}, u32[]{:S(2)}) collective-permute-start(bf16[320,2304]{1,0:T(8,128)(2,1)} %get-tuple-element.36), channel_id=1, source_target_pairs={{0,3},{1,2},{2,1},{3,0},{4,7},{5,6},{6,5},{7,4},{8,11},{9,10},{10,... | collective-permute-start | bytes 4423688 | tf_op jit(solution)/shard_map/ppermute | solution.py:228
  658.9 137.1 %collective-permute-start.13 = (bf16[320,2304]{1,0:T(8,128)(2,1)}, bf16[320,2304]{1,0:T(8,128)(2,1)}, u32[]{:S(2)}, u32[]{:S(2)}) collective-permute-start(bf16[320,2304]{1,0:T(8,128)(2,1)} %get-tuple-element.31), channel_id=1, source_target_pairs={{0,2},{1,3},{2,0},{3,1},{4,6},{5,7},{6,4},{7,5},{8,10},{9,11},{10,... | collective-permute-start | bytes 4423688 | tf_op jit(solution)/shard_map/ppermute | solution.py:228
  726.8 69.6 %copy-start.8 = (s32[8,17]{1,0:T(8,128)S(1)}, s32[8,17]{1,0:T(8,128)}, u32[]{:S(2)}) copy-start(s32[8,17]{1,0:T(8,128)} %copy-done.7) | copy-start | bytes 1636
  726.8 69.7 %copy-start.9 = (f32[8,1024]{1,0:T(8,128)S(1)}, f32[8,1024]{1,0:T(8,128)}, u32[]{:S(2)}) copy-start(f32[8,1024]{1,0:T(8,128)} %get-tuple-element.22) | copy-start | bytes 98308
  792.5 35.2 %collective-permute-start.17 = (bf16[320,2304]{1,0:T(8,128)(2,1)}, bf16[320,2304]{1,0:T(8,128)(2,1)}, u32[]{:S(2)}, u32[]{:S(2)}) collective-permute-start(bf16[320,2304]{1,0:T(8,128)(2,1)} %get-tuple-element.35), channel_id=1, source_target_pairs={{0,3},{1,2},{2,1},{3,0},{4,7},{5,6},{6,5},{7,4},{8,11},{9,10},{10,... | collective-permute-start | bytes 4423688 | tf_op jit(solution)/shard_map/ppermute | solution.py:228
  792.5 61.7 %collective-permute-start.12 = (bf16[320,2304]{1,0:T(8,128)(2,1)}, bf16[320,2304]{1,0:T(8,128)(2,1)S(1)}, u32[]{:S(2)}, u32[]{:S(2)}) collective-permute-start(bf16[320,2304]{1,0:T(8,128)(2,1)} %get-tuple-element.30), channel_id=1, source_target_pairs={{0,2},{1,3},{2,0},{3,1},{4,6},{5,7},{6,4},{7,5},{8,10},{9,11},{10,... | collective-permute-start | bytes 4423688 | tf_op jit(solution)/shard_map/ppermute | solution.py:228
  792.6 98.3 %collective-permute-start.16 = (bf16[320,2304]{1,0:T(8,128)(2,1)}, bf16[320,2304]{1,0:T(8,128)(2,1)}, u32[]{:S(2)}, u32[]{:S(2)}) collective-permute-start(bf16[320,2304]{1,0:T(8,128)(2,1)} %get-tuple-element.34), channel_id=1, source_target_pairs={{0,3},{1,2},{2,1},{3,0},{4,7},{5,6},{6,5},{7,4},{8,11},{9,10},{10,... | collective-permute-start | bytes 4423688 | tf_op jit(solution)/shard_map/ppermute | solution.py:228
  794.3 123.1 %collective-permute-start.11 = (bf16[320,2304]{1,0:T(8,128)(2,1)}, bf16[320,2304]{1,0:T(8,128)(2,1)}, u32[]{:S(2)}, u32[]{:S(2)}) collective-permute-start(bf16[320,2304]{1,0:T(8,128)(2,1)} %get-tuple-element.29), channel_id=1, source_target_pairs={{0,2},{1,3},{2,0},{3,1},{4,6},{5,7},{6,4},{7,5},{8,10},{9,11},{10,... | collective-permute-start | bytes 4423688 | tf_op jit(solution)/shard_map/ppermute | solution.py:228
  796.0 141.5 %collective-permute-start.15 = (bf16[320,2304]{1,0:T(8,128)(2,1)}, bf16[320,2304]{1,0:T(8,128)(2,1)}, u32[]{:S(2)}, u32[]{:S(2)}) collective-permute-start(bf16[320,2304]{1,0:T(8,128)(2,1)} %get-tuple-element.33), channel_id=1, source_target_pairs={{0,3},{1,2},{2,1},{3,0},{4,7},{5,6},{6,5},{7,4},{8,11},{9,10},{10,... | collective-permute-start | bytes 4423688 | tf_op jit(solution)/shard_map/ppermute | solution.py:228
  800.6 136.9 %copy-start.2 = (s32[8,2048]{0,1:T(8,128)S(1)}, s32[8,2048]{0,1:T(8,128)}, u32[]{:S(2)}) copy-start(s32[8,2048]{0,1:T(8,128)} %copy-done) | copy-start | bytes 196612
  (5 other events, 8.5 us)

commit v2 on v1

v2 whole, which is shorter than its diff:
```python
import functools

import jax
import jax.numpy as jnp
from jax import lax
from jax.experimental import pallas as pl
from jax.experimental.pallas import tpu as pltpu
from jax.sharding import PartitionSpec as P


LN_EPS = 1e-5
F32, BF16, I32 = jnp.float32, jnp.bfloat16, jnp.int32
VMEM_LIMIT = 67043328
NORM_ROWS = 256
PACK_ROWS = 512
PACK_WIN = 128
TILE = 160
FF_BLOCK = 1280
FF_SPLIT = 768
MIX_ROWS = 128
MIX_WIN = 256
MIX_COLS = 256


def norm_kernel(x_ref, gamma_ref, beta_ref, u_ref):
    values = x_ref[...].astype(F32)
    centred = values - jnp.mean(values, axis=-1, keepdims=True)
    variance = jnp.mean(centred * centred, axis=-1, keepdims=True)
    u_ref[...] = (centred * lax.rsqrt(variance + LN_EPS) * gamma_ref[...] + beta_ref[...]).astype(BF16)


def norm_call(part, parts, hidden, gamma, beta):
    tokens, width = hidden.shape
    rows = tokens // parts
    steps = rows // NORM_ROWS
    vector = pl.BlockSpec((1, width), lambda i: (0, 0))
    return pl.pallas_call(
        norm_kernel,
        grid=(steps,),
        in_specs=[pl.BlockSpec((NORM_ROWS, width), lambda i: (i + part * steps, 0)), vector, vector],
        out_specs=pl.BlockSpec((NORM_ROWS, width), lambda i: (i, 0)),
        out_shape=jax.ShapeDtypeStruct((rows, width), BF16),
        compiler_params=pltpu.CompilerParams(vmem_limit_bytes=VMEM_LIMIT),
        cost_estimate=pl.CostEstimate(flops=rows * width * 60, bytes_accessed=rows * width * 4, transcendentals=0),
        name="norm",
    )(hidden, gamma, beta)


def gate_kernel(u_ref, router_ref, choice_ref, rel_ref, first_ref, second_ref, gate_ref):
    scores = lax.dot_general(router_ref[...], u_ref[...], (((1,), (1,)), ((), ())), preferred_element_type=F32)
    expert_ids = lax.broadcasted_iota(I32, scores.shape, 0)
    gates = jnp.zeros_like(scores)
    for j, mask_ref in enumerate((first_ref, second_ref)):
        masked = jnp.where(mask_ref[...] > 0, scores, -jnp.inf)
        weights = jnp.exp(masked - jnp.max(masked, axis=0, keepdims=True))
        picked = jnp.where(expert_ids == choice_ref[j:j + 1, :], weights, 0.0)
        gate = jnp.sum(picked, axis=0, keepdims=True) / jnp.sum(weights, axis=0, keepdims=True)
        gates = gates + jnp.where(expert_ids == rel_ref[j:j + 1, :], gate, 0.0)
    gate_ref[...] = gates


def gate_call(part, u, router_t, choice_t, rel_t, first_t, second_t):
    rows, width = u.shape
    experts = router_t.shape[0]
    steps = rows // NORM_ROWS
    lanes = lambda n: pl.BlockSpec((n, NORM_ROWS), lambda i: (0, i + part * steps))
    return pl.pallas_call(
        gate_kernel,
        grid=(steps,),
        in_specs=[pl.BlockSpec((NORM_ROWS, width), lambda i: (i, 0)), pl.BlockSpec((experts, width), lambda i: (0, 0)),
                  lanes(2), lanes(2), lanes(experts), lanes(experts)],
        out_specs=pl.BlockSpec((experts, NORM_ROWS), lambda i: (0, i)),
        out_shape=jax.ShapeDtypeStruct((experts, rows), F32),
        compiler_params=pltpu.CompilerParams(vmem_limit_bytes=VMEM_LIMIT),
        cost_estimate=pl.CostEstimate(flops=rows * width * 60, bytes_accessed=rows * width * 2, transcendentals=0),
        name="gate",
    )(u, router_t, choice_t, rel_t, first_t, second_t)


def pack_kernel(half_steps, start_ref, pos_ref, low_ref, high_ref, rows_ref):
    step = pl.program_id(0)
    experts = rows_ref.shape[0]
    steps = 2 * half_steps

    @pl.when(step == 0)
    def _():
        rows_ref[...] = jnp.zeros_like(rows_ref)

    def pack(block_ref):
        for e in range(experts):
            begin = start_ref[e * (steps + 1) + step]
            end = start_ref[e * (steps + 1) + step + 1]
            base = (begin // 16) * 16
            windows = jnp.where(end > begin, (end - base + PACK_WIN - 1) // PACK_WIN, 0)
            slots = jnp.broadcast_to(pos_ref[e:e + 1, :], (PACK_WIN, PACK_ROWS))
            sublane = lax.broadcasted_iota(I32, (PACK_WIN, PACK_ROWS), 0)

            def window(w, carry):
                at = pl.multiple_of(base + w * PACK_WIN, 16)
                onehot = (slots - at == sublane).astype(F32).astype(BF16)
                picked = jnp.dot(onehot, block_ref[...], preferred_element_type=F32)
                held = rows_ref[e, pl.ds(at, PACK_WIN), :]
                rows_ref[e, pl.ds(at, PACK_WIN), :] = (held.astype(F32) + picked).astype(BF16)
                return carry

            lax.fori_loop(0, windows, window, 0)

    pl.when(step < half_steps)(lambda: pack(low_ref))
    pl.when(step >= half_steps)(lambda: pack(high_ref))


def pack_call(starts, pos, low, high, capacity):
    half, width = low.shape
    experts = pos.shape[0]
    half_steps = half // PACK_ROWS
    padded = (capacity + PACK_WIN - 1) // PACK_WIN * PACK_WIN + PACK_WIN
    return pl.pallas_call(
        functools.partial(pack_kernel, half_steps),
        grid_spec=pltpu.PrefetchScalarGridSpec(
            num_scalar_prefetch=1,
            grid=(2 * half_steps,),
            in_specs=[pl.BlockSpec((experts, PACK_ROWS), lambda i, s: (0, i)),
                      pl.BlockSpec((PACK_ROWS, width), lambda i, s: (jnp.minimum(i, half_steps - 1), 0)),
                      pl.BlockSpec((PACK_ROWS, width), lambda i, s: (jnp.maximum(i - half_steps, 0), 0))],
            out_specs=pl.BlockSpec((experts, padded, width), lambda i, s: (0, 0, 0)),
        ),
        out_shape=jax.ShapeDtypeStruct((experts, padded, width), BF16),
        compiler_params=pltpu.CompilerParams(vmem_limit_bytes=VMEM_LIMIT),
        cost_estimate=pl.CostEstimate(flops=experts * 2 * half * PACK_ROWS * width, bytes_accessed=4 * half * width * 3,
                                      transcendentals=0),
        name="pack",
    )(starts, pos, low, high)


def mlp_kernel(splits, tail_splits, tiles_ref, one_ref, two_ref, gate_ref, up_ref, down_ref, out_one_ref, out_two_ref, acc_ref):
    step = pl.program_id(1)
    tiles = tiles_ref[pl.program_id(0)]
    rows = out_one_ref.shape[1]

    def accumulate(parts, first):
        def tile(i, carry):
            at = pl.multiple_of(i * TILE, TILE)
            both = pl.ds(pl.multiple_of(i * 2 * TILE, 2 * TILE), 2 * TILE)
            tokens = jnp.concatenate([one_ref[0, pl.ds(at, TILE), :], two_ref[0, pl.ds(at, TILE), :]], axis=0)
            projs = []
            for lo, hi in parts:
                joined = jnp.concatenate([gate_ref[0, :, lo:hi], up_ref[0, :, lo:hi]], axis=1)
                projs.append(jnp.dot(tokens, joined, preferred_element_type=F32))
            for n, (lo, hi) in enumerate(parts):
                inner = (jax.nn.silu(projs[n][:, :hi - lo]) * projs[n][:, hi - lo:]).astype(BF16)
                down = jnp.dot(inner, down_ref[0, lo:hi, :], preferred_element_type=F32)
                if first and n == 0:
                    acc_ref[both, :] = down
                else:
                    acc_ref[both, :] += down
            return carry

        lax.fori_loop(0, tiles, tile, 0)

    pl.when(step == 0)(lambda: accumulate(tail_splits, True))
    pl.when(step > 0)(lambda: accumulate(splits, False))

    @pl.when(step == pl.num_programs(1) - 1)
    def _():
        for i in range(rows // TILE):
            outs = [(ref, (2 * i + n) * TILE) for n, ref in enumerate((out_one_ref, out_two_ref))]

            @pl.when(i < tiles)
            def _():
                for ref, at in outs:
                    ref[0, i * TILE:(i + 1) * TILE, :] = acc_ref[at:at + TILE, :].astype(BF16)

            @pl.when(i >= tiles)
            def _():
                for ref, _at in outs:
                    ref[0, i * TILE:(i + 1) * TILE, :] = jnp.zeros((TILE, ref.shape[2]), BF16)


def mlp_call(rows, chunk, tiles, packed_one, packed_two, w_gate, w_up, w_down):
    experts, width, ff = w_gate.shape
    full_steps, tail = divmod(ff, FF_BLOCK)
    splits = ((0, FF_SPLIT), (FF_SPLIT, FF_BLOCK))
    tail_splits = ((0, tail),)
    once = pl.Buffered(1)

    def block(e, f, t):
        return jnp.where((f == 0) | (t[e] == 0), full_steps, f - 1)

    packed_spec = pl.BlockSpec((1, rows, width), lambda e, f, t: (e, chunk, 0), pipeline_mode=once)
    out_spec = pl.BlockSpec((1, rows, width), lambda e, f, t: (e, 0, 0), pipeline_mode=once)
    in_spec = pl.BlockSpec((1, width, FF_BLOCK), lambda e, f, t: (e, 0, block(e, f, t)))
    out = jax.ShapeDtypeStruct((experts, rows, width), BF16)
    return pl.pallas_call(
        functools.partial(mlp_kernel, splits, tail_splits),
        grid_spec=pltpu.PrefetchScalarGridSpec(
            num_scalar_prefetch=1,
            grid=(experts, full_steps + 1),
            in_specs=[packed_spec, packed_spec, in_spec, in_spec,
                      pl.BlockSpec((1, FF_BLOCK, width), lambda e, f, t: (e, block(e, f, t), 0))],
            out_specs=[out_spec, out_spec],
            scratch_shapes=[pltpu.VMEM((2 * rows, width), F32)],
        ),
        out_shape=[out, out],
        compiler_params=pltpu.CompilerParams(vmem_limit_bytes=VMEM_LIMIT),
        cost_estimate=pl.CostEstimate(flops=6 * 2 * experts * rows * width * ff, bytes_accessed=6 * experts * width * ff,
                                      transcendentals=0),
        name="mlp",
    )(tiles, packed_one, packed_two, w_gate, w_up, w_down)


def mix_kernel(columns, starts_at, capacity, start_ref, base_ref, pos_ref, gate_ref, *rest):
    piece_refs, (out_ref, held_ref, sem) = rest[:-3], rest[-3:]
    step = pl.program_id(0)
    steps = pl.num_programs(0)
    width = base_ref.shape[1]

    @pl.when(step == 0)
    def _():
        copies = []
        for n, piece in enumerate(piece_refs):
            first, at = starts_at[n]
            experts, rows = piece.shape[:2]
            copies.append(pltpu.make_async_copy(
                piece, held_ref.at[pl.ds(first, experts), pl.ds(at, rows), :], sem.at[n]))
        for copy in copies:
            copy.start()
        for copy in copies:
            copy.wait()

    lane = lax.broadcasted_iota(I32, (MIX_ROWS, MIX_WIN), 1)
    bases, onehots, gates = [], [], []
    for column in columns:
        begin = start_ref[column * (steps + 1) + step]
        base = pl.multiple_of(jnp.minimum((begin // 16) * 16, capacity - MIX_WIN), 16)
        bases.append(base)
        onehots.append((pos_ref[:, column:column + 1] - base == lane).astype(F32).astype(BF16))
        gates.append(gate_ref[:, column:column + 1])
    for lo in range(0, width, MIX_COLS):
        cols = slice(lo, lo + MIX_COLS)
        total = base_ref[:, cols].astype(F32)
        for n in range(len(columns)):
            picked = jnp.dot(onehots[n], held_ref[n, pl.ds(bases[n], MIX_WIN), cols], preferred_element_type=F32)
            total = total + gates[n] * picked
        out_ref[:, cols] = total.astype(out_ref.dtype)


def mix_call(columns, starts_at, capacity, starts, base, pos, gates, pieces, out_dtype):
    tokens, width = base.shape
    block = pl.BlockSpec((MIX_ROWS, width), lambda i, s: (i, 0))
    small = pl.BlockSpec((MIX_ROWS, pos.shape[1]), lambda i, s: (i, 0))
    return pl.pallas_call(
        functools.partial(mix_kernel, columns, starts_at, capacity),
        grid_spec=pltpu.PrefetchScalarGridSpec(
            num_scalar_prefetch=1,
            grid=(tokens // MIX_ROWS,),
            in_specs=[block, small, small] + [pl.BlockSpec(memory_space=pl.ANY)] * len(pieces),
            out_specs=block,
            scratch_shapes=[pltpu.VMEM((len(columns), capacity, width), BF16), pltpu.SemaphoreType.DMA((len(pieces),))],
        ),
        out_shape=jax.ShapeDtypeStruct((tokens, width), out_dtype),
        compiler_params=pltpu.CompilerParams(vmem_limit_bytes=VMEM_LIMIT),
        cost_estimate=pl.CostEstimate(flops=2 * tokens * MIX_WIN * width * len(columns),
                                      bytes_accessed=tokens * width * 10, transcendentals=0),
        name="mix",
    )(starts, base, pos, gates, *pieces)


def solution(mesh):
    group_size = mesh.shape["ep"]
    rows_spec = P(("dp", "ep"))

    def swap(array, distance):
        return lax.ppermute(array, "ep", [(i, i ^ distance) for i in range(group_size)])

    def device_step(hidden, ln_gamma, ln_beta, w_router, w_gate, w_up, w_down, choice, mask_first, mask_second):
        tokens, _ = hidden.shape
        local = w_gate.shape[0]
        experts = local * group_size
        capacity = (10 * tokens + 4 * experts - 1) // (4 * experts)

        choice_t = choice.T
        rel_t = choice_t ^ (local * lax.axis_index("ep"))
        ids = lax.broadcasted_iota(I32, (experts, 1), 0)
        hit = ((rel_t[0:1] == ids) | (rel_t[1:2] == ids)).astype(I32)
        through = jnp.cumsum(hit, axis=1)
        before = through - hit
        pos = jnp.where((hit > 0) & (before < capacity), before, -1)
        starts = jnp.minimum(jnp.concatenate([before[:, ::MIX_ROWS], through[:, -1:]], axis=1), capacity)
        pack_starts = starts[:, ::PACK_ROWS // MIX_ROWS]
        marks = pack_starts.shape[1]
        meta = jnp.concatenate([pos, jnp.pad(pack_starts, ((0, 0), (0, 128 - marks)))], axis=1)
        metas = [meta[:local]] + [swap(meta[local * m:local * (m + 1)], m) for m in range(1, group_size)]

        halves = []
        for part in range(2):
            halves.append(norm_call(part, 2, hidden, ln_gamma[None], ln_beta[None]))

        sources = [halves, [swap(u, 1) for u in halves],
                   [swap(u, 2) for u in halves]]
        sources.append([swap(u, 1) for u in sources[2]])

        def pack(m):
            return pack_call(metas[m][:, tokens:tokens + marks].reshape(-1), metas[m][:, :tokens], *sources[m], capacity)

        def run(m_one, m_two, begin, rows, packed):
            most = jnp.maximum(metas[m_one][:, tokens + marks - 1], metas[m_two][:, tokens + marks - 1])
            tiles = jnp.clip((most - begin + TILE - 1) // TILE, 0, rows // TILE)
            return mlp_call(rows, begin // rows, tiles, *packed, w_gate, w_up, w_down)

        early = capacity - TILE
        near = [pack(0), pack(1)]
        near_early = run(0, 1, 0, early, near)
        home_early = swap(near_early[1], 1)

        far = [pack(2), pack(3)]
        far_rows = []
        for c in range(capacity // TILE):
            one, two = run(2, 3, c * TILE, TILE, far)
            far_rows.append((swap(one, 2), swap(two, 3)))

        near_late = run(0, 1, early, TILE, near)
        home_late = swap(near_late[1], 1)

        gates = [gate_call(part, u, w_router.T, choice_t, rel_t, mask_first.T, mask_second.T)
                 for part, u in enumerate(halves)]
        gates_t = jnp.concatenate(gates, axis=1).T
        pos_t = pos.T

        flat = starts.reshape(-1)
        total = mix_call(tuple(range(2 * local)), ((0, 0), (0, early), (local, 0), (local, early)), capacity, flat,
                         hidden, pos_t, gates_t, (near_early[0], near_late[0], home_early, home_late), F32)
        starts_at = tuple((local * n, c * TILE) for c in range(capacity // TILE) for n in range(2))
        return mix_call(tuple(range(2 * local, experts)), starts_at, capacity, flat, total, pos_t, gates_t,
                        tuple(piece for pair in far_rows for piece in pair), BF16)

    return jax.shard_map(device_step, mesh=mesh,
                         in_specs=(rows_spec, P(), P(), P(), P("ep"), P("ep"), P("ep"), rows_spec, rows_spec, rows_spec),
                         out_specs=rows_spec, check_vma=False)
```

time: 972 us -> 780 us (0.80)
  the two profiles are of different devices: /device:TPU:5 before, /device:TPU:7 now
where the time goes in v2:
time: 780 us; the launch traced here: 771 us
  Pallas kernels  584 us (75%)
  waiting for transfers between devices  117 us (15%)
  starting transfers between devices  42.9 us (6%)
  local copies, waits for them, and re-layouts  17 us (2%)
  other arithmetic  9.49 us (1%)
    pallas_call x6, Pallas kernels, mlp_call(): pl.pallas_call(functools.partial(mlp_kernel, splits, tail_splits), grid_s...  460 us
    ppermute x19, waiting for transfers between devices, swap(): lax.ppermute(array, 'ep', [(i, i ^ distance) for i in range(group_size)])  117 us
    pallas_call x2, Pallas kernels, mix_call(): pl.pallas_call(functools.partial(mix_kernel, columns, starts_at, capacity...  53.9 us
    pallas_call x4, Pallas kernels, pack_call(): pl.pallas_call(functools.partial(pack_kernel, half_steps), grid_spec=pltp...  47.4 us
    ppermute x19, starting transfers between devices, swap(): lax.ppermute(array, 'ep', [(i, i ^ distance) for i in range(group_size)])  42.9 us
  transfers between devices with their start and end apart: 19, of which 5 were waited for; matrix products, arithmetic and copies ran while one was open for 3% of the time, Pallas kernels for 71%

profile of v2, /device:TPU:7, one launch (start us, length us, event | category | flops | bytes accessed | tf_op | source)
XLA Modules:
  0.0 771.2 jit_solution(5816673431671182938)
XLA Ops:
  2.6 6.7 norm.2.u_ref.low_ref
  10.0 6.7 norm.3.u_ref.high_ref
  18.0 2.3 reduce-window.6
  27.7 12.8 %pack.4.one_ref = bf16[2,768,2304]{2,1,0:T(8,128)(2,1)} custom-call(s32[10]{0:T(128)} %reshape.109.start_ref, s32[2,2048]{1,0:T(2,128)} %copy.45.pos_ref, bf16[1024,2304]{1,0:T(8,128)(2,1)} %norm.2.u_ref.low_ref, bf16[1024,2304]{1,0:T(8,128)(2,1)} %norm.3.u_ref.high_ref), custom_call_target="tpu_custom_call" | custom-call | flops 4831838208 | bytes 28311552 | tf_op jit(solution)/shard_map/pack/pallas_call | solution.py:117
  53.6 12.2 %pack.5.two_ref = bf16[2,768,2304]{2,1,0:T(8,128)(2,1)} custom-call(s32[10]{0:T(128)} %reshape.110.start_ref, s32[2,2048]{1,0:T(2,128)} %slice.112.pos_ref, bf16[1024,2304]{1,0:T(8,128)(2,1)} %collective-permute-done.1.low_ref, bf16[1024,2304]{1,0:T(8,128)(2,1)} %collective-permute-done.2.high_ref), custom_call_target="tpu_custom_call" | custom-call | flops 4831838208 | bytes 28311552 | tf_op jit(solution)/shard_map/pack/pallas_call | solution.py:117
  65.7 179.1 %mlp.6 = (bf16[2,480,2304]{2,1,0:T(8,128)(2,1)}, bf16[2,480,2304]{2,1,0:T(8,128)(2,1)}) custom-call(s32[2]{0:T(128)} %get-tuple-element.50.tiles_ref, bf16[2,768,2304]{2,1,0:T(8,128)(2,1)} %pack.4.one_ref, bf16[2,768,2304]{2,1,0:T(8,128)(2,1)} %pack.5.two_ref, bf16[2,2304,5760]{2,1,0:T(8,128)(2,1)} %gate_ref.11, bf16[2,2304,5760]{2,1,0:T(8,128)(2,1)} %up_ref.11, ...), custom_call_target="tpu_custom_call" | custom-call | flops 152882380800 | bytes 159252480 | tf_op jit(solution)/shard_map/mlp/pallas_call | solution.py:193
  246.1 67.4 %mlp.7 = (bf16[2,160,2304]{2,1,0:T(8,128)(2,1)}, bf16[2,160,2304]{2,1,0:T(8,128)(2,1)}) custom-call(s32[2]{0:T(128)} %get-tuple-element.51.tiles_ref, bf16[2,768,2304]{2,1,0:T(8,128)(2,1)} %pack.4.one_ref, bf16[2,768,2304]{2,1,0:T(8,128)(2,1)} %pack.5.two_ref, bf16[2,2304,5760]{2,1,0:T(8,128)(2,1)} %gate_ref.11, bf16[2,2304,5760]{2,1,0:T(8,128)(2,1)} %up_ref.11, ...), custom_call_target="tpu_custom_call" | custom-call | flops 50960793600 | bytes 159252480 | tf_op jit(solution)/shard_map/mlp/pallas_call | solution.py:193
  314.0 11.3 %pack.6.one_ref = bf16[2,768,2304]{2,1,0:T(8,128)(2,1)} custom-call(s32[10]{0:T(128)} %reshape.111.start_ref, s32[2,2048]{1,0:T(2,128)} %slice.116.pos_ref, bf16[1024,2304]{1,0:T(8,128)(2,1)} %collective-permute-done.7.low_ref, bf16[1024,2304]{1,0:T(8,128)(2,1)} %collective-permute-done.8.high_ref), custom_call_target="tpu_custom_call" | custom-call | flops 4831838208 | bytes 28311552 | tf_op jit(solution)/shard_map/pack/pallas_call | solution.py:117
  325.3 11.2 %pack.7.two_ref = bf16[2,768,2304]{2,1,0:T(8,128)(2,1)} custom-call(s32[10]{0:T(128)} %reshape.112.start_ref, s32[2,2048]{1,0:T(2,128)} %slice.118.pos_ref, bf16[1024,2304]{1,0:T(8,128)(2,1)} %collective-permute-done.9.low_ref, bf16[1024,2304]{1,0:T(8,128)(2,1)} %collective-permute-done.10.high_ref), custom_call_target="tpu_custom_call" | custom-call | flops 4831838208 | bytes 28311552 | tf_op jit(solution)/shard_map/pack/pallas_call | solution.py:117
  336.5 10.8 %mlp.11 = (bf16[2,160,2304]{2,1,0:T(8,128)(2,1)}, bf16[2,160,2304]{2,1,0:T(8,128)(2,1)}) custom-call(s32[2]{0:T(128)} %get-tuple-element.55.tiles_ref, bf16[2,768,2304]{2,1,0:T(8,128)(2,1)} %pack.6.one_ref, bf16[2,768,2304]{2,1,0:T(8,128)(2,1)} %pack.7.two_ref, bf16[2,2304,5760]{2,1,0:T(8,128)(2,1)} %gate_ref.11, bf16[2,2304,5760]{2,1,0:T(8,128)(2,1)} %up_ref.11, ...), custom_call_target="tpu_custom_call" | custom-call | flops 50960793600 | bytes 159252480 | tf_op jit(solution)/shard_map/mlp/pallas_call | solution.py:193
  347.3 33.4 %collective-permute-start.18 = (bf16[2,160,2304]{2,1,0:T(8,128)(2,1)}, bf16[2,160,2304]{2,1,0:T(8,128)(2,1)}, u32[]{:S(2)}, u32[]{:S(2)}) collective-permute-start(bf16[2,160,2304]{2,1,0:T(8,128)(2,1)} %get-tuple-element.28), channel_id=1, source_target_pairs={{0,3},{1,2},{2,1},{3,0},{4,7},{5,6},{6,5},{7,4},{8,11},{9,10},{10,... | collective-permute-start | bytes 4423688 | tf_op jit(solution)/shard_map/ppermute | solution.py:273
  380.7 67.6 %mlp.10 = (bf16[2,160,2304]{2,1,0:T(8,128)(2,1)}, bf16[2,160,2304]{2,1,0:T(8,128)(2,1)}) custom-call(s32[2]{0:T(128)} %get-tuple-element.54.tiles_ref, bf16[2,768,2304]{2,1,0:T(8,128)(2,1)} %pack.6.one_ref, bf16[2,768,2304]{2,1,0:T(8,128)(2,1)} %pack.7.two_ref, bf16[2,2304,5760]{2,1,0:T(8,128)(2,1)} %gate_ref.11, bf16[2,2304,5760]{2,1,0:T(8,128)(2,1)} %up_ref.11, ...), custom_call_target="tpu_custom_call" | custom-call | flops 50960793600 | bytes 159252480 | tf_op jit(solution)/shard_map/mlp/pallas_call | solution.py:193
  448.2 67.4 %mlp.9 = (bf16[2,160,2304]{2,1,0:T(8,128)(2,1)}, bf16[2,160,2304]{2,1,0:T(8,128)(2,1)}) custom-call(s32[2]{0:T(128)} %get-tuple-element.53.tiles_ref, bf16[2,768,2304]{2,1,0:T(8,128)(2,1)} %pack.6.one_ref, bf16[2,768,2304]{2,1,0:T(8,128)(2,1)} %pack.7.two_ref, bf16[2,2304,5760]{2,1,0:T(8,128)(2,1)} %gate_ref.11, bf16[2,2304,5760]{2,1,0:T(8,128)(2,1)} %up_ref.11, ...), custom_call_target="tpu_custom_call" | custom-call | flops 50960793600 | bytes 159252480 | tf_op jit(solution)/shard_map/mlp/pallas_call | solution.py:193
  515.6 67.4 %mlp.8 = (bf16[2,160,2304]{2,1,0:T(8,128)(2,1)}, bf16[2,160,2304]{2,1,0:T(8,128)(2,1)}) custom-call(s32[2]{0:T(128)} %get-tuple-element.52.tiles_ref, bf16[2,768,2304]{2,1,0:T(8,128)(2,1)} %pack.6.one_ref, bf16[2,768,2304]{2,1,0:T(8,128)(2,1)} %pack.7.two_ref, bf16[2,2304,5760]{2,1,0:T(8,128)(2,1)} %gate_ref.11, bf16[2,2304,5760]{2,1,0:T(8,128)(2,1)} %up_ref.11, ...), custom_call_target="tpu_custom_call" | custom-call | flops 50960793600 | bytes 159252480 | tf_op jit(solution)/shard_map/mlp/pallas_call | solution.py:193
  583.0 1.7 collective-permute-start.13
  584.8 1.7 collective-permute-start.14
  588.2 4.9 gate.3
  593.0 4.9 gate.2
  600.0 27.0 %mix.2.base_ref = f32[2048,2304]{1,0:T(8,128)} custom-call(s32[136]{0:T(256)} %min.40.start_ref, bf16[2048,2304]{1,0:T(8,128)(2,1)} %base_ref.1, s32[2048,8]{1,0:T(8,128)} %bitcast.18, f32[2048,8]{1,0:T(8,128)} %bitcast.20, bf16[2,480,2304]{2,1,0:T(8,128)(2,1)} %get-tuple-element.17.rest_0_, bf16[2,160,2304]{2,1,0:T(8,128)(2,1)} %get-tuple-element.18.rest_1_, ...), custom_call_target="tpu_custom_call" | custom-call | flops 9663676416 | bytes 47185920 | tf_op jit(solution)/shard_map/mix/pallas_call | solution.py:251
  627.0 22.2 %collective-permute-done.13.rest_2_ = bf16[2,160,2304]{2,1,0:T(8,128)(2,1)} collective-permute-done((bf16[2,160,2304]{2,1,0:T(8,128)(2,1)}, bf16[2,160,2304]{2,1,0:T(8,128)(2,1)}, u32[]{:S(2)}, u32[]{:S(2)}) %collective-permute-start.13) | collective-permute-done | bytes 1474592 | tf_op jit(solution)/shard_map/ppermute | solution.py:273
  649.2 31.9 %collective-permute-done.14.rest_3_ = bf16[2,160,2304]{2,1,0:T(8,128)(2,1)} collective-permute-done((bf16[2,160,2304]{2,1,0:T(8,128)(2,1)}, bf16[2,160,2304]{2,1,0:T(8,128)(2,1)}, u32[]{:S(2)}, u32[]{:S(2)}) %collective-permute-start.14) | collective-permute-done | bytes 1474592 | tf_op jit(solution)/shard_map/ppermute | solution.py:273
  681.1 31.3 %collective-permute-done.11.rest_0_ = bf16[2,160,2304]{2,1,0:T(8,128)(2,1)} collective-permute-done((bf16[2,160,2304]{2,1,0:T(8,128)(2,1)}, bf16[2,160,2304]{2,1,0:T(8,128)(2,1)}, u32[]{:S(2)}, u32[]{:S(2)}) %collective-permute-start.11) | collective-permute-done | bytes 1474592 | tf_op jit(solution)/shard_map/ppermute | solution.py:273
  712.4 31.6 %collective-permute-done.12.rest_1_ = bf16[2,160,2304]{2,1,0:T(8,128)(2,1)} collective-permute-done((bf16[2,160,2304]{2,1,0:T(8,128)(2,1)}, bf16[2,160,2304]{2,1,0:T(8,128)(2,1)}, u32[]{:S(2)}, u32[]{:S(2)}) %collective-permute-start.12) | collective-permute-done | bytes 1474592 | tf_op jit(solution)/shard_map/ppermute | solution.py:273
  744.0 27.0 %mix.3 = bf16[2048,2304]{1,0:T(8,128)(2,1)} custom-call(s32[136]{0:T(256)} %min.40.start_ref, f32[2048,2304]{1,0:T(8,128)} %mix.2.base_ref, s32[2048,8]{1,0:T(8,128)} %bitcast.19, f32[2048,8]{1,0:T(8,128)} %bitcast.21, bf16[2,160,2304]{2,1,0:T(8,128)(2,1)} %collective-permute-done.11.rest_0_, bf16[2,160,2304]{2,1,0:T(8,128)(2,1)} %collective-permute-done.12.rest_1_, ...), custom_call_target="tpu_custom_call" | custom-call | flops 9663676416 | bytes 47185920 | tf_op jit(solution)/shard_map/mix/pallas_call | solution.py:251
  (79 shorter events, 30.6 us)
Async XLA Ops:
  9.3 44.3 %collective-permute-start.1 = (bf16[1024,2304]{1,0:T(8,128)(2,1)}, bf16[1024,2304]{1,0:T(8,128)(2,1)}, u32[]{:S(2)}, u32[]{:S(2)}) collective-permute-start(bf16[1024,2304]{1,0:T(8,128)(2,1)} %norm.2.u_ref.low_ref), channel_id=1, source_target_pairs={{0,1},{1,0},{2,3},{3,2},{4,5},{5,4},{6,7},{7,6},{8,9},{9,8},{10,11... | collective-permute-start | bytes 14155784 | tf_op jit(solution)/shard_map/ppermute | solution.py:273
  16.7 36.9 %collective-permute-start.2 = (bf16[1024,2304]{1,0:T(8,128)(2,1)}, bf16[1024,2304]{1,0:T(8,128)(2,1)}, u32[]{:S(2)}, u32[]{:S(2)}) collective-permute-start(bf16[1024,2304]{1,0:T(8,128)(2,1)} %norm.3.u_ref.high_ref), channel_id=1, source_target_pairs={{0,1},{1,0},{2,3},{3,2},{4,5},{5,4},{6,7},{7,6},{8,9},{9,8},{10,11... | collective-permute-start | bytes 14155784 | tf_op jit(solution)/shard_map/ppermute | solution.py:273
  17.4 0.6 copy-start.1
  22.1 4.6 copy-start
  22.3 0.7 copy-start.2
  23.0 3.1 copy-start.3
  24.0 16.4 %collective-permute-start.5 = (s32[2,2176]{1,0:T(2,128)}, s32[2,2176]{1,0:T(2,128)}, u32[]{:S(2)}, u32[]{:S(2)}) collective-permute-start(s32[2,2176]{1,0:T(2,128)} %get-tuple-element.45), channel_id=1, source_target_pairs={{0,2},{1,3},{2,0},{3,1},{4,6},{5,7},{6,4},{7,5},{8,10},{9,11},{10,... | collective-permute-start | bytes 52232 | tf_op jit(solution)/shard_map/ppermute | solution.py:273
  24.2 17.6 %collective-permute-start = (s32[2,2176]{1,0:T(2,128)}, s32[2,2176]{1,0:T(2,128)}, u32[]{:S(2)}, u32[]{:S(2)}) collective-permute-start(s32[2,2176]{1,0:T(2,128)} %get-tuple-element.46), channel_id=1, source_target_pairs={{0,1},{1,0},{2,3},{3,2},{4,5},{5,4},{6,7},{7,6},{8,9},{9,8},{10,11... | collective-permute-start | bytes 52232 | tf_op jit(solution)/shard_map/ppermute | solution.py:273
  25.0 19.4 %collective-permute-start.6 = (s32[2,2176]{1,0:T(2,128)}, s32[2,2176]{1,0:T(2,128)}, u32[]{:S(2)}, u32[]{:S(2)}) collective-permute-start(s32[2,2176]{1,0:T(2,128)} %get-tuple-element.47), channel_id=1, source_target_pairs={{0,3},{1,2},{2,1},{3,0},{4,7},{5,6},{6,5},{7,4},{8,11},{9,10},{10,... | collective-permute-start | bytes 52232 | tf_op jit(solution)/shard_map/ppermute | solution.py:273
  40.4 204.5 %collective-permute-start.7 = (bf16[1024,2304]{1,0:T(8,128)(2,1)}, bf16[1024,2304]{1,0:T(8,128)(2,1)}, u32[]{:S(2)}, u32[]{:S(2)}) collective-permute-start(bf16[1024,2304]{1,0:T(8,128)(2,1)} %norm.2.u_ref.low_ref), channel_id=1, source_target_pairs={{0,2},{1,3},{2,0},{3,1},{4,6},{5,7},{6,4},{7,5},{8,10},{9,11},{10,... | collective-permute-start | bytes 14155784 | tf_op jit(solution)/shard_map/ppermute | solution.py:273
  41.9 203.3 %collective-permute-start.8 = (bf16[1024,2304]{1,0:T(8,128)(2,1)}, bf16[1024,2304]{1,0:T(8,128)(2,1)}, u32[]{:S(2)}, u32[]{:S(2)}) collective-permute-start(bf16[1024,2304]{1,0:T(8,128)(2,1)} %norm.3.u_ref.high_ref), channel_id=1, source_target_pairs={{0,2},{1,3},{2,0},{3,1},{4,6},{5,7},{6,4},{7,5},{8,10},{9,11},{10,... | collective-permute-start | bytes 14155784 | tf_op jit(solution)/shard_map/ppermute | solution.py:273
  244.9 80.4 %collective-permute-start.9 = (bf16[1024,2304]{1,0:T(8,128)(2,1)}, bf16[1024,2304]{1,0:T(8,128)(2,1)}, u32[]{:S(2)}, u32[]{:S(2)}) collective-permute-start(bf16[1024,2304]{1,0:T(8,128)(2,1)} %collective-permute-done.7.low_ref), channel_id=1, source_target_pairs={{0,1},{1,0},{2,3},{3,2},{4,5},{5,4},{6,7},{7,6},{8,9},{9,8},{10,11... | collective-permute-start | bytes 14155784 | tf_op jit(solution)/shard_map/ppermute | solution.py:273
  245.2 80.1 %collective-permute-start.10 = (bf16[1024,2304]{1,0:T(8,128)(2,1)}, bf16[1024,2304]{1,0:T(8,128)(2,1)}, u32[]{:S(2)}, u32[]{:S(2)}) collective-permute-start(bf16[1024,2304]{1,0:T(8,128)(2,1)} %collective-permute-done.8.high_ref), channel_id=1, source_target_pairs={{0,1},{1,0},{2,3},{3,2},{4,5},{5,4},{6,7},{7,6},{8,9},{9,8},{10,11... | collective-permute-start | bytes 14155784 | tf_op jit(solution)/shard_map/ppermute | solution.py:273
  313.5 269.5 %collective-permute-start.4 = (bf16[2,160,2304]{2,1,0:T(8,128)(2,1)}, bf16[2,160,2304]{2,1,0:T(8,128)(2,1)}, u32[]{:S(2)}, u32[]{:S(2)}) collective-permute-start(bf16[2,160,2304]{2,1,0:T(8,128)(2,1)} %get-tuple-element.20), channel_id=1, source_target_pairs={{0,1},{1,0},{2,3},{3,2},{4,5},{5,4},{6,7},{7,6},{8,9},{9,8},{10,11... | collective-permute-start | bytes 4423688 | tf_op jit(solution)/shard_map/ppermute | solution.py:273
  313.5 269.5 %collective-permute-start.3 = (bf16[2,480,2304]{2,1,0:T(8,128)(2,1)}, bf16[2,480,2304]{2,1,0:T(8,128)(2,1)}, u32[]{:S(2)}, u32[]{:S(2)}) collective-permute-start(bf16[2,480,2304]{2,1,0:T(8,128)(2,1)} %get-tuple-element.19), channel_id=1, source_target_pairs={{0,1},{1,0},{2,3},{3,2},{4,5},{5,4},{6,7},{7,6},{8,9},{9,8},{10,11... | collective-permute-start | bytes 13271048 | tf_op jit(solution)/shard_map/ppermute | solution.py:273
  347.3 237.5 %collective-permute-start.17 = (bf16[2,160,2304]{2,1,0:T(8,128)(2,1)}, bf16[2,160,2304]{2,1,0:T(8,128)(2,1)}, u32[]{:S(2)}, u32[]{:S(2)}) collective-permute-start(bf16[2,160,2304]{2,1,0:T(8,128)(2,1)} %get-tuple-element.27), channel_id=1, source_target_pairs={{0,2},{1,3},{2,0},{3,1},{4,6},{5,7},{6,4},{7,5},{8,10},{9,11},{10,... | collective-permute-start | bytes 4423688 | tf_op jit(solution)/shard_map/ppermute | solution.py:273
  347.3 239.2 %collective-permute-start.18 = (bf16[2,160,2304]{2,1,0:T(8,128)(2,1)}, bf16[2,160,2304]{2,1,0:T(8,128)(2,1)}, u32[]{:S(2)}, u32[]{:S(2)}) collective-permute-start(bf16[2,160,2304]{2,1,0:T(8,128)(2,1)} %get-tuple-element.28), channel_id=1, source_target_pairs={{0,3},{1,2},{2,1},{3,0},{4,7},{5,6},{6,5},{7,4},{8,11},{9,10},{10,... | collective-permute-start | bytes 4423688 | tf_op jit(solution)/shard_map/ppermute | solution.py:273
  448.2 138.3 %collective-permute-start.15 = (bf16[2,160,2304]{2,1,0:T(8,128)(2,1)}, bf16[2,160,2304]{2,1,0:T(8,128)(2,1)}, u32[]{:S(2)}, u32[]{:S(2)}) collective-permute-start(bf16[2,160,2304]{2,1,0:T(8,128)(2,1)} %get-tuple-element.25), channel_id=1, source_target_pairs={{0,2},{1,3},{2,0},{3,1},{4,6},{5,7},{6,4},{7,5},{8,10},{9,11},{10,... | collective-permute-start | bytes 4423688 | tf_op jit(solution)/shard_map/ppermute | solution.py:273
  583.0 44.0 %collective-permute-start.16 = (bf16[2,160,2304]{2,1,0:T(8,128)(2,1)}, bf16[2,160,2304]{2,1,0:T(8,128)(2,1)}, u32[]{:S(2)}, u32[]{:S(2)}) collective-permute-start(bf16[2,160,2304]{2,1,0:T(8,128)(2,1)} %get-tuple-element.26), channel_id=1, source_target_pairs={{0,3},{1,2},{2,1},{3,0},{4,7},{5,6},{6,5},{7,4},{8,11},{9,10},{10,... | collective-permute-start | bytes 4423688 | tf_op jit(solution)/shard_map/ppermute | solution.py:273
  583.0 66.2 %collective-permute-start.13 = (bf16[2,160,2304]{2,1,0:T(8,128)(2,1)}, bf16[2,160,2304]{2,1,0:T(8,128)(2,1)}, u32[]{:S(2)}, u32[]{:S(2)}) collective-permute-start(bf16[2,160,2304]{2,1,0:T(8,128)(2,1)} %get-tuple-element.23), channel_id=1, source_target_pairs={{0,2},{1,3},{2,0},{3,1},{4,6},{5,7},{6,4},{7,5},{8,10},{9,11},{10,... | collective-permute-start | bytes 4423688 | tf_op jit(solution)/shard_map/ppermute | solution.py:273
  584.8 96.3 %collective-permute-start.14 = (bf16[2,160,2304]{2,1,0:T(8,128)(2,1)}, bf16[2,160,2304]{2,1,0:T(8,128)(2,1)}, u32[]{:S(2)}, u32[]{:S(2)}) collective-permute-start(bf16[2,160,2304]{2,1,0:T(8,128)(2,1)} %get-tuple-element.24), channel_id=1, source_target_pairs={{0,3},{1,2},{2,1},{3,0},{4,7},{5,6},{6,5},{7,4},{8,11},{9,10},{10,... | collective-permute-start | bytes 4423688 | tf_op jit(solution)/shard_map/ppermute | solution.py:273
  586.5 125.9 %collective-permute-start.11 = (bf16[2,160,2304]{2,1,0:T(8,128)(2,1)}, bf16[2,160,2304]{2,1,0:T(8,128)(2,1)}, u32[]{:S(2)}, u32[]{:S(2)}) collective-permute-start(bf16[2,160,2304]{2,1,0:T(8,128)(2,1)} %get-tuple-element.21), channel_id=1, source_target_pairs={{0,2},{1,3},{2,0},{3,1},{4,6},{5,7},{6,4},{7,5},{8,10},{9,11},{10,... | collective-permute-start | bytes 4423688 | tf_op jit(solution)/shard_map/ppermute | solution.py:273
  586.5 157.5 %collective-permute-start.12 = (bf16[2,160,2304]{2,1,0:T(8,128)(2,1)}, bf16[2,160,2304]{2,1,0:T(8,128)(2,1)}, u32[]{:S(2)}, u32[]{:S(2)}) collective-permute-start(bf16[2,160,2304]{2,1,0:T(8,128)(2,1)} %get-tuple-element.22), channel_id=1, source_target_pairs={{0,3},{1,2},{2,1},{3,0},{4,7},{5,6},{6,5},{7,4},{8,11},{9,10},{10,... | collective-permute-start | bytes 4423688 | tf_op jit(solution)/shard_map/ppermute | solution.py:273

commit v3 on v2

--- a/solution.py
+++ b/solution.py
@@ -12,28 +12,83 @@
 F32, BF16, I32 = jnp.float32, jnp.bfloat16, jnp.int32
 VMEM_LIMIT = 67043328
 NORM_ROWS = 256
+NORM_GROUP = 16
+GATE_ROWS = 512
 PACK_ROWS = 512
 PACK_WIN = 128
 TILE = 160
 FF_BLOCK = 1280
 FF_SPLIT = 768
-MIX_ROWS = 128
+MIX_ROWS = 256
 MIX_WIN = 256
+WIDE_WIN = 272
+LANES = 128
 MIX_COLS = 256
 
 
+def route_kernel(capacity, first_ref, choice_ref, table_ref, rel_ref, *meta_refs):
+    experts = table_ref.shape[0]
+    tokens = choice_ref.shape[1]
+    rows = meta_refs[0].shape[0]
+    rel = choice_ref[...] ^ first_ref[0]
+    rel_ref[...] = rel
+    ids = lax.broadcasted_iota(I32, (experts, LANES), 0)
+    lane = lax.broadcasted_iota(I32, (experts, LANES), 1)
+    earlier = (lax.broadcasted_iota(I32, (LANES, LANES), 0) < lax.broadcasted_iota(I32, (LANES, LANES), 1))
+    earlier = earlier.astype(F32).astype(BF16)
+    carry = jnp.zeros((experts, 1), F32)
+    marks = jnp.zeros((experts, LANES), F32)
+
+    def store(block, lo):
+        table_ref[:, lo:lo + LANES] = block
+        for m, ref in enumerate(meta_refs):
+            ref[:, lo:lo + LANES] = block[m * rows:(m + 1) * rows, :]
+
+    for n in range(tokens // LANES):
+        lo = n * LANES
+        hit = ((rel[0:1, lo:lo + LANES] == ids) | (rel[1:2, lo:lo + LANES] == ids)).astype(F32)
+        before = jnp.dot(hit.astype(BF16), earlier, preferred_element_type=F32) + carry
+        kept = (hit > 0) & (before < capacity)
+        store(jnp.where(kept, before, -1.0).astype(I32), lo)
+        marks = jnp.where(lane == n, carry, marks)
+        carry = carry + jnp.sum(hit, axis=1, keepdims=True)
+    marks = jnp.where(lane == tokens // LANES, carry, marks)
+    store(jnp.minimum(marks, float(capacity)).astype(I32), tokens)
+
+
+def route_call(first, choice_t, experts, local, capacity):
+    tokens = choice_t.shape[1]
+    table = lambda n: jax.ShapeDtypeStruct((n, tokens + LANES), I32)
+    return pl.pallas_call(
+        functools.partial(route_kernel, capacity),
+        in_specs=[pl.BlockSpec(memory_space=pltpu.SMEM), pl.BlockSpec(memory_space=pltpu.VMEM)],
+        out_specs=[pl.BlockSpec(memory_space=pltpu.VMEM)] * (2 + experts // local),
+        out_shape=[table(experts), jax.ShapeDtypeStruct((2, tokens), I32)] + [table(local)] * (experts // local),
+        cost_estimate=pl.CostEstimate(flops=1 << 24, bytes_accessed=1 << 18, transcendentals=0),
+        name="route",
+    )(first, choice_t)
+
+
 def norm_kernel(x_ref, gamma_ref, beta_ref, u_ref):
-    values = x_ref[...].astype(F32)
-    centred = values - jnp.mean(values, axis=-1, keepdims=True)
-    variance = jnp.mean(centred * centred, axis=-1, keepdims=True)
-    u_ref[...] = (centred * lax.rsqrt(variance + LN_EPS) * gamma_ref[...] + beta_ref[...]).astype(BF16)
+    gamma = gamma_ref[...][None, :]
+    beta = beta_ref[...][None, :]
+
+    def group(n, carry):
+        rows = pl.ds(pl.multiple_of(n * NORM_GROUP, NORM_GROUP), NORM_GROUP)
+        values = x_ref[rows, :].astype(F32)
+        centred = values - jnp.mean(values, axis=-1, keepdims=True)
+        variance = jnp.mean(centred * centred, axis=-1, keepdims=True)
+        u_ref[rows, :] = (centred * lax.rsqrt(variance + LN_EPS) * gamma + beta).astype(BF16)
+        return carry
+
+    lax.fori_loop(0, x_ref.shape[0] // NORM_GROUP, group, 0, unroll=4)
 
 
 def norm_call(part, parts, hidden, gamma, beta):
     tokens, width = hidden.shape
     rows = tokens // parts
     steps = rows // NORM_ROWS
-    vector = pl.BlockSpec((1, width), lambda i: (0, 0))
+    vector = pl.BlockSpec((width,), lambda i: (0,))
     return pl.pallas_call(
         norm_kernel,
         grid=(steps,),
@@ -62,14 +117,14 @@
 def gate_call(part, u, router_t, choice_t, rel_t, first_t, second_t):
     rows, width = u.shape
     experts = router_t.shape[0]
-    steps = rows // NORM_ROWS
-    lanes = lambda n: pl.BlockSpec((n, NORM_ROWS), lambda i: (0, i + part * steps))
+    steps = rows // GATE_ROWS
+    lanes = lambda n: pl.BlockSpec((n, GATE_ROWS), lambda i: (0, i + part * steps))
     return pl.pallas_call(
         gate_kernel,
         grid=(steps,),
-        in_specs=[pl.BlockSpec((NORM_ROWS, width), lambda i: (i, 0)), pl.BlockSpec((experts, width), lambda i: (0, 0)),
+        in_specs=[pl.BlockSpec((GATE_ROWS, width), lambda i: (i, 0)), pl.BlockSpec((experts, width), lambda i: (0, 0)),
                   lanes(2), lanes(2), lanes(experts), lanes(experts)],
-        out_specs=pl.BlockSpec((experts, NORM_ROWS), lambda i: (0, i)),
+        out_specs=pl.BlockSpec((experts, GATE_ROWS), lambda i: (0, i)),
         out_shape=jax.ShapeDtypeStruct((experts, rows), F32),
         compiler_params=pltpu.CompilerParams(vmem_limit_bytes=VMEM_LIMIT),
         cost_estimate=pl.CostEstimate(flops=rows * width * 60, bytes_accessed=rows * width * 2, transcendentals=0),
@@ -77,10 +132,14 @@
     )(u, router_t, choice_t, rel_t, first_t, second_t)
 
 
-def pack_kernel(half_steps, start_ref, pos_ref, low_ref, high_ref, rows_ref):
+def mark(tokens, rows, block):
+    return tokens + block * (rows // LANES)
+
+
+def pack_kernel(half_steps, meta_ref, pos_ref, low_ref, high_ref, rows_ref):
     step = pl.program_id(0)
     experts = rows_ref.shape[0]
-    steps = 2 * half_steps
+    tokens = 2 * half_steps * PACK_ROWS
 
     @pl.when(step == 0)
     def _():
@@ -88,8 +147,8 @@
 
     def pack(block_ref):
         for e in range(experts):
-            begin = start_ref[e * (steps + 1) + step]
-            end = start_ref[e * (steps + 1) + step + 1]
+            begin = meta_ref[e, mark(tokens, PACK_ROWS, step)]
+            end = meta_ref[e, mark(tokens, PACK_ROWS, step + 1)]
             base = (begin // 16) * 16
             windows = jnp.where(end > begin, (end - base + PACK_WIN - 1) // PACK_WIN, 0)
             slots = jnp.broadcast_to(pos_ref[e:e + 1, :], (PACK_WIN, PACK_ROWS))
@@ -109,9 +168,9 @@
     pl.when(step >= half_steps)(lambda: pack(high_ref))
 
 
-def pack_call(starts, pos, low, high, capacity):
+def pack_call(meta, low, high, capacity):
     half, width = low.shape
-    experts = pos.shape[0]
+    experts = meta.shape[0]
     half_steps = half // PACK_ROWS
     padded = (capacity + PACK_WIN - 1) // PACK_WIN * PACK_WIN + PACK_WIN
     return pl.pallas_call(
@@ -129,38 +188,49 @@
         cost_estimate=pl.CostEstimate(flops=experts * 2 * half * PACK_ROWS * width, bytes_accessed=4 * half * width * 3,
                                       transcendentals=0),
         name="pack",
-    )(starts, pos, low, high)
-
-
-def mlp_kernel(splits, tail_splits, tiles_ref, one_ref, two_ref, gate_ref, up_ref, down_ref, out_one_ref, out_two_ref, acc_ref):
-    step = pl.program_id(1)
-    tiles = tiles_ref[pl.program_id(0)]
+    )(meta, meta, low, high)
+
+
+def row_tiles(begin, rows, tokens, expert, one_meta_ref, two_meta_ref):
+    last = mark(tokens, tokens, 1)
+    most = jnp.maximum(one_meta_ref[expert, last], two_meta_ref[expert, last])
+    return jnp.clip((most - begin + TILE - 1) // TILE, 0, rows // TILE)
+
+
+def tail_step(expert, step, steps):
+    return step == jnp.where(expert % 2 == 0, 0, steps - 1)
+
+
+def mlp_kernel(begin, tokens, splits, tail_splits, one_meta_ref, two_meta_ref, one_ref, two_ref, gate_ref, up_ref, down_ref, out_one_ref, out_two_ref, acc_ref):
+    expert, step, steps = pl.program_id(0), pl.program_id(1), pl.num_programs(1)
     rows = out_one_ref.shape[1]
-
-    def accumulate(parts, first):
+    tiles = row_tiles(begin, rows, tokens, expert, one_meta_ref, two_meta_ref)
+    is_tail = tail_step(expert, step, steps)
+
+    def accumulate(parts):
         def tile(i, carry):
             at = pl.multiple_of(i * TILE, TILE)
             both = pl.ds(pl.multiple_of(i * 2 * TILE, 2 * TILE), 2 * TILE)
-            tokens = jnp.concatenate([one_ref[0, pl.ds(at, TILE), :], two_ref[0, pl.ds(at, TILE), :]], axis=0)
+            taken = jnp.concatenate([one_ref[0, pl.ds(at, TILE), :], two_ref[0, pl.ds(at, TILE), :]], axis=0)
             projs = []
             for lo, hi in parts:
                 joined = jnp.concatenate([gate_ref[0, :, lo:hi], up_ref[0, :, lo:hi]], axis=1)
-                projs.append(jnp.dot(tokens, joined, preferred_element_type=F32))
+                projs.append(jnp.dot(taken, joined, preferred_element_type=F32))
             for n, (lo, hi) in enumerate(parts):
                 inner = (jax.nn.silu(projs[n][:, :hi - lo]) * projs[n][:, hi - lo:]).astype(BF16)
                 down = jnp.dot(inner, down_ref[0, lo:hi, :], preferred_element_type=F32)
-                if first and n == 0:
-                    acc_ref[both, :] = down
-                else:
-                    acc_ref[both, :] += down
+                held = acc_ref[both, :]
+                if n == 0:
+                    held = jnp.where(step == 0, 0.0, held)
+                acc_ref[both, :] = held + down
             return carry
 
         lax.fori_loop(0, tiles, tile, 0)
 
-    pl.when(step == 0)(lambda: accumulate(tail_splits, True))
-    pl.when(step > 0)(lambda: accumulate(splits, False))
-
-    @pl.when(step == pl.num_programs(1) - 1)
+    pl.when(is_tail)(lambda: accumulate(tail_splits))
+    pl.when(jnp.logical_not(is_tail))(lambda: accumulate(splits))
+
+    @pl.when(step == steps - 1)
     def _():
         for i in range(rows // TILE):
             outs = [(ref, (2 * i + n) * TILE) for n, ref in enumerate((out_one_ref, out_two_ref))]
@@ -176,27 +246,28 @@
                     ref[0, i * TILE:(i + 1) * TILE, :] = jnp.zeros((TILE, ref.shape[2]), BF16)
 
 
-def mlp_call(rows, chunk, tiles, packed_one, packed_two, w_gate, w_up, w_down):
+def mlp_call(tokens, begin, rows, meta_one, meta_two, packed_one, packed_two, w_gate, w_up, w_down):
     experts, width, ff = w_gate.shape
     full_steps, tail = divmod(ff, FF_BLOCK)
     splits = ((0, FF_SPLIT), (FF_SPLIT, FF_BLOCK))
     tail_splits = ((0, tail),)
     once = pl.Buffered(1)
 
-    def block(e, f, t):
-        return jnp.where((f == 0) | (t[e] == 0), full_steps, f - 1)
-
-    packed_spec = pl.BlockSpec((1, rows, width), lambda e, f, t: (e, chunk, 0), pipeline_mode=once)
-    out_spec = pl.BlockSpec((1, rows, width), lambda e, f, t: (e, 0, 0), pipeline_mode=once)
-    in_spec = pl.BlockSpec((1, width, FF_BLOCK), lambda e, f, t: (e, 0, block(e, f, t)))
+    def block(e, f, one, two):
+        idle = row_tiles(begin, rows, tokens, e, one, two) == 0
+        return jnp.where(tail_step(e, f, full_steps + 1) | idle, full_steps, jnp.where(e % 2 == 0, f - 1, f))
+
+    packed_spec = pl.BlockSpec((1, rows, width), lambda e, f, one, two: (e, begin // rows, 0), pipeline_mode=once)
+    out_spec = pl.BlockSpec((1, rows, width), lambda e, f, one, two: (e, 0, 0), pipeline_mode=once)
+    in_spec = pl.BlockSpec((1, width, FF_BLOCK), lambda e, f, one, two: (e, 0, block(e, f, one, two)))
     out = jax.ShapeDtypeStruct((experts, rows, width), BF16)
     return pl.pallas_call(
-        functools.partial(mlp_kernel, splits, tail_splits),
+        functools.partial(mlp_kernel, begin, tokens, splits, tail_splits),
         grid_spec=pltpu.PrefetchScalarGridSpec(
-            num_scalar_prefetch=1,
+            num_scalar_prefetch=2,
             grid=(experts, full_steps + 1),
             in_specs=[packed_spec, packed_spec, in_spec, in_spec,
-                      pl.BlockSpec((1, FF_BLOCK, width), lambda e, f, t: (e, block(e, f, t), 0))],
+                      pl.BlockSpec((1, FF_BLOCK, width), lambda e, f, one, two: (e, block(e, f, one, two), 0))],
             out_specs=[out_spec, out_spec],
             scratch_shapes=[pltpu.VMEM((2 * rows, width), F32)],
         ),
@@ -205,13 +276,12 @@
         cost_estimate=pl.CostEstimate(flops=6 * 2 * experts * rows * width * ff, bytes_accessed=6 * experts * width * ff,
                                       transcendentals=0),
         name="mlp",
-    )(tiles, packed_one, packed_two, w_gate, w_up, w_down)
+    )(meta_one, meta_two, packed_one, packed_two, w_gate, w_up, w_down)
 
 
 def mix_kernel(columns, starts_at, capacity, start_ref, base_ref, pos_ref, gate_ref, *rest):
     piece_refs, (out_ref, held_ref, sem) = rest[:-3], rest[-3:]
     step = pl.program_id(0)
-    steps = pl.num_programs(0)
     width = base_ref.shape[1]
 
     @pl.when(step == 0)
@@ -227,21 +297,30 @@
         for copy in copies:
             copy.wait()
 
-    lane = lax.broadcasted_iota(I32, (MIX_ROWS, MIX_WIN), 1)
-    bases, onehots, gates = [], [], []
-    for column in columns:
-        begin = start_ref[column * (steps + 1) + step]
-        base = pl.multiple_of(jnp.minimum((begin // 16) * 16, capacity - MIX_WIN), 16)
-        bases.append(base)
-        onehots.append((pos_ref[:, column:column + 1] - base == lane).astype(F32).astype(BF16))
-        gates.append(gate_ref[:, column:column + 1])
-    for lo in range(0, width, MIX_COLS):
-        cols = slice(lo, lo + MIX_COLS)
-        total = base_ref[:, cols].astype(F32)
-        for n in range(len(columns)):
-            picked = jnp.dot(onehots[n], held_ref[n, pl.ds(bases[n], MIX_WIN), cols], preferred_element_type=F32)
-            total = total + gates[n] * picked
-        out_ref[:, cols] = total.astype(out_ref.dtype)
+    def spans(window):
+        for column in columns:
+            begin = start_ref[column, step * (MIX_ROWS // LANES)]
+            end = start_ref[column, (step + 1) * (MIX_ROWS // LANES)]
+            base = pl.multiple_of(jnp.minimum((begin // 16) * 16, capacity - window), 16)
+            yield base, end - base
+
+    def mix(window):
+        lane = lax.broadcasted_iota(I32, (MIX_ROWS, window), 1)
+        bases = [base for base, _ in spans(window)]
+        onehots = [(pos_ref[:, column:column + 1] - base == lane).astype(F32).astype(BF16)
+                   for column, base in zip(columns, bases)]
+        gates = [gate_ref[:, column:column + 1] for column in columns]
+        for lo in range(0, width, MIX_COLS):
+            cols = slice(lo, lo + MIX_COLS)
+            total = base_ref[:, cols].astype(F32)
+            for n in range(len(columns)):
+                picked = jnp.dot(onehots[n], held_ref[n, pl.ds(bases[n], window), cols], preferred_element_type=F32)
+                total = total + gates[n] * picked
+            out_ref[:, cols] = total.astype(out_ref.dtype)
+
+    fits = functools.reduce(jnp.logical_and, [rows <= MIX_WIN for _, rows in spans(MIX_WIN)])
+    pl.when(fits)(lambda: mix(MIX_WIN))
+    pl.when(jnp.logical_not(fits))(lambda: mix(WIDE_WIN))
 
 
 def mix_call(columns, starts_at, capacity, starts, base, pos, gates, pieces, out_dtype):
@@ -279,33 +358,23 @@
         capacity = (10 * tokens + 4 * experts - 1) // (4 * experts)
 
         choice_t = choice.T
-        rel_t = choice_t ^ (local * lax.axis_index("ep"))
-        ids = lax.broadcasted_iota(I32, (experts, 1), 0)
-        hit = ((rel_t[0:1] == ids) | (rel_t[1:2] == ids)).astype(I32)
-        through = jnp.cumsum(hit, axis=1)
-        before = through - hit
-        pos = jnp.where((hit > 0) & (before < capacity), before, -1)
-        starts = jnp.minimum(jnp.concatenate([before[:, ::MIX_ROWS], through[:, -1:]], axis=1), capacity)
-        pack_starts = starts[:, ::PACK_ROWS // MIX_ROWS]
-        marks = pack_starts.shape[1]
-        meta = jnp.concatenate([pos, jnp.pad(pack_starts, ((0, 0), (0, 128 - marks)))], axis=1)
-        metas = [meta[:local]] + [swap(meta[local * m:local * (m + 1)], m) for m in range(1, group_size)]
+        first = (local * lax.axis_index("ep")).astype(I32)[None]
+        table, rel_t, *metas = route_call(first, choice_t, experts, local, capacity)
+        metas = [metas[0]] + [swap(metas[m], m) for m in range(1, group_size)]
 
         halves = []
         for part in range(2):
-            halves.append(norm_call(part, 2, hidden, ln_gamma[None], ln_beta[None]))
+            halves.append(norm_call(part, 2, hidden, ln_gamma, ln_beta))
 
         sources = [halves, [swap(u, 1) for u in halves],
                    [swap(u, 2) for u in halves]]
         sources.append([swap(u, 1) for u in sources[2]])
 
         def pack(m):
-            return pack_call(metas[m][:, tokens:tokens + marks].reshape(-1), metas[m][:, :tokens], *sources[m], capacity)
+            return pack_call(metas[m], *sources[m], capacity)
 
         def run(m_one, m_two, begin, rows, packed):
-            most = jnp.maximum(metas[m_one][:, tokens + marks - 1], metas[m_two][:, tokens + marks - 1])
-            tiles = jnp.clip((most - begin + TILE - 1) // TILE, 0, rows // TILE)
-            return mlp_call(rows, begin // rows, tiles, *packed, w_gate, w_up, w_down)
+            return mlp_call(tokens, begin, rows, metas[m_one], metas[m_two], *packed, w_gate, w_up, w_down)
 
         early = capacity - TILE
         near = [pack(0), pack(1)]
@@ -324,13 +393,12 @@
         gates = [gate_call(part, u, w_router.T, choice_t, rel_t, mask_first.T, mask_second.T)
                  for part, u in enumerate(halves)]
         gates_t = jnp.concatenate(gates, axis=1).T
-        pos_t = pos.T
-
-        flat = starts.reshape(-1)
-        total = mix_call(tuple(range(2 * local)), ((0, 0), (0, early), (local, 0), (local, early)), capacity, flat,
+        pos_t = table[:, :tokens].T
+        marks = table[:, tokens:]
+        total = mix_call(tuple(range(2 * local)), ((0, 0), (0, early), (local, 0), (local, early)), capacity, marks,
                          hidden, pos_t, gates_t, (near_early[0], near_late[0], home_early, home_late), F32)
         starts_at = tuple((local * n, c * TILE) for c in range(capacity // TILE) for n in range(2))
-        return mix_call(tuple(range(2 * local, experts)), starts_at, capacity, flat, total, pos_t, gates_t,
+        return mix_call(tuple(range(2 * local, experts)), starts_at, capacity, marks, total, pos_t, gates_t,
                         tuple(piece for pair in far_rows for piece in pair), BF16)
 
     return jax.shard_map(device_step, mesh=mesh,

time: 780 us -> 893 us (1.14)
  the two profiles are of different devices: /device:TPU:7 before, /device:TPU:13 now
where the time goes in v3:
time: 893 us; the launch traced here: 887 us
  Pallas kernels  611 us (68%)
  waiting for transfers between devices  253 us (28%)
  starting transfers between devices  16.5 us (2%)
    pallas_call x6, Pallas kernels, mlp_call(): pl.pallas_call(functools.partial(mlp_kernel, begin, tokens, splits, tail_...  490 us
    ppermute x19, waiting for transfers between devices, swap(): lax.ppermute(array, 'ep', [(i, i ^ distance) for i in range(group_size)])  253 us
    pallas_call x4, Pallas kernels, pack_call(): pl.pallas_call(functools.partial(pack_kernel, half_steps), grid_spec=pltp...  49.5 us
    pallas_call x2, Pallas kernels, mix_call(): pl.pallas_call(functools.partial(mix_kernel, columns, starts_at, capacity...  46.6 us
  transfers between devices with their start and end apart: 19, of which 6 were waited for; matrix products, arithmetic and copies ran while one was open for 1% of the time, Pallas kernels for 65%

profile of v3, /device:TPU:13, one launch (start us, length us, event | category | flops | bytes accessed | tf_op | source)
XLA Modules:
  0.0 886.9 jit_solution(8852881895119005998)
XLA Ops:
  0.0 7.9 norm.2.u_ref.low_ref
  8.5 7.9 norm.3.u_ref.high_ref
  20.6 12.5 %pack.4.one_ref = bf16[2,768,2304]{2,1,0:T(8,128)(2,1)} custom-call(s32[2,2176]{1,0:T(2,128)} %get-tuple-element.25.meta_ref.pos_ref.one_meta_ref, s32[2,2176]{1,0:T(2,128)} %get-tuple-element.25.meta_ref.pos_ref.one_meta_ref, bf16[1024,2304]{1,0:T(8,128)(2,1)} %norm.2.u_ref.low_ref, bf16[1024,2304]{1,0:T(8,128)(2,1)} %norm.3.u_ref.high_ref), custom_call_target="tpu_custom_call" | custom-call | flops 4831838208 | bytes 28311552 | tf_op jit(solution)/shard_map/pack/pallas_call | solution.py:176
  34.8 12.0 %pack.5.two_ref = bf16[2,768,2304]{2,1,0:T(8,128)(2,1)} custom-call(s32[2,2176]{1,0:T(2,128)} %collective-permute-done.meta_ref.pos_ref.two_meta_ref, s32[2,2176]{1,0:T(2,128)} %collective-permute-done.meta_ref.pos_ref.two_meta_ref, bf16[1024,2304]{1,0:T(8,128)(2,1)} %collective-permute-done.1.low_ref, bf16[1024,2304]{1,0:T(8,128)(2,1)} %collective-permute-done.2.high_ref), custom_call_target="tpu_custom_call" | custom-call | flops 4831838208 | bytes 28311552 | tf_op jit(solution)/shard_map/pack/pallas_call | solution.py:176
  46.8 39.0 %mlp.7 = (bf16[2,160,2304]{2,1,0:T(8,128)(2,1)}, bf16[2,160,2304]{2,1,0:T(8,128)(2,1)}) custom-call(s32[2,2176]{1,0:T(2,128)} %get-tuple-element.25.meta_ref.pos_ref.one_meta_ref, s32[2,2176]{1,0:T(2,128)} %collective-permute-done.meta_ref.pos_ref.two_meta_ref, bf16[2,768,2304]{2,1,0:T(8,128)(2,1)} %pack.4.one_ref, bf16[2,768,2304]{2,1,0:T(8,128)(2,1)} %pack.5.two_ref, ...), custom_call_target="tpu_custom_call" | custom-call | flops 50960793600 | bytes 159252480 | tf_op jit(solution)/shard_map/mlp/pallas_call | solution.py:264
  85.9 33.7 %collective-permute-done.7.low_ref = bf16[1024,2304]{1,0:T(8,128)(2,1)} collective-permute-done((bf16[1024,2304]{1,0:T(8,128)(2,1)}, bf16[1024,2304]{1,0:T(8,128)(2,1)}, u32[]{:S(2)}, u32[]{:S(2)}) %collective-permute-start.7) | collective-permute-done | bytes 4718624 | tf_op jit(solution)/shard_map/ppermute | solution.py:352
  119.6 2.3 collective-permute-start.9
  121.9 98.8 %collective-permute-done.8.high_ref = bf16[1024,2304]{1,0:T(8,128)(2,1)} collective-permute-done((bf16[1024,2304]{1,0:T(8,128)(2,1)}, bf16[1024,2304]{1,0:T(8,128)(2,1)}, u32[]{:S(2)}, u32[]{:S(2)}) %collective-permute-start.8) | collective-permute-done | bytes 4718624 | tf_op jit(solution)/shard_map/ppermute | solution.py:352
  222.4 181.0 %mlp.6 = (bf16[2,480,2304]{2,1,0:T(8,128)(2,1)}, bf16[2,480,2304]{2,1,0:T(8,128)(2,1)}) custom-call(s32[2,2176]{1,0:T(2,128)} %get-tuple-element.25.meta_ref.pos_ref.one_meta_ref, s32[2,2176]{1,0:T(2,128)} %collective-permute-done.meta_ref.pos_ref.two_meta_ref, bf16[2,768,2304]{2,1,0:T(8,128)(2,1)} %pack.4.one_ref, bf16[2,768,2304]{2,1,0:T(8,128)(2,1)} %pack.5.two_ref, ...), custom_call_target="tpu_custom_call" | custom-call | flops 152882380800 | bytes 159252480 | tf_op jit(solution)/shard_map/mlp/pallas_call | solution.py:264
  403.5 12.6 %pack.6.one_ref = bf16[2,768,2304]{2,1,0:T(8,128)(2,1)} custom-call(s32[2,2176]{1,0:T(2,128)} %collective-permute-done.5.meta_ref.pos_ref.one_meta_ref, s32[2,2176]{1,0:T(2,128)} %collective-permute-done.5.meta_ref.pos_ref.one_meta_ref, bf16[1024,2304]{1,0:T(8,128)(2,1)} %collective-permute-done.7.low_ref, bf16[1024,2304]{1,0:T(8,128)(2,1)} %collective-permute-done.8.high_ref), custom_call_target="tpu_custom_call" | custom-call | flops 4831838208 | bytes 28311552 | tf_op jit(solution)/shard_map/pack/pallas_call | solution.py:176
  416.1 12.4 %pack.7.two_ref = bf16[2,768,2304]{2,1,0:T(8,128)(2,1)} custom-call(s32[2,2176]{1,0:T(2,128)} %collective-permute-done.6.meta_ref.pos_ref.two_meta_ref, s32[2,2176]{1,0:T(2,128)} %collective-permute-done.6.meta_ref.pos_ref.two_meta_ref, bf16[1024,2304]{1,0:T(8,128)(2,1)} %collective-permute-done.9.low_ref, bf16[1024,2304]{1,0:T(8,128)(2,1)} %collective-permute-done.10.high_ref), custom_call_target="tpu_custom_call" | custom-call | flops 4831838208 | bytes 28311552 | tf_op jit(solution)/shard_map/pack/pallas_call | solution.py:176
  428.5 67.4 %mlp.11 = (bf16[2,160,2304]{2,1,0:T(8,128)(2,1)}, bf16[2,160,2304]{2,1,0:T(8,128)(2,1)}) custom-call(s32[2,2176]{1,0:T(2,128)} %collective-permute-done.5.meta_ref.pos_ref.one_meta_ref, s32[2,2176]{1,0:T(2,128)} %collective-permute-done.6.meta_ref.pos_ref.two_meta_ref, bf16[2,768,2304]{2,1,0:T(8,128)(2,1)} %pack.6.one_ref, ...), custom_call_target="tpu_custom_call" | custom-call | flops 50960793600 | bytes 159252480 | tf_op jit(solution)/shard_map/mlp/pallas_call | solution.py:264
  495.9 3.5 collective-permute-start.18
  499.4 67.6 %mlp.10 = (bf16[2,160,2304]{2,1,0:T(8,128)(2,1)}, bf16[2,160,2304]{2,1,0:T(8,128)(2,1)}) custom-call(s32[2,2176]{1,0:T(2,128)} %collective-permute-done.5.meta_ref.pos_ref.one_meta_ref, s32[2,2176]{1,0:T(2,128)} %collective-permute-done.6.meta_ref.pos_ref.two_meta_ref, bf16[2,768,2304]{2,1,0:T(8,128)(2,1)} %pack.6.one_ref, ...), custom_call_target="tpu_custom_call" | custom-call | flops 50960793600 | bytes 159252480 | tf_op jit(solution)/shard_map/mlp/pallas_call | solution.py:264
  567.0 67.6 %mlp.9 = (bf16[2,160,2304]{2,1,0:T(8,128)(2,1)}, bf16[2,160,2304]{2,1,0:T(8,128)(2,1)}) custom-call(s32[2,2176]{1,0:T(2,128)} %collective-permute-done.5.meta_ref.pos_ref.one_meta_ref, s32[2,2176]{1,0:T(2,128)} %collective-permute-done.6.meta_ref.pos_ref.two_meta_ref, bf16[2,768,2304]{2,1,0:T(8,128)(2,1)} %pack.6.one_ref, ...), custom_call_target="tpu_custom_call" | custom-call | flops 50960793600 | bytes 159252480 | tf_op jit(solution)/shard_map/mlp/pallas_call | solution.py:264
  634.6 67.6 %mlp.8 = (bf16[2,160,2304]{2,1,0:T(8,128)(2,1)}, bf16[2,160,2304]{2,1,0:T(8,128)(2,1)}) custom-call(s32[2,2176]{1,0:T(2,128)} %collective-permute-done.5.meta_ref.pos_ref.one_meta_ref, s32[2,2176]{1,0:T(2,128)} %collective-permute-done.6.meta_ref.pos_ref.two_meta_ref, bf16[2,768,2304]{2,1,0:T(8,128)(2,1)} %pack.6.one_ref, ...), custom_call_target="tpu_custom_call" | custom-call | flops 50960793600 | bytes 159252480 | tf_op jit(solution)/shard_map/mlp/pallas_call | solution.py:264
  709.5 3.9 gate.3
  713.4 3.9 gate.2
  719.3 23.5 %mix.2.base_ref = f32[2048,2304]{1,0:T(8,128)} custom-call(s32[8,128]{1,0:T(8,128)} %slice.6.start_ref, bf16[2048,2304]{1,0:T(8,128)(2,1)} %base_ref.1, s32[2048,8]{1,0:T(8,128)} %bitcast.7, f32[2048,8]{1,0:T(8,128)} %bitcast.9, bf16[2,480,2304]{2,1,0:T(8,128)(2,1)} %get-tuple-element.27.rest_0_, bf16[2,160,2304]{2,1,0:T(8,128)(2,1)} %get-tuple-element.28.rest_1_, ...), custom_call_target="tpu_custom_call" | custom-call | flops 9663676416 | bytes 47185920 | tf_op jit(solution)/shard_map/mix/pallas_call | solution.py:330
  742.8 25.6 %collective-permute-done.13.rest_2_ = bf16[2,160,2304]{2,1,0:T(8,128)(2,1)} collective-permute-done((bf16[2,160,2304]{2,1,0:T(8,128)(2,1)}, bf16[2,160,2304]{2,1,0:T(8,128)(2,1)}, u32[]{:S(2)}, u32[]{:S(2)}) %collective-permute-start.13) | collective-permute-done | bytes 1474592 | tf_op jit(solution)/shard_map/ppermute | solution.py:352
  768.4 31.9 %collective-permute-done.14.rest_3_ = bf16[2,160,2304]{2,1,0:T(8,128)(2,1)} collective-permute-done((bf16[2,160,2304]{2,1,0:T(8,128)(2,1)}, bf16[2,160,2304]{2,1,0:T(8,128)(2,1)}, u32[]{:S(2)}, u32[]{:S(2)}) %collective-permute-start.14) | collective-permute-done | bytes 1474592 | tf_op jit(solution)/shard_map/ppermute | solution.py:352
  800.3 31.3 %collective-permute-done.11.rest_0_ = bf16[2,160,2304]{2,1,0:T(8,128)(2,1)} collective-permute-done((bf16[2,160,2304]{2,1,0:T(8,128)(2,1)}, bf16[2,160,2304]{2,1,0:T(8,128)(2,1)}, u32[]{:S(2)}, u32[]{:S(2)}) %collective-permute-start.11) | collective-permute-done | bytes 1474592 | tf_op jit(solution)/shard_map/ppermute | solution.py:352
  831.6 31.6 %collective-permute-done.12.rest_1_ = bf16[2,160,2304]{2,1,0:T(8,128)(2,1)} collective-permute-done((bf16[2,160,2304]{2,1,0:T(8,128)(2,1)}, bf16[2,160,2304]{2,1,0:T(8,128)(2,1)}, u32[]{:S(2)}, u32[]{:S(2)}) %collective-permute-start.12) | collective-permute-done | bytes 1474592 | tf_op jit(solution)/shard_map/ppermute | solution.py:352
  863.2 23.1 %mix.3 = bf16[2048,2304]{1,0:T(8,128)(2,1)} custom-call(s32[8,128]{1,0:T(8,128)} %slice.6.start_ref, f32[2048,2304]{1,0:T(8,128)} %mix.2.base_ref, s32[2048,8]{1,0:T(8,128)} %bitcast.8, f32[2048,8]{1,0:T(8,128)} %bitcast.10, bf16[2,160,2304]{2,1,0:T(8,128)(2,1)} %collective-permute-done.11.rest_0_, bf16[2,160,2304]{2,1,0:T(8,128)(2,1)} %collective-permute-done.12.rest_1_, ...), custom_call_target="tpu_custom_call" | custom-call | flops 9663676416 | bytes 47185920 | tf_op jit(solution)/shard_map/mix/pallas_call | solution.py:330
  (36 shorter events, 17.8 us)
Async XLA Ops:
  7.9 26.0 %collective-permute-start.1 = (bf16[1024,2304]{1,0:T(8,128)(2,1)}, bf16[1024,2304]{1,0:T(8,128)(2,1)}, u32[]{:S(2)}, u32[]{:S(2)}) collective-permute-start(bf16[1024,2304]{1,0:T(8,128)(2,1)} %norm.2.u_ref.low_ref), channel_id=1, source_target_pairs={{0,1},{1,0},{2,3},{3,2},{4,5},{5,4},{6,7},{7,6},{8,9},{9,8},{10,11... | collective-permute-start | bytes 14155784 | tf_op jit(solution)/shard_map/ppermute | solution.py:352
  16.4 18.4 %collective-permute-start.2 = (bf16[1024,2304]{1,0:T(8,128)(2,1)}, bf16[1024,2304]{1,0:T(8,128)(2,1)}, u32[]{:S(2)}, u32[]{:S(2)}) collective-permute-start(bf16[1024,2304]{1,0:T(8,128)(2,1)} %norm.3.u_ref.high_ref), channel_id=1, source_target_pairs={{0,1},{1,0},{2,3},{3,2},{4,5},{5,4},{6,7},{7,6},{8,9},{9,8},{10,11... | collective-permute-start | bytes 14155784 | tf_op jit(solution)/shard_map/ppermute | solution.py:352
  16.4 103.2 %collective-permute-start.7 = (bf16[1024,2304]{1,0:T(8,128)(2,1)}, bf16[1024,2304]{1,0:T(8,128)(2,1)}, u32[]{:S(2)}, u32[]{:S(2)}) collective-permute-start(bf16[1024,2304]{1,0:T(8,128)(2,1)} %norm.2.u_ref.low_ref), channel_id=1, source_target_pairs={{0,2},{1,3},{2,0},{3,1},{4,6},{5,7},{6,4},{7,5},{8,10},{9,11},{10,... | collective-permute-start | bytes 14155784 | tf_op jit(solution)/shard_map/ppermute | solution.py:352
  17.6 203.1 %collective-permute-start.8 = (bf16[1024,2304]{1,0:T(8,128)(2,1)}, bf16[1024,2304]{1,0:T(8,128)(2,1)}, u32[]{:S(2)}, u32[]{:S(2)}) collective-permute-start(bf16[1024,2304]{1,0:T(8,128)(2,1)} %norm.3.u_ref.high_ref), channel_id=1, source_target_pairs={{0,2},{1,3},{2,0},{3,1},{4,6},{5,7},{6,4},{7,5},{8,10},{9,11},{10,... | collective-permute-start | bytes 14155784 | tf_op jit(solution)/shard_map/ppermute | solution.py:352
  19.5 13.6 %collective-permute-start = (s32[2,2176]{1,0:T(2,128)}, s32[2,2176]{1,0:T(2,128)}, u32[]{:S(2)}, u32[]{:S(2)}) collective-permute-start(s32[2,2176]{1,0:T(2,128)} %get-tuple-element.26), channel_id=1, source_target_pairs={{0,1},{1,0},{2,3},{3,2},{4,5},{5,4},{6,7},{7,6},{8,9},{9,8},{10,11... | collective-permute-start | bytes 52232 | tf_op jit(solution)/shard_map/ppermute | solution.py:352
  33.1 370.4 %collective-permute-start.5 = (s32[2,2176]{1,0:T(2,128)}, s32[2,2176]{1,0:T(2,128)}, u32[]{:S(2)}, u32[]{:S(2)}) collective-permute-start(s32[2,2176]{1,0:T(2,128)} %get-tuple-element.31), channel_id=1, source_target_pairs={{0,2},{1,3},{2,0},{3,1},{4,6},{5,7},{6,4},{7,5},{8,10},{9,11},{10,... | collective-permute-start | bytes 52232 | tf_op jit(solution)/shard_map/ppermute | solution.py:352
  33.8 382.2 %collective-permute-start.6 = (s32[2,2176]{1,0:T(2,128)}, s32[2,2176]{1,0:T(2,128)}, u32[]{:S(2)}, u32[]{:S(2)}) collective-permute-start(s32[2,2176]{1,0:T(2,128)} %get-tuple-element.32), channel_id=1, source_target_pairs={{0,3},{1,2},{2,1},{3,0},{4,7},{5,6},{6,5},{7,4},{8,11},{9,10},{10,... | collective-permute-start | bytes 52232 | tf_op jit(solution)/shard_map/ppermute | solution.py:352
  85.8 616.4 %collective-permute-start.4 = (bf16[2,160,2304]{2,1,0:T(8,128)(2,1)}, bf16[2,160,2304]{2,1,0:T(8,128)(2,1)}, u32[]{:S(2)}, u32[]{:S(2)}) collective-permute-start(bf16[2,160,2304]{2,1,0:T(8,128)(2,1)} %get-tuple-element.30), channel_id=1, source_target_pairs={{0,1},{1,0},{2,3},{3,2},{4,5},{5,4},{6,7},{7,6},{8,9},{9,8},{10,11... | collective-permute-start | bytes 4423688 | tf_op jit(solution)/shard_map/ppermute | solution.py:352
  119.6 296.4 %collective-permute-start.9 = (bf16[1024,2304]{1,0:T(8,128)(2,1)}, bf16[1024,2304]{1,0:T(8,128)(2,1)}, u32[]{:S(2)}, u32[]{:S(2)}) collective-permute-start(bf16[1024,2304]{1,0:T(8,128)(2,1)} %collective-permute-done.7.low_ref), channel_id=1, source_target_pairs={{0,1},{1,0},{2,3},{3,2},{4,5},{5,4},{6,7},{7,6},{8,9},{9,8},{10,11... | collective-permute-start | bytes 14155784 | tf_op jit(solution)/shard_map/ppermute | solution.py:352
  220.7 195.3 %collective-permute-start.10 = (bf16[1024,2304]{1,0:T(8,128)(2,1)}, bf16[1024,2304]{1,0:T(8,128)(2,1)}, u32[]{:S(2)}, u32[]{:S(2)}) collective-permute-start(bf16[1024,2304]{1,0:T(8,128)(2,1)} %collective-permute-done.8.high_ref), channel_id=1, source_target_pairs={{0,1},{1,0},{2,3},{3,2},{4,5},{5,4},{6,7},{7,6},{8,9},{9,8},{10,11... | collective-permute-start | bytes 14155784 | tf_op jit(solution)/shard_map/ppermute | solution.py:352
  403.4 298.8 %collective-permute-start.3 = (bf16[2,480,2304]{2,1,0:T(8,128)(2,1)}, bf16[2,480,2304]{2,1,0:T(8,128)(2,1)}, u32[]{:S(2)}, u32[]{:S(2)}) collective-permute-start(bf16[2,480,2304]{2,1,0:T(8,128)(2,1)} %get-tuple-element.29), channel_id=1, source_target_pairs={{0,1},{1,0},{2,3},{3,2},{4,5},{5,4},{6,7},{7,6},{8,9},{9,8},{10,11... | collective-permute-start | bytes 13271048 | tf_op jit(solution)/shard_map/ppermute | solution.py:352
  495.9 208.1 %collective-permute-start.17 = (bf16[2,160,2304]{2,1,0:T(8,128)(2,1)}, bf16[2,160,2304]{2,1,0:T(8,128)(2,1)}, u32[]{:S(2)}, u32[]{:S(2)}) collective-permute-start(bf16[2,160,2304]{2,1,0:T(8,128)(2,1)} %get-tuple-element.39), channel_id=1, source_target_pairs={{0,2},{1,3},{2,0},{3,1},{4,6},{5,7},{6,4},{7,5},{8,10},{9,11},{10,... | collective-permute-start | bytes 4423688 | tf_op jit(solution)/shard_map/ppermute | solution.py:352
  495.9 209.9 %collective-permute-start.18 = (bf16[2,160,2304]{2,1,0:T(8,128)(2,1)}, bf16[2,160,2304]{2,1,0:T(8,128)(2,1)}, u32[]{:S(2)}, u32[]{:S(2)}) collective-permute-start(bf16[2,160,2304]{2,1,0:T(8,128)(2,1)} %get-tuple-element.40), channel_id=1, source_target_pairs={{0,3},{1,2},{2,1},{3,0},{4,7},{5,6},{6,5},{7,4},{8,11},{9,10},{10,... | collective-permute-start | bytes 4423688 | tf_op jit(solution)/shard_map/ppermute | solution.py:352
  567.0 138.8 %collective-permute-start.15 = (bf16[2,160,2304]{2,1,0:T(8,128)(2,1)}, bf16[2,160,2304]{2,1,0:T(8,128)(2,1)}, u32[]{:S(2)}, u32[]{:S(2)}) collective-permute-start(bf16[2,160,2304]{2,1,0:T(8,128)(2,1)} %get-tuple-element.37), channel_id=1, source_target_pairs={{0,2},{1,3},{2,0},{3,1},{4,6},{5,7},{6,4},{7,5},{8,10},{9,11},{10,... | collective-permute-start | bytes 4423688 | tf_op jit(solution)/shard_map/ppermute | solution.py:352
  702.2 40.6 %collective-permute-start.16 = (bf16[2,160,2304]{2,1,0:T(8,128)(2,1)}, bf16[2,160,2304]{2,1,0:T(8,128)(2,1)}, u32[]{:S(2)}, u32[]{:S(2)}) collective-permute-start(bf16[2,160,2304]{2,1,0:T(8,128)(2,1)} %get-tuple-element.38), channel_id=1, source_target_pairs={{0,3},{1,2},{2,1},{3,0},{4,7},{5,6},{6,5},{7,4},{8,11},{9,10},{10,... | collective-permute-start | bytes 4423688 | tf_op jit(solution)/shard_map/ppermute | solution.py:352
  702.2 66.2 %collective-permute-start.13 = (bf16[2,160,2304]{2,1,0:T(8,128)(2,1)}, bf16[2,160,2304]{2,1,0:T(8,128)(2,1)}, u32[]{:S(2)}, u32[]{:S(2)}) collective-permute-start(bf16[2,160,2304]{2,1,0:T(8,128)(2,1)} %get-tuple-element.35), channel_id=1, source_target_pairs={{0,2},{1,3},{2,0},{3,1},{4,6},{5,7},{6,4},{7,5},{8,10},{9,11},{10,... | collective-permute-start | bytes 4423688 | tf_op jit(solution)/shard_map/ppermute | solution.py:352
  704.0 96.4 %collective-permute-start.14 = (bf16[2,160,2304]{2,1,0:T(8,128)(2,1)}, bf16[2,160,2304]{2,1,0:T(8,128)(2,1)}, u32[]{:S(2)}, u32[]{:S(2)}) collective-permute-start(bf16[2,160,2304]{2,1,0:T(8,128)(2,1)} %get-tuple-element.36), channel_id=1, source_target_pairs={{0,3},{1,2},{2,1},{3,0},{4,7},{5,6},{6,5},{7,4},{8,11},{9,10},{10,... | collective-permute-start | bytes 4423688 | tf_op jit(solution)/shard_map/ppermute | solution.py:352
  705.7 125.9 %collective-permute-start.11 = (bf16[2,160,2304]{2,1,0:T(8,128)(2,1)}, bf16[2,160,2304]{2,1,0:T(8,128)(2,1)}, u32[]{:S(2)}, u32[]{:S(2)}) collective-permute-start(bf16[2,160,2304]{2,1,0:T(8,128)(2,1)} %get-tuple-element.33), channel_id=1, source_target_pairs={{0,2},{1,3},{2,0},{3,1},{4,6},{5,7},{6,4},{7,5},{8,10},{9,11},{10,... | collective-permute-start | bytes 4423688 | tf_op jit(solution)/shard_map/ppermute | solution.py:352
  705.7 157.5 %collective-permute-start.12 = (bf16[2,160,2304]{2,1,0:T(8,128)(2,1)}, bf16[2,160,2304]{2,1,0:T(8,128)(2,1)}, u32[]{:S(2)}, u32[]{:S(2)}) collective-permute-start(bf16[2,160,2304]{2,1,0:T(8,128)(2,1)} %get-tuple-element.34), channel_id=1, source_target_pairs={{0,3},{1,2},{2,1},{3,0},{4,7},{5,6},{6,5},{7,4},{8,11},{9,10},{10,... | collective-permute-start | bytes 4423688 | tf_op jit(solution)/shard_map/ppermute | solution.py:352

commit v4 on v3

--- a/solution.py
+++ b/solution.py
@@ -12,16 +12,17 @@
 F32, BF16, I32 = jnp.float32, jnp.bfloat16, jnp.int32
 VMEM_LIMIT = 67043328
 NORM_ROWS = 256
-NORM_GROUP = 16
 GATE_ROWS = 512
 PACK_ROWS = 512
 PACK_WIN = 128
-TILE = 160
+FAR_TILE = 160
+NEAR_TILE = 240
+LATE_TILE = 80
 FF_BLOCK = 1280
 FF_SPLIT = 768
-MIX_ROWS = 256
+MIX_ROWS = 512
 MIX_WIN = 256
-WIDE_WIN = 272
+WIDE_WIN = 528
 LANES = 128
 MIX_COLS = 256
 
@@ -70,18 +71,11 @@
 
 
 def norm_kernel(x_ref, gamma_ref, beta_ref, u_ref):
-    gamma = gamma_ref[...][None, :]
-    beta = beta_ref[...][None, :]
-
-    def group(n, carry):
-        rows = pl.ds(pl.multiple_of(n * NORM_GROUP, NORM_GROUP), NORM_GROUP)
-        values = x_ref[rows, :].astype(F32)
-        centred = values - jnp.mean(values, axis=-1, keepdims=True)
-        variance = jnp.mean(centred * centred, axis=-1, keepdims=True)
-        u_ref[rows, :] = (centred * lax.rsqrt(variance + LN_EPS) * gamma + beta).astype(BF16)
-        return carry
-
-    lax.fori_loop(0, x_ref.shape[0] // NORM_GROUP, group, 0, unroll=4)
+    values = x_ref[...].astype(F32)
+    centred = values - jnp.mean(values, axis=-1, keepdims=True)
+    variance = jnp.mean(centred * centred, axis=-1, keepdims=True)
+    normed = centred * lax.rsqrt(variance + LN_EPS) * gamma_ref[...][None, :] + beta_ref[...][None, :]
+    u_ref[...] = normed.astype(BF16)
 
 
 def norm_call(part, parts, hidden, gamma, beta):
@@ -158,8 +152,9 @@
                 at = pl.multiple_of(base + w * PACK_WIN, 16)
                 onehot = (slots - at == sublane).astype(F32).astype(BF16)
                 picked = jnp.dot(onehot, block_ref[...], preferred_element_type=F32)
-                held = rows_ref[e, pl.ds(at, PACK_WIN), :]
-                rows_ref[e, pl.ds(at, PACK_WIN), :] = (held.astype(F32) + picked).astype(BF16)
+                held = rows_ref[e, pl.ds(at, 16), :]
+                rows_ref[e, pl.ds(at, 16), :] = (held.astype(F32) + picked[:16]).astype(BF16)
+                rows_ref[e, pl.ds(pl.multiple_of(at + 16, 16), PACK_WIN - 16), :] = picked[16:].astype(BF16)
                 return carry
 
             lax.fori_loop(0, windows, window, 0)
@@ -191,27 +186,31 @@
     )(meta, meta, low, high)
 
 
-def row_tiles(begin, rows, tokens, expert, one_meta_ref, two_meta_ref):
+def row_tiles(begin, rows, tile, tokens, expert, meta_refs):
     last = mark(tokens, tokens, 1)
-    most = jnp.maximum(one_meta_ref[expert, last], two_meta_ref[expert, last])
-    return jnp.clip((most - begin + TILE - 1) // TILE, 0, rows // TILE)
-
-
-def tail_step(expert, step, steps):
-    return step == jnp.where(expert % 2 == 0, 0, steps - 1)
-
-
-def mlp_kernel(begin, tokens, splits, tail_splits, one_meta_ref, two_meta_ref, one_ref, two_ref, gate_ref, up_ref, down_ref, out_one_ref, out_two_ref, acc_ref):
-    expert, step, steps = pl.program_id(0), pl.program_id(1), pl.num_programs(1)
-    rows = out_one_ref.shape[1]
-    tiles = row_tiles(begin, rows, tokens, expert, one_meta_ref, two_meta_ref)
-    is_tail = tail_step(expert, step, steps)
+    most = functools.reduce(jnp.maximum, [ref[expert, last] for ref in meta_refs])
+    return jnp.clip((most - begin + tile - 1) // tile, 0, rows // tile)
+
+
+def tail_step(turn, step, steps):
+    return step == jnp.where(turn % 2 == 0, 0, steps - 1)
+
+
+def mlp_kernel(begin, tile_rows, tokens, first_expert, splits, tail_splits, sources, *refs):
+    meta_refs, row_refs = refs[:sources], refs[sources:2 * sources]
+    gate_ref, up_ref, down_ref = refs[2 * sources:2 * sources + 3]
+    out_refs, acc_ref = refs[2 * sources + 3:-1], refs[-1]
+    turn, step, steps = pl.program_id(0), pl.program_id(1), pl.num_programs(1)
+    rows = out_refs[0].shape[1]
+    height = sources * tile_rows
+    tiles = row_tiles(begin, rows, tile_rows, tokens, first_expert + turn, meta_refs)
+    is_tail = tail_step(turn, step, steps)
 
     def accumulate(parts):
         def tile(i, carry):
-            at = pl.multiple_of(i * TILE, TILE)
-            both = pl.ds(pl.multiple_of(i * 2 * TILE, 2 * TILE), 2 * TILE)
-            taken = jnp.concatenate([one_ref[0, pl.ds(at, TILE), :], two_ref[0, pl.ds(at, TILE), :]], axis=0)
+            at = pl.multiple_of(i * tile_rows, tile_rows)
+            held_rows = pl.ds(pl.multiple_of(i * height, height), height)
+            taken = jnp.concatenate([ref[0, pl.ds(at, tile_rows), :] for ref in row_refs], axis=0)
             projs = []
             for lo, hi in parts:
                 joined = jnp.concatenate([gate_ref[0, :, lo:hi], up_ref[0, :, lo:hi]], axis=1)
@@ -219,10 +218,10 @@
             for n, (lo, hi) in enumerate(parts):
                 inner = (jax.nn.silu(projs[n][:, :hi - lo]) * projs[n][:, hi - lo:]).astype(BF16)
                 down = jnp.dot(inner, down_ref[0, lo:hi, :], preferred_element_type=F32)
-                held = acc_ref[both, :]
+                held = acc_ref[held_rows, :]
                 if n == 0:
                     held = jnp.where(step == 0, 0.0, held)
-                acc_ref[both, :] = held + down
+                acc_ref[held_rows, :] = held + down
             return carry
 
         lax.fori_loop(0, tiles, tile, 0)
@@ -232,51 +231,51 @@
 
     @pl.when(step == steps - 1)
     def _():
-        for i in range(rows // TILE):
-            outs = [(ref, (2 * i + n) * TILE) for n, ref in enumerate((out_one_ref, out_two_ref))]
-
+        for i in range(rows // tile_rows):
             @pl.when(i < tiles)
             def _():
-                for ref, at in outs:
-                    ref[0, i * TILE:(i + 1) * TILE, :] = acc_ref[at:at + TILE, :].astype(BF16)
+                for n, ref in enumerate(out_refs):
+                    at = (sources * i + n) * tile_rows
+                    ref[0, i * tile_rows:(i + 1) * tile_rows, :] = acc_ref[at:at + tile_rows, :].astype(BF16)
 
             @pl.when(i >= tiles)
             def _():
-                for ref, _at in outs:
-                    ref[0, i * TILE:(i + 1) * TILE, :] = jnp.zeros((TILE, ref.shape[2]), BF16)
-
-
-def mlp_call(tokens, begin, rows, meta_one, meta_two, packed_one, packed_two, w_gate, w_up, w_down):
-    experts, width, ff = w_gate.shape
+                for ref in out_refs:
+                    ref[0, i * tile_rows:(i + 1) * tile_rows, :] = jnp.zeros((tile_rows, ref.shape[2]), BF16)
+
+
+def mlp_call(tokens, begin, rows, tile_rows, first_expert, experts, metas, packed, w_gate, w_up, w_down):
+    width, ff = w_gate.shape[1:]
+    sources = len(metas)
     full_steps, tail = divmod(ff, FF_BLOCK)
     splits = ((0, FF_SPLIT), (FF_SPLIT, FF_BLOCK))
     tail_splits = ((0, tail),)
     once = pl.Buffered(1)
 
-    def block(e, f, one, two):
-        idle = row_tiles(begin, rows, tokens, e, one, two) == 0
+    def block(e, f, refs):
+        idle = row_tiles(begin, rows, tile_rows, tokens, first_expert + e, refs) == 0
         return jnp.where(tail_step(e, f, full_steps + 1) | idle, full_steps, jnp.where(e % 2 == 0, f - 1, f))
 
-    packed_spec = pl.BlockSpec((1, rows, width), lambda e, f, one, two: (e, begin // rows, 0), pipeline_mode=once)
-    out_spec = pl.BlockSpec((1, rows, width), lambda e, f, one, two: (e, 0, 0), pipeline_mode=once)
-    in_spec = pl.BlockSpec((1, width, FF_BLOCK), lambda e, f, one, two: (e, 0, block(e, f, one, two)))
+    packed_spec = pl.BlockSpec((1, rows, width), lambda e, f, *m: (first_expert + e, begin // rows, 0), pipeline_mode=once)
+    out_spec = pl.BlockSpec((1, rows, width), lambda e, f, *m: (e, 0, 0), pipeline_mode=once)
+    in_spec = pl.BlockSpec((1, width, FF_BLOCK), lambda e, f, *m: (first_expert + e, 0, block(e, f, m)))
+    down_spec = pl.BlockSpec((1, FF_BLOCK, width), lambda e, f, *m: (first_expert + e, block(e, f, m), 0))
     out = jax.ShapeDtypeStruct((experts, rows, width), BF16)
     return pl.pallas_call(
-        functools.partial(mlp_kernel, begin, tokens, splits, tail_splits),
+        functools.partial(mlp_kernel, begin, tile_rows, tokens, first_expert, splits, tail_splits, sources),
         grid_spec=pltpu.PrefetchScalarGridSpec(
-            num_scalar_prefetch=2,
+            num_scalar_prefetch=sources,
             grid=(experts, full_steps + 1),
-            in_specs=[packed_spec, packed_spec, in_spec, in_spec,
-                      pl.BlockSpec((1, FF_BLOCK, width), lambda e, f, one, two: (e, block(e, f, one, two), 0))],
-            out_specs=[out_spec, out_spec],
-            scratch_shapes=[pltpu.VMEM((2 * rows, width), F32)],
+            in_specs=[packed_spec] * sources + [in_spec, in_spec, down_spec],
+            out_specs=[out_spec] * sources,
+            scratch_shapes=[pltpu.VMEM((sources * rows, width), F32)],
         ),
-        out_shape=[out, out],
+        out_shape=[out] * sources,
         compiler_params=pltpu.CompilerParams(vmem_limit_bytes=VMEM_LIMIT),
-        cost_estimate=pl.CostEstimate(flops=6 * 2 * experts * rows * width * ff, bytes_accessed=6 * experts * width * ff,
-                                      transcendentals=0),
+        cost_estimate=pl.CostEstimate(flops=6 * sources * experts * rows * width * ff,
+                                      bytes_accessed=6 * experts * width * ff, transcendentals=0),
         name="mlp",
-    )(meta_one, meta_two, packed_one, packed_two, w_gate, w_up, w_down)
+    )(*metas, *packed, w_gate, w_up, w_down)
 
 
 def mix_kernel(columns, starts_at, capacity, start_ref, base_ref, pos_ref, gate_ref, *rest):
@@ -323,7 +322,8 @@
     pl.when(jnp.logical_not(fits))(lambda: mix(WIDE_WIN))
 
 
-def mix_call(columns, starts_at, capacity, starts, base, pos, gates, pieces, out_dtype):
+def mix_call(columns, capacity, starts, base, pos, gates, placed, out_dtype):
+    starts_at, pieces = zip(*placed)
     tokens, width = base.shape
     block = pl.BlockSpec((MIX_ROWS, width), lambda i, s: (i, 0))
     small = pl.BlockSpec((MIX_ROWS, pos.shape[1]), lambda i, s: (i, 0))
@@ -373,33 +373,40 @@
         def pack(m):
             return pack_call(metas[m], *sources[m], capacity)
 
-        def run(m_one, m_two, begin, rows, packed):
-            return mlp_call(tokens, begin, rows, metas[m_one], metas[m_two], *packed, w_gate, w_up, w_down)
-
-        early = capacity - TILE
-        near = [pack(0), pack(1)]
-        near_early = run(0, 1, 0, early, near)
-        home_early = swap(near_early[1], 1)
-
-        far = [pack(2), pack(3)]
+        packed = {}
+
+        def run(places, begin, rows, tile_rows, first_expert=0, count=local):
+            return mlp_call(tokens, begin, rows, tile_rows, first_expert, count, [metas[m] for m in places],
+                            [packed[m] for m in places], w_gate, w_up, w_down)
+
+        late = capacity - FAR_TILE
+        packed[0], packed[1] = pack(0), pack(1)
+        near_early = run((0, 1), 0, late, NEAR_TILE)
+        near_rows = [((0, 0), near_early[0]), ((local, 0), swap(near_early[1], 1))]
+
+        packed[2], packed[3] = pack(2), pack(3)
         far_rows = []
-        for c in range(capacity // TILE):
-            one, two = run(2, 3, c * TILE, TILE, far)
-            far_rows.append((swap(one, 2), swap(two, 3)))
-
-        near_late = run(0, 1, early, TILE, near)
-        home_late = swap(near_late[1], 1)
+
+        def send_far(expert, at, two, three):
+            far_rows.append(((expert, at), swap(two, 2)))
+            far_rows.append(((local + expert, at), swap(three, 3)))
+
+        for c in range(late // FAR_TILE - 1):
+            send_far(0, c * FAR_TILE, *run((2, 3), c * FAR_TILE, FAR_TILE, FAR_TILE))
+        zero, one, two, three = run((0, 1, 2, 3), late, FAR_TILE, LATE_TILE)
+        send_far(0, late, two, three)
+        near_rows += [((0, late), zero), ((local, late), swap(one, 1))]
+        final = late - FAR_TILE
+        for e in range(local):
+            send_far(e, final, *run((2, 3), final, FAR_TILE, FAR_TILE, e, 1))
 
         gates = [gate_call(part, u, w_router.T, choice_t, rel_t, mask_first.T, mask_second.T)
                  for part, u in enumerate(halves)]
         gates_t = jnp.concatenate(gates, axis=1).T
         pos_t = table[:, :tokens].T
         marks = table[:, tokens:]
-        total = mix_call(tuple(range(2 * local)), ((0, 0), (0, early), (local, 0), (local, early)), capacity, marks,
-                         hidden, pos_t, gates_t, (near_early[0], near_late[0], home_early, home_late), F32)
-        starts_at = tuple((local * n, c * TILE) for c in range(capacity // TILE) for n in range(2))
-        return mix_call(tuple(range(2 * local, experts)), starts_at, capacity, marks, total, pos_t, gates_t,
-                        tuple(piece for pair in far_rows for piece in pair), BF16)
+        total = mix_call(tuple(range(2 * local)), capacity, marks, hidden, pos_t, gates_t, near_rows, F32)
+        return mix_call(tuple(range(2 * local, experts)), capacity, marks, total, pos_t, gates_t, far_rows, BF16)
 
     return jax.shard_map(device_step, mesh=mesh,
                          in_specs=(rows_spec, P(), P(), P(), P("ep"), P("ep"), P("ep"), rows_spec, rows_spec, rows_spec),

time: 893 us -> 930 us (1.041)
  the two profiles are of different devices: /device:TPU:13 before, /device:TPU:15 now
where the time goes in v4:
time: 930 us; the launch traced here: 923 us
  Pallas kernels  545 us (59%)
  waiting for transfers between devices  301 us (32%)
  starting transfers between devices  71.4 us (8%)
    pallas_call x6, Pallas kernels, mlp_call(): pl.pallas_call(functools.partial(mlp_kernel, begin, tile_rows, tokens, fi...  429 us
    ppermute x21, waiting for transfers between devices, swap(): lax.ppermute(array, 'ep', [(i, i ^ distance) for i in range(group_size)])  301 us
    ppermute x21, starting transfers between devices, swap(): lax.ppermute(array, 'ep', [(i, i ^ distance) for i in range(group_size)])  71.4 us
    pallas_call x4, Pallas kernels, pack_call(): pl.pallas_call(functools.partial(pack_kernel, half_steps), grid_spec=pltp...  49.4 us
    pallas_call x2, Pallas kernels, mix_call(): pl.pallas_call(functools.partial(mix_kernel, columns, starts_at, capacity...  44.6 us
  transfers between devices with their start and end apart: 21, of which 6 were waited for; matrix products, arithmetic and copies ran while one was open for 1% of the time, Pallas kernels for 56%

profile of v4, /device:TPU:15, one launch (start us, length us, event | category | flops | bytes accessed | tf_op | source)
XLA Modules:
  0.0 923.4 jit_solution(14237656769307586976)
XLA Ops:
  0.0 6.7 norm.2.u_ref.low_ref
  7.6 6.8 norm.3.u_ref.high_ref
  17.8 12.1 %pack.4.refs_2_.refs_4_ = bf16[2,768,2304]{2,1,0:T(8,128)(2,1)} custom-call(s32[2,2176]{1,0:T(2,128)} %get-tuple-element.27.meta_ref.pos_ref.refs_0_, s32[2,2176]{1,0:T(2,128)} %get-tuple-element.27.meta_ref.pos_ref.refs_0_, bf16[1024,2304]{1,0:T(8,128)(2,1)} %norm.2.u_ref.low_ref, bf16[1024,2304]{1,0:T(8,128)(2,1)} %norm.3.u_ref.high_ref), custom_call_target="tpu_custom_call" | custom-call | flops 4831838208 | bytes 28311552 | tf_op jit(solution)/shard_map/pack/pallas_call | solution.py:171
  31.5 79.5 %collective-permute-done.6.low_ref = bf16[1024,2304]{1,0:T(8,128)(2,1)} collective-permute-done((bf16[1024,2304]{1,0:T(8,128)(2,1)}, bf16[1024,2304]{1,0:T(8,128)(2,1)}, u32[]{:S(2)}, u32[]{:S(2)}) %collective-permute-start.6) | collective-permute-done | bytes 4718624 | tf_op jit(solution)/shard_map/ppermute | solution.py:352
  112.4 99.8 %collective-permute-done.7.high_ref = bf16[1024,2304]{1,0:T(8,128)(2,1)} collective-permute-done((bf16[1024,2304]{1,0:T(8,128)(2,1)}, bf16[1024,2304]{1,0:T(8,128)(2,1)}, u32[]{:S(2)}, u32[]{:S(2)}) %collective-permute-start.7) | collective-permute-done | bytes 4718624 | tf_op jit(solution)/shard_map/ppermute | solution.py:352
  213.4 12.5 %pack.5.refs_3_.refs_5_ = bf16[2,768,2304]{2,1,0:T(8,128)(2,1)} custom-call(s32[2,2176]{1,0:T(2,128)} %collective-permute-done.meta_ref.pos_ref.refs_1_, s32[2,2176]{1,0:T(2,128)} %collective-permute-done.meta_ref.pos_ref.refs_1_, bf16[1024,2304]{1,0:T(8,128)(2,1)} %collective-permute-done.1.low_ref, bf16[1024,2304]{1,0:T(8,128)(2,1)} %collective-permute-done.2.high_ref), custom_call_target="tpu_custom_call" | custom-call | flops 4831838208 | bytes 28311552 | tf_op jit(solution)/shard_map/pack/pallas_call | solution.py:171
  225.9 179.8 %mlp.6 = (bf16[2,480,2304]{2,1,0:T(8,128)(2,1)}, bf16[2,480,2304]{2,1,0:T(8,128)(2,1)}) custom-call(s32[2,2176]{1,0:T(2,128)} %get-tuple-element.27.meta_ref.pos_ref.refs_0_, s32[2,2176]{1,0:T(2,128)} %collective-permute-done.meta_ref.pos_ref.refs_1_, bf16[2,768,2304]{2,1,0:T(8,128)(2,1)} %pack.4.refs_2_.refs_4_, bf16[2,768,2304]{2,1,0:T(8,128)(2,1)} %pack.5.refs_3_.refs_5_, ...), custom_call_target="tpu_custom_call" | custom-call | flops 152882380800 | bytes 159252480 | tf_op jit(solution)/shard_map/mlp/pallas_call | solution.py:264
  405.7 12.8 %pack.6.refs_6_.refs_2_ = bf16[2,768,2304]{2,1,0:T(8,128)(2,1)} custom-call(s32[2,2176]{1,0:T(2,128)} %collective-permute-done.4.meta_ref.pos_ref.refs_2_.refs_0_, s32[2,2176]{1,0:T(2,128)} %collective-permute-done.4.meta_ref.pos_ref.refs_2_.refs_0_, bf16[1024,2304]{1,0:T(8,128)(2,1)} %collective-permute-done.6.low_ref, ...), custom_call_target="tpu_custom_call" | custom-call | flops 4831838208 | bytes 28311552 | tf_op jit(solution)/shard_map/pack/pallas_call | solution.py:171
  418.5 12.0 %pack.7.refs_7_.refs_3_ = bf16[2,768,2304]{2,1,0:T(8,128)(2,1)} custom-call(s32[2,2176]{1,0:T(2,128)} %collective-permute-done.5.meta_ref.pos_ref.refs_3_.refs_1_, s32[2,2176]{1,0:T(2,128)} %collective-permute-done.5.meta_ref.pos_ref.refs_3_.refs_1_, bf16[1024,2304]{1,0:T(8,128)(2,1)} %collective-permute-done.8.low_ref, ...), custom_call_target="tpu_custom_call" | custom-call | flops 4831838208 | bytes 28311552 | tf_op jit(solution)/shard_map/pack/pallas_call | solution.py:171
  430.5 41.5 %mlp.7 = (bf16[2,160,2304]{2,1,0:T(8,128)(2,1)}, bf16[2,160,2304]{2,1,0:T(8,128)(2,1)}, bf16[2,160,2304]{2,1,0:T(8,128)(2,1)}, bf16[2,160,2304]{2,1,0:T(8,128)(2,1)}) custom-call(s32[2,2176]{1,0:T(2,128)} %get-tuple-element.27.meta_ref.pos_ref.refs_0_, s32[2,2176]{1,0:T(2,128)} %collective-permute-done.meta_ref.pos_ref.refs_1_, ...), custom_call_target="tpu_custom_call" | custom-call | flops 101921587200 | bytes 159252480 | tf_op jit(solution)/shard_map/mlp/pallas_call | solution.py:264
  472.1 67.7 %mlp.8 = (bf16[2,160,2304]{2,1,0:T(8,128)(2,1)}, bf16[2,160,2304]{2,1,0:T(8,128)(2,1)}) custom-call(s32[2,2176]{1,0:T(2,128)} %collective-permute-done.4.meta_ref.pos_ref.refs_2_.refs_0_, s32[2,2176]{1,0:T(2,128)} %collective-permute-done.5.meta_ref.pos_ref.refs_3_.refs_1_, bf16[2,768,2304]{2,1,0:T(8,128)(2,1)} %pack.6.refs_6_.refs_2_, ...), custom_call_target="tpu_custom_call" | custom-call | flops 50960793600 | bytes 159252480 | tf_op jit(solution)/shard_map/mlp/pallas_call | solution.py:264
  539.8 57.2 %collective-permute-start.11 = (bf16[2,160,2304]{2,1,0:T(8,128)(2,1)}, bf16[2,160,2304]{2,1,0:T(8,128)(2,1)}, u32[]{:S(2)}, u32[]{:S(2)}) collective-permute-start(bf16[2,160,2304]{2,1,0:T(8,128)(2,1)} %get-tuple-element.35), channel_id=1, source_target_pairs={{0,2},{1,3},{2,0},{3,1},{4,6},{5,7},{6,4},{7,5},{8,10},{9,11},{10,... | collective-permute-start | bytes 4423688 | tf_op jit(solution)/shard_map/ppermute | solution.py:352
  597.0 36.0 %mlp.10 = (bf16[1,160,2304]{2,1,0:T(8,128)(2,1)}, bf16[1,160,2304]{2,1,0:T(8,128)(2,1)}) custom-call(s32[2,2176]{1,0:T(2,128)} %collective-permute-done.4.meta_ref.pos_ref.refs_2_.refs_0_, s32[2,2176]{1,0:T(2,128)} %collective-permute-done.5.meta_ref.pos_ref.refs_3_.refs_1_, bf16[2,768,2304]{2,1,0:T(8,128)(2,1)} %pack.6.refs_6_.refs_2_, ...), custom_call_target="tpu_custom_call" | custom-call | flops 25480396800 | bytes 79626240 | tf_op jit(solution)/shard_map/mlp/pallas_call | solution.py:264
  633.0 1.9 collective-permute-start.18
  634.9 36.0 %mlp.11 = (bf16[1,160,2304]{2,1,0:T(8,128)(2,1)}, bf16[1,160,2304]{2,1,0:T(8,128)(2,1)}) custom-call(s32[2,2176]{1,0:T(2,128)} %collective-permute-done.4.meta_ref.pos_ref.refs_2_.refs_0_, s32[2,2176]{1,0:T(2,128)} %collective-permute-done.5.meta_ref.pos_ref.refs_3_.refs_1_, bf16[2,768,2304]{2,1,0:T(8,128)(2,1)} %pack.6.refs_6_.refs_2_, ...), custom_call_target="tpu_custom_call" | custom-call | flops 25480396800 | bytes 79626240 | tf_op jit(solution)/shard_map/mlp/pallas_call | solution.py:264
  672.5 67.6 %mlp.9 = (bf16[2,160,2304]{2,1,0:T(8,128)(2,1)}, bf16[2,160,2304]{2,1,0:T(8,128)(2,1)}) custom-call(s32[2,2176]{1,0:T(2,128)} %collective-permute-done.4.meta_ref.pos_ref.refs_2_.refs_0_, s32[2,2176]{1,0:T(2,128)} %collective-permute-done.5.meta_ref.pos_ref.refs_3_.refs_1_, bf16[2,768,2304]{2,1,0:T(8,128)(2,1)} %pack.6.refs_6_.refs_2_, ...), custom_call_target="tpu_custom_call" | custom-call | flops 50960793600 | bytes 159252480 | tf_op jit(solution)/shard_map/mlp/pallas_call | solution.py:264
  747.3 3.9 gate.3
  751.2 3.9 gate.2
  757.2 22.4 %mix.2.base_ref = f32[2048,2304]{1,0:T(8,128)} custom-call(s32[8,128]{1,0:T(8,128)} %slice.6.start_ref, bf16[2048,2304]{1,0:T(8,128)(2,1)} %base_ref.1, s32[2048,8]{1,0:T(8,128)} %bitcast.7, f32[2048,8]{1,0:T(8,128)} %bitcast.9, bf16[2,480,2304]{2,1,0:T(8,128)(2,1)} %get-tuple-element.29.rest_0_, bf16[2,480,2304]{2,1,0:T(8,128)(2,1)} %collective-permute-done.3.rest_1_, ...), custom_call_target="tpu_custom_call" | custom-call | flops 9663676416 | bytes 47185920 | tf_op jit(solution)/shard_map/mix/pallas_call | solution.py:330
  779.5 26.5 %collective-permute-done.13.rest_2_ = bf16[2,160,2304]{2,1,0:T(8,128)(2,1)} collective-permute-done((bf16[2,160,2304]{2,1,0:T(8,128)(2,1)}, bf16[2,160,2304]{2,1,0:T(8,128)(2,1)}, u32[]{:S(2)}, u32[]{:S(2)}) %collective-permute-start.13) | collective-permute-done | bytes 1474592 | tf_op jit(solution)/shard_map/ppermute | solution.py:352
  806.0 32.1 %collective-permute-done.14.rest_3_ = bf16[2,160,2304]{2,1,0:T(8,128)(2,1)} collective-permute-done((bf16[2,160,2304]{2,1,0:T(8,128)(2,1)}, bf16[2,160,2304]{2,1,0:T(8,128)(2,1)}, u32[]{:S(2)}, u32[]{:S(2)}) %collective-permute-start.14) | collective-permute-done | bytes 1474592 | tf_op jit(solution)/shard_map/ppermute | solution.py:352
  838.1 31.1 %collective-permute-done.15.rest_4_ = bf16[2,160,2304]{2,1,0:T(8,128)(2,1)} collective-permute-done((bf16[2,160,2304]{2,1,0:T(8,128)(2,1)}, bf16[2,160,2304]{2,1,0:T(8,128)(2,1)}, u32[]{:S(2)}, u32[]{:S(2)}) %collective-permute-start.15) | collective-permute-done | bytes 1474592 | tf_op jit(solution)/shard_map/ppermute | solution.py:352
  869.2 31.7 %collective-permute-done.16.rest_5_ = bf16[2,160,2304]{2,1,0:T(8,128)(2,1)} collective-permute-done((bf16[2,160,2304]{2,1,0:T(8,128)(2,1)}, bf16[2,160,2304]{2,1,0:T(8,128)(2,1)}, u32[]{:S(2)}, u32[]{:S(2)}) %collective-permute-start.16) | collective-permute-done | bytes 1474592 | tf_op jit(solution)/shard_map/ppermute | solution.py:352
  900.9 22.3 %mix.3 = bf16[2048,2304]{1,0:T(8,128)(2,1)} custom-call(s32[8,128]{1,0:T(8,128)} %slice.6.start_ref, f32[2048,2304]{1,0:T(8,128)} %mix.2.base_ref, s32[2048,8]{1,0:T(8,128)} %bitcast.8, f32[2048,8]{1,0:T(8,128)} %bitcast.10, bf16[2,160,2304]{2,1,0:T(8,128)(2,1)} %collective-permute-done.11.rest_0_, bf16[2,160,2304]{2,1,0:T(8,128)(2,1)} %collective-permute-done.12.rest_1_, ...), custom_call_target="tpu_custom_call" | custom-call | flops 9663676416 | bytes 47185920 | tf_op jit(solution)/shard_map/mix/pallas_call | solution.py:330
  (40 shorter events, 19.5 us)
Async XLA Ops:
  6.7 24.0 %collective-permute-start.1 = (bf16[1024,2304]{1,0:T(8,128)(2,1)}, bf16[1024,2304]{1,0:T(8,128)(2,1)}, u32[]{:S(2)}, u32[]{:S(2)}) collective-permute-start(bf16[1024,2304]{1,0:T(8,128)(2,1)} %norm.2.u_ref.low_ref), channel_id=1, source_target_pairs={{0,1},{1,0},{2,3},{3,2},{4,5},{5,4},{6,7},{7,6},{8,9},{9,8},{10,11... | collective-permute-start | bytes 14155784 | tf_op jit(solution)/shard_map/ppermute | solution.py:352
  7.4 103.7 %collective-permute-start.6 = (bf16[1024,2304]{1,0:T(8,128)(2,1)}, bf16[1024,2304]{1,0:T(8,128)(2,1)}, u32[]{:S(2)}, u32[]{:S(2)}) collective-permute-start(bf16[1024,2304]{1,0:T(8,128)(2,1)} %norm.2.u_ref.low_ref), channel_id=1, source_target_pairs={{0,2},{1,3},{2,0},{3,1},{4,6},{5,7},{6,4},{7,5},{8,10},{9,11},{10,... | collective-permute-start | bytes 14155784 | tf_op jit(solution)/shard_map/ppermute | solution.py:352
  14.4 197.8 %collective-permute-start.7 = (bf16[1024,2304]{1,0:T(8,128)(2,1)}, bf16[1024,2304]{1,0:T(8,128)(2,1)}, u32[]{:S(2)}, u32[]{:S(2)}) collective-permute-start(bf16[1024,2304]{1,0:T(8,128)(2,1)} %norm.3.u_ref.high_ref), channel_id=1, source_target_pairs={{0,2},{1,3},{2,0},{3,1},{4,6},{5,7},{6,4},{7,5},{8,10},{9,11},{10,... | collective-permute-start | bytes 14155784 | tf_op jit(solution)/shard_map/ppermute | solution.py:352
  15.6 197.8 %collective-permute-start.2 = (bf16[1024,2304]{1,0:T(8,128)(2,1)}, bf16[1024,2304]{1,0:T(8,128)(2,1)}, u32[]{:S(2)}, u32[]{:S(2)}) collective-permute-start(bf16[1024,2304]{1,0:T(8,128)(2,1)} %norm.3.u_ref.high_ref), channel_id=1, source_target_pairs={{0,1},{1,0},{2,3},{3,2},{4,5},{5,4},{6,7},{7,6},{8,9},{9,8},{10,11... | collective-permute-start | bytes 14155784 | tf_op jit(solution)/shard_map/ppermute | solution.py:352
  17.8 12.1 %collective-permute-start = (s32[2,2176]{1,0:T(2,128)}, s32[2,2176]{1,0:T(2,128)}, u32[]{:S(2)}, u32[]{:S(2)}) collective-permute-start(s32[2,2176]{1,0:T(2,128)} %get-tuple-element.28), channel_id=1, source_target_pairs={{0,1},{1,0},{2,3},{3,2},{4,5},{5,4},{6,7},{7,6},{8,9},{9,8},{10,11... | collective-permute-start | bytes 52232 | tf_op jit(solution)/shard_map/ppermute | solution.py:352
  29.9 375.8 %collective-permute-start.4 = (s32[2,2176]{1,0:T(2,128)}, s32[2,2176]{1,0:T(2,128)}, u32[]{:S(2)}, u32[]{:S(2)}) collective-permute-start(s32[2,2176]{1,0:T(2,128)} %get-tuple-element.31), channel_id=1, source_target_pairs={{0,2},{1,3},{2,0},{3,1},{4,6},{5,7},{6,4},{7,5},{8,10},{9,11},{10,... | collective-permute-start | bytes 52232 | tf_op jit(solution)/shard_map/ppermute | solution.py:352
  30.6 387.8 %collective-permute-start.5 = (s32[2,2176]{1,0:T(2,128)}, s32[2,2176]{1,0:T(2,128)}, u32[]{:S(2)}, u32[]{:S(2)}) collective-permute-start(s32[2,2176]{1,0:T(2,128)} %get-tuple-element.32), channel_id=1, source_target_pairs={{0,3},{1,2},{2,1},{3,0},{4,7},{5,6},{6,5},{7,4},{8,11},{9,10},{10,... | collective-permute-start | bytes 52232 | tf_op jit(solution)/shard_map/ppermute | solution.py:352
  111.0 307.4 %collective-permute-start.8 = (bf16[1024,2304]{1,0:T(8,128)(2,1)}, bf16[1024,2304]{1,0:T(8,128)(2,1)}, u32[]{:S(2)}, u32[]{:S(2)}) collective-permute-start(bf16[1024,2304]{1,0:T(8,128)(2,1)} %collective-permute-done.6.low_ref), channel_id=1, source_target_pairs={{0,1},{1,0},{2,3},{3,2},{4,5},{5,4},{6,7},{7,6},{8,9},{9,8},{10,11... | collective-permute-start | bytes 14155784 | tf_op jit(solution)/shard_map/ppermute | solution.py:352
  212.1 206.3 %collective-permute-start.9 = (bf16[1024,2304]{1,0:T(8,128)(2,1)}, bf16[1024,2304]{1,0:T(8,128)(2,1)}, u32[]{:S(2)}, u32[]{:S(2)}) collective-permute-start(bf16[1024,2304]{1,0:T(8,128)(2,1)} %collective-permute-done.7.high_ref), channel_id=1, source_target_pairs={{0,1},{1,0},{2,3},{3,2},{4,5},{5,4},{6,7},{7,6},{8,9},{9,8},{10,11... | collective-permute-start | bytes 14155784 | tf_op jit(solution)/shard_map/ppermute | solution.py:352
  405.7 265.2 %collective-permute-start.3 = (bf16[2,480,2304]{2,1,0:T(8,128)(2,1)}, bf16[2,480,2304]{2,1,0:T(8,128)(2,1)}, u32[]{:S(2)}, u32[]{:S(2)}) collective-permute-start(bf16[2,480,2304]{2,1,0:T(8,128)(2,1)} %get-tuple-element.30), channel_id=1, source_target_pairs={{0,1},{1,0},{2,3},{3,2},{4,5},{5,4},{6,7},{7,6},{8,9},{9,8},{10,11... | collective-permute-start | bytes 13271048 | tf_op jit(solution)/shard_map/ppermute | solution.py:352
  472.1 270.2 %collective-permute-start.10 = (bf16[2,160,2304]{2,1,0:T(8,128)(2,1)}, bf16[2,160,2304]{2,1,0:T(8,128)(2,1)}, u32[]{:S(2)}, u32[]{:S(2)}) collective-permute-start(bf16[2,160,2304]{2,1,0:T(8,128)(2,1)} %get-tuple-element.34), channel_id=1, source_target_pairs={{0,1},{1,0},{2,3},{3,2},{4,5},{5,4},{6,7},{7,6},{8,9},{9,8},{10,11... | collective-permute-start | bytes 4423688 | tf_op jit(solution)/shard_map/ppermute | solution.py:352
  539.8 203.8 %collective-permute-start.11 = (bf16[2,160,2304]{2,1,0:T(8,128)(2,1)}, bf16[2,160,2304]{2,1,0:T(8,128)(2,1)}, u32[]{:S(2)}, u32[]{:S(2)}) collective-permute-start(bf16[2,160,2304]{2,1,0:T(8,128)(2,1)} %get-tuple-element.35), channel_id=1, source_target_pairs={{0,2},{1,3},{2,0},{3,1},{4,6},{5,7},{6,4},{7,5},{8,10},{9,11},{10,... | collective-permute-start | bytes 4423688 | tf_op jit(solution)/shard_map/ppermute | solution.py:352
  633.0 37.9 %collective-permute-start.17 = (bf16[1,160,2304]{2,1,0:T(8,128)(2,1)}, bf16[1,160,2304]{2,1,0:T(8,128)(2,1)}, u32[]{:S(2)}, u32[]{:S(2)}) collective-permute-start(bf16[1,160,2304]{2,1,0:T(8,128)(2,1)} %get-tuple-element.41), channel_id=1, source_target_pairs={{0,2},{1,3},{2,0},{3,1},{4,6},{5,7},{6,4},{7,5},{8,10},{9,11},{10,... | collective-permute-start | bytes 2211848 | tf_op jit(solution)/shard_map/ppermute | solution.py:352
  633.0 107.1 %collective-permute-start.18 = (bf16[1,160,2304]{2,1,0:T(8,128)(2,1)}, bf16[1,160,2304]{2,1,0:T(8,128)(2,1)}, u32[]{:S(2)}, u32[]{:S(2)}) collective-permute-start(bf16[1,160,2304]{2,1,0:T(8,128)(2,1)} %get-tuple-element.42), channel_id=1, source_target_pairs={{0,3},{1,2},{2,1},{3,0},{4,7},{5,6},{6,5},{7,4},{8,11},{9,10},{10,... | collective-permute-start | bytes 2211848 | tf_op jit(solution)/shard_map/ppermute | solution.py:352
  670.9 69.4 %collective-permute-start.19 = (bf16[1,160,2304]{2,1,0:T(8,128)(2,1)}, bf16[1,160,2304]{2,1,0:T(8,128)(2,1)}, u32[]{:S(2)}, u32[]{:S(2)}) collective-permute-start(bf16[1,160,2304]{2,1,0:T(8,128)(2,1)} %get-tuple-element.43), channel_id=1, source_target_pairs={{0,2},{1,3},{2,0},{3,1},{4,6},{5,7},{6,4},{7,5},{8,10},{9,11},{10,... | collective-permute-start | bytes 2211848 | tf_op jit(solution)/shard_map/ppermute | solution.py:352
  670.9 70.8 %collective-permute-start.20 = (bf16[1,160,2304]{2,1,0:T(8,128)(2,1)}, bf16[1,160,2304]{2,1,0:T(8,128)(2,1)}, u32[]{:S(2)}, u32[]{:S(2)}) collective-permute-start(bf16[1,160,2304]{2,1,0:T(8,128)(2,1)} %get-tuple-element.44), channel_id=1, source_target_pairs={{0,3},{1,2},{2,1},{3,0},{4,7},{5,6},{6,5},{7,4},{8,11},{9,10},{10,... | collective-permute-start | bytes 2211848 | tf_op jit(solution)/shard_map/ppermute | solution.py:352
  740.0 39.5 %collective-permute-start.12 = (bf16[2,160,2304]{2,1,0:T(8,128)(2,1)}, bf16[2,160,2304]{2,1,0:T(8,128)(2,1)}, u32[]{:S(2)}, u32[]{:S(2)}) collective-permute-start(bf16[2,160,2304]{2,1,0:T(8,128)(2,1)} %get-tuple-element.36), channel_id=1, source_target_pairs={{0,3},{1,2},{2,1},{3,0},{4,7},{5,6},{6,5},{7,4},{8,11},{9,10},{10,... | collective-permute-start | bytes 4423688 | tf_op jit(solution)/shard_map/ppermute | solution.py:352
  740.3 65.8 %collective-permute-start.13 = (bf16[2,160,2304]{2,1,0:T(8,128)(2,1)}, bf16[2,160,2304]{2,1,0:T(8,128)(2,1)}, u32[]{:S(2)}, u32[]{:S(2)}) collective-permute-start(bf16[2,160,2304]{2,1,0:T(8,128)(2,1)} %get-tuple-element.37), channel_id=1, source_target_pairs={{0,2},{1,3},{2,0},{3,1},{4,6},{5,7},{6,4},{7,5},{8,10},{9,11},{10,... | collective-permute-start | bytes 4423688 | tf_op jit(solution)/shard_map/ppermute | solution.py:352
  741.7 96.5 %collective-permute-start.14 = (bf16[2,160,2304]{2,1,0:T(8,128)(2,1)}, bf16[2,160,2304]{2,1,0:T(8,128)(2,1)}, u32[]{:S(2)}, u32[]{:S(2)}) collective-permute-start(bf16[2,160,2304]{2,1,0:T(8,128)(2,1)} %get-tuple-element.38), channel_id=1, source_target_pairs={{0,3},{1,2},{2,1},{3,0},{4,7},{5,6},{6,5},{7,4},{8,11},{9,10},{10,... | collective-permute-start | bytes 4423688 | tf_op jit(solution)/shard_map/ppermute | solution.py:352
  742.2 127.0 %collective-permute-start.15 = (bf16[2,160,2304]{2,1,0:T(8,128)(2,1)}, bf16[2,160,2304]{2,1,0:T(8,128)(2,1)}, u32[]{:S(2)}, u32[]{:S(2)}) collective-permute-start(bf16[2,160,2304]{2,1,0:T(8,128)(2,1)} %get-tuple-element.39), channel_id=1, source_target_pairs={{0,2},{1,3},{2,0},{3,1},{4,6},{5,7},{6,4},{7,5},{8,10},{9,11},{10,... | collective-permute-start | bytes 4423688 | tf_op jit(solution)/shard_map/ppermute | solution.py:352
  743.5 157.4 %collective-permute-start.16 = (bf16[2,160,2304]{2,1,0:T(8,128)(2,1)}, bf16[2,160,2304]{2,1,0:T(8,128)(2,1)}, u32[]{:S(2)}, u32[]{:S(2)}) collective-permute-start(bf16[2,160,2304]{2,1,0:T(8,128)(2,1)} %get-tuple-element.40), channel_id=1, source_target_pairs={{0,3},{1,2},{2,1},{3,0},{4,7},{5,6},{6,5},{7,4},{8,11},{9,10},{10,... | collective-permute-start | bytes 4423688 | tf_op jit(solution)/shard_map/ppermute | solution.py:352

commit v5 on v4

--- a/solution.py
+++ b/solution.py
@@ -13,11 +13,12 @@
 VMEM_LIMIT = 67043328
 NORM_ROWS = 256
 GATE_ROWS = 512
-PACK_ROWS = 512
+PACK_ROWS = 256
 PACK_WIN = 128
-FAR_TILE = 160
-NEAR_TILE = 240
-LATE_TILE = 80
+FAR_TILE = 192
+NEAR_TILE = 256
+LATE_TILE = 64
+LATE_ROWS = 128
 FF_BLOCK = 1280
 FF_SPLIT = 768
 MIX_ROWS = 512
@@ -140,24 +141,33 @@
         rows_ref[...] = jnp.zeros_like(rows_ref)
 
     def pack(block_ref):
+        sublane = lax.broadcasted_iota(I32, (PACK_WIN, PACK_ROWS), 0)
+        spans, slots = [], []
         for e in range(experts):
             begin = meta_ref[e, mark(tokens, PACK_ROWS, step)]
-            end = meta_ref[e, mark(tokens, PACK_ROWS, step + 1)]
             base = (begin // 16) * 16
-            windows = jnp.where(end > begin, (end - base + PACK_WIN - 1) // PACK_WIN, 0)
-            slots = jnp.broadcast_to(pos_ref[e:e + 1, :], (PACK_WIN, PACK_ROWS))
-            sublane = lax.broadcasted_iota(I32, (PACK_WIN, PACK_ROWS), 0)
+            spans.append((base, meta_ref[e, mark(tokens, PACK_ROWS, step + 1)] - base))
+            slots.append(jnp.broadcast_to(pos_ref[e:e + 1, :], (PACK_WIN, PACK_ROWS)))
+
+        def onehot(e, at):
+            return (slots[e] - at == sublane).astype(F32)
+
+        def put(e, at, picked):
+            head, body = pl.ds(pl.multiple_of(at, 16), 16), pl.ds(pl.multiple_of(at + 16, 16), PACK_WIN - 16)
+            rows_ref[e, head, :] = (rows_ref[e, head, :].astype(F32) + picked[:16]).astype(BF16)
+            rows_ref[e, body, :] = picked[16:].astype(BF16)
+
+        joined = jnp.concatenate([onehot(e, spans[e][0]) for e in range(experts)], axis=0).astype(BF16)
+        picked = jnp.dot(joined, block_ref[...], preferred_element_type=F32)
+        for e in range(experts):
+            put(e, spans[e][0], picked[e * PACK_WIN:(e + 1) * PACK_WIN])
 
             def window(w, carry):
-                at = pl.multiple_of(base + w * PACK_WIN, 16)
-                onehot = (slots - at == sublane).astype(F32).astype(BF16)
-                picked = jnp.dot(onehot, block_ref[...], preferred_element_type=F32)
-                held = rows_ref[e, pl.ds(at, 16), :]
-                rows_ref[e, pl.ds(at, 16), :] = (held.astype(F32) + picked[:16]).astype(BF16)
-                rows_ref[e, pl.ds(pl.multiple_of(at + 16, 16), PACK_WIN - 16), :] = picked[16:].astype(BF16)
+                at = spans[e][0] + w * PACK_WIN
+                put(e, at, jnp.dot(onehot(e, at).astype(BF16), block_ref[...], preferred_element_type=F32))
                 return carry
 
-            lax.fori_loop(0, windows, window, 0)
+            lax.fori_loop(1, (spans[e][1] + PACK_WIN - 1) // PACK_WIN, window, 0)
 
     pl.when(step < half_steps)(lambda: pack(low_ref))
     pl.when(step >= half_steps)(lambda: pack(high_ref))
@@ -379,7 +389,8 @@
             return mlp_call(tokens, begin, rows, tile_rows, first_expert, count, [metas[m] for m in places],
                             [packed[m] for m in places], w_gate, w_up, w_down)
 
-        late = capacity - FAR_TILE
+        late = capacity - LATE_ROWS
+        final = late // FAR_TILE * FAR_TILE
         packed[0], packed[1] = pack(0), pack(1)
         near_early = run((0, 1), 0, late, NEAR_TILE)
         near_rows = [((0, 0), near_early[0]), ((local, 0), swap(near_early[1], 1))]
@@ -391,14 +402,13 @@
             far_rows.append(((expert, at), swap(two, 2)))
             far_rows.append(((local + expert, at), swap(three, 3)))
 
-        for c in range(late // FAR_TILE - 1):
+        for c in range(final // FAR_TILE):
             send_far(0, c * FAR_TILE, *run((2, 3), c * FAR_TILE, FAR_TILE, FAR_TILE))
-        zero, one, two, three = run((0, 1, 2, 3), late, FAR_TILE, LATE_TILE)
+        zero, one, two, three = run((0, 1, 2, 3), late, LATE_ROWS, LATE_TILE)
         send_far(0, late, two, three)
         near_rows += [((0, late), zero), ((local, late), swap(one, 1))]
-        final = late - FAR_TILE
         for e in range(local):
-            send_far(e, final, *run((2, 3), final, FAR_TILE, FAR_TILE, e, 1))
+            send_far(e, final, *run((2, 3), final, late - final, late - final, e, 1))
 
         gates = [gate_call(part, u, w_router.T, choice_t, rel_t, mask_first.T, mask_second.T)
                  for part, u in enumerate(halves)]

time: 930 us -> 936 us (level)
  the two profiles are of different devices: /device:TPU:15 before, /device:TPU:0 now
where the time goes in v5:
time: 936 us; the launch traced here: 928 us
  Pallas kernels  543 us (58%)
  waiting for transfers between devices  320 us (34%)
  starting transfers between devices  59.4 us (6%)
    pallas_call x6, Pallas kernels, mlp_call(): pl.pallas_call(functools.partial(mlp_kernel, begin, tile_rows, tokens, fi...  424 us
    ppermute x21, waiting for transfers between devices, swap(): lax.ppermute(array, 'ep', [(i, i ^ distance) for i in range(group_size)])  320 us
    ppermute x21, starting transfers between devices, swap(): lax.ppermute(array, 'ep', [(i, i ^ distance) for i in range(group_size)])  59.4 us
    pallas_call x4, Pallas kernels, pack_call(): pl.pallas_call(functools.partial(pack_kernel, half_steps), grid_spec=pltp...  51.3 us
    pallas_call x2, Pallas kernels, mix_call(): pl.pallas_call(functools.partial(mix_kernel, columns, starts_at, capacity...  44.4 us
  transfers between devices with their start and end apart: 21, of which 3 were waited for; matrix products, arithmetic and copies ran while one was open for 1% of the time, Pallas kernels for 55%

profile of v5, /device:TPU:0, one launch (start us, length us, event | category | flops | bytes accessed | tf_op | source)
XLA Modules:
  0.0 927.6 jit_solution(2346388003590333814)
XLA Ops:
  0.0 6.7 norm.2.u_ref.low_ref
  7.5 2.5 collective-permute-start.6
  9.9 6.7 norm.3.u_ref.high_ref
  16.8 1.6 route.1
  18.8 12.8 %pack.4.refs_2_.refs_4_ = bf16[2,768,2304]{2,1,0:T(8,128)(2,1)} custom-call(s32[2,2176]{1,0:T(2,128)} %get-tuple-element.27.meta_ref.pos_ref.refs_0_, s32[2,2176]{1,0:T(2,128)} %get-tuple-element.27.meta_ref.pos_ref.refs_0_, bf16[1024,2304]{1,0:T(8,128)(2,1)} %norm.2.u_ref.low_ref, bf16[1024,2304]{1,0:T(8,128)(2,1)} %norm.3.u_ref.high_ref), custom_call_target="tpu_custom_call" | custom-call | flops 2415919104 | bytes 28311552 | tf_op jit(solution)/shard_map/pack/pallas_call | solution.py:181
  31.6 2.0 collective-permute-start.4
  33.6 79.3 %collective-permute-done.6.low_ref = bf16[1024,2304]{1,0:T(8,128)(2,1)} collective-permute-done((bf16[1024,2304]{1,0:T(8,128)(2,1)}, bf16[1024,2304]{1,0:T(8,128)(2,1)}, u32[]{:S(2)}, u32[]{:S(2)}) %collective-permute-start.6) | collective-permute-done | bytes 4718624 | tf_op jit(solution)/shard_map/ppermute | solution.py:362
  112.9 101.1 %collective-permute-done.7.high_ref = bf16[1024,2304]{1,0:T(8,128)(2,1)} collective-permute-done((bf16[1024,2304]{1,0:T(8,128)(2,1)}, bf16[1024,2304]{1,0:T(8,128)(2,1)}, u32[]{:S(2)}, u32[]{:S(2)}) %collective-permute-start.7) | collective-permute-done | bytes 4718624 | tf_op jit(solution)/shard_map/ppermute | solution.py:362
  214.0 12.7 %pack.5.refs_3_.refs_5_ = bf16[2,768,2304]{2,1,0:T(8,128)(2,1)} custom-call(s32[2,2176]{1,0:T(2,128)} %collective-permute-done.meta_ref.pos_ref.refs_1_, s32[2,2176]{1,0:T(2,128)} %collective-permute-done.meta_ref.pos_ref.refs_1_, bf16[1024,2304]{1,0:T(8,128)(2,1)} %collective-permute-done.1.low_ref, bf16[1024,2304]{1,0:T(8,128)(2,1)} %collective-permute-done.2.high_ref), custom_call_target="tpu_custom_call" | custom-call | flops 2415919104 | bytes 28311552 | tf_op jit(solution)/shard_map/pack/pallas_call | solution.py:181
  226.8 189.8 %mlp.6 = (bf16[2,512,2304]{2,1,0:T(8,128)(2,1)}, bf16[2,512,2304]{2,1,0:T(8,128)(2,1)}) custom-call(s32[2,2176]{1,0:T(2,128)} %get-tuple-element.27.meta_ref.pos_ref.refs_0_, s32[2,2176]{1,0:T(2,128)} %collective-permute-done.meta_ref.pos_ref.refs_1_, bf16[2,768,2304]{2,1,0:T(8,128)(2,1)} %pack.4.refs_2_.refs_4_, bf16[2,768,2304]{2,1,0:T(8,128)(2,1)} %pack.5.refs_3_.refs_5_, ...), custom_call_target="tpu_custom_call" | custom-call | flops 163074539520 | bytes 159252480 | tf_op jit(solution)/shard_map/mlp/pallas_call | solution.py:274
  417.0 13.0 %pack.6.refs_6_.refs_2_ = bf16[2,768,2304]{2,1,0:T(8,128)(2,1)} custom-call(s32[2,2176]{1,0:T(2,128)} %collective-permute-done.4.meta_ref.pos_ref.refs_2_.refs_0_, s32[2,2176]{1,0:T(2,128)} %collective-permute-done.4.meta_ref.pos_ref.refs_2_.refs_0_, bf16[1024,2304]{1,0:T(8,128)(2,1)} %collective-permute-done.6.low_ref, ...), custom_call_target="tpu_custom_call" | custom-call | flops 2415919104 | bytes 28311552 | tf_op jit(solution)/shard_map/pack/pallas_call | solution.py:181
  430.0 12.8 %pack.7.refs_7_.refs_3_ = bf16[2,768,2304]{2,1,0:T(8,128)(2,1)} custom-call(s32[2,2176]{1,0:T(2,128)} %collective-permute-done.5.meta_ref.pos_ref.refs_3_.refs_1_, s32[2,2176]{1,0:T(2,128)} %collective-permute-done.5.meta_ref.pos_ref.refs_3_.refs_1_, bf16[1024,2304]{1,0:T(8,128)(2,1)} %collective-permute-done.8.low_ref, ...), custom_call_target="tpu_custom_call" | custom-call | flops 2415919104 | bytes 28311552 | tf_op jit(solution)/shard_map/pack/pallas_call | solution.py:181
  442.8 13.4 %mlp.7 = (bf16[2,128,2304]{2,1,0:T(8,128)(2,1)}, bf16[2,128,2304]{2,1,0:T(8,128)(2,1)}, bf16[2,128,2304]{2,1,0:T(8,128)(2,1)}, bf16[2,128,2304]{2,1,0:T(8,128)(2,1)}) custom-call(s32[2,2176]{1,0:T(2,128)} %get-tuple-element.27.meta_ref.pos_ref.refs_0_, s32[2,2176]{1,0:T(2,128)} %collective-permute-done.meta_ref.pos_ref.refs_1_, ...), custom_call_target="tpu_custom_call" | custom-call | flops 81537269760 | bytes 159252480 | tf_op jit(solution)/shard_map/mlp/pallas_call | solution.py:274
  456.2 45.8 %collective-permute-start.15 = (bf16[2,128,2304]{2,1,0:T(8,128)(2,1)}, bf16[2,128,2304]{2,1,0:T(8,128)(2,1)}, u32[]{:S(2)}, u32[]{:S(2)}) collective-permute-start(bf16[2,128,2304]{2,1,0:T(8,128)(2,1)} %get-tuple-element.39), channel_id=1, source_target_pairs={{0,2},{1,3},{2,0},{3,1},{4,6},{5,7},{6,4},{7,5},{8,10},{9,11},{10,... | collective-permute-start | bytes 3538952 | tf_op jit(solution)/shard_map/ppermute | solution.py:362
  502.1 32.6 %mlp.10 = (bf16[1,128,2304]{2,1,0:T(8,128)(2,1)}, bf16[1,128,2304]{2,1,0:T(8,128)(2,1)}) custom-call(s32[2,2176]{1,0:T(2,128)} %collective-permute-done.4.meta_ref.pos_ref.refs_2_.refs_0_, s32[2,2176]{1,0:T(2,128)} %collective-permute-done.5.meta_ref.pos_ref.refs_3_.refs_1_, bf16[2,768,2304]{2,1,0:T(8,128)(2,1)} %pack.6.refs_6_.refs_2_, ...), custom_call_target="tpu_custom_call" | custom-call | flops 20384317440 | bytes 79626240 | tf_op jit(solution)/shard_map/mlp/pallas_call | solution.py:274
  535.8 77.8 %mlp.8 = (bf16[2,192,2304]{2,1,0:T(8,128)(2,1)}, bf16[2,192,2304]{2,1,0:T(8,128)(2,1)}) custom-call(s32[2,2176]{1,0:T(2,128)} %collective-permute-done.4.meta_ref.pos_ref.refs_2_.refs_0_, s32[2,2176]{1,0:T(2,128)} %collective-permute-done.5.meta_ref.pos_ref.refs_3_.refs_1_, bf16[2,768,2304]{2,1,0:T(8,128)(2,1)} %pack.6.refs_6_.refs_2_, ...), custom_call_target="tpu_custom_call" | custom-call | flops 61152952320 | bytes 159252480 | tf_op jit(solution)/shard_map/mlp/pallas_call | solution.py:274
  613.6 32.8 %mlp.11 = (bf16[1,128,2304]{2,1,0:T(8,128)(2,1)}, bf16[1,128,2304]{2,1,0:T(8,128)(2,1)}) custom-call(s32[2,2176]{1,0:T(2,128)} %collective-permute-done.4.meta_ref.pos_ref.refs_2_.refs_0_, s32[2,2176]{1,0:T(2,128)} %collective-permute-done.5.meta_ref.pos_ref.refs_3_.refs_1_, bf16[2,768,2304]{2,1,0:T(8,128)(2,1)} %pack.6.refs_6_.refs_2_, ...), custom_call_target="tpu_custom_call" | custom-call | flops 20384317440 | bytes 79626240 | tf_op jit(solution)/shard_map/mlp/pallas_call | solution.py:274
  647.4 1.5 collective-permute-start.20
  648.8 77.8 %mlp.9 = (bf16[2,192,2304]{2,1,0:T(8,128)(2,1)}, bf16[2,192,2304]{2,1,0:T(8,128)(2,1)}) custom-call(s32[2,2176]{1,0:T(2,128)} %collective-permute-done.4.meta_ref.pos_ref.refs_2_.refs_0_, s32[2,2176]{1,0:T(2,128)} %collective-permute-done.5.meta_ref.pos_ref.refs_3_.refs_1_, bf16[2,768,2304]{2,1,0:T(8,128)(2,1)} %pack.6.refs_6_.refs_2_, ...), custom_call_target="tpu_custom_call" | custom-call | flops 61152952320 | bytes 159252480 | tf_op jit(solution)/shard_map/mlp/pallas_call | solution.py:274
  733.9 3.9 gate.3
  737.8 3.9 gate.2
  743.7 22.2 %mix.2.base_ref = f32[2048,2304]{1,0:T(8,128)} custom-call(s32[8,128]{1,0:T(8,128)} %slice.6.start_ref, bf16[2048,2304]{1,0:T(8,128)(2,1)} %base_ref.1, s32[2048,8]{1,0:T(8,128)} %bitcast.7, f32[2048,8]{1,0:T(8,128)} %bitcast.9, bf16[2,512,2304]{2,1,0:T(8,128)(2,1)} %get-tuple-element.29.rest_0_, bf16[2,512,2304]{2,1,0:T(8,128)(2,1)} %collective-permute-done.3.rest_1_, ...), custom_call_target="tpu_custom_call" | custom-call | flops 9663676416 | bytes 47185920 | tf_op jit(solution)/shard_map/mix/pallas_call | solution.py:340
  765.9 139.3 %collective-permute-done.16.rest_5_ = bf16[2,128,2304]{2,1,0:T(8,128)(2,1)} collective-permute-done((bf16[2,128,2304]{2,1,0:T(8,128)(2,1)}, bf16[2,128,2304]{2,1,0:T(8,128)(2,1)}, u32[]{:S(2)}, u32[]{:S(2)}) %collective-permute-start.16) | collective-permute-done | bytes 1179680 | tf_op jit(solution)/shard_map/ppermute | solution.py:362
  905.2 22.2 %mix.3 = bf16[2048,2304]{1,0:T(8,128)(2,1)} custom-call(s32[8,128]{1,0:T(8,128)} %slice.6.start_ref, f32[2048,2304]{1,0:T(8,128)} %mix.2.base_ref, s32[2048,8]{1,0:T(8,128)} %bitcast.8, f32[2048,8]{1,0:T(8,128)} %bitcast.10, bf16[2,192,2304]{2,1,0:T(8,128)(2,1)} %collective-permute-done.11.rest_0_, bf16[2,192,2304]{2,1,0:T(8,128)(2,1)} %collective-permute-done.12.rest_1_, ...), custom_call_target="tpu_custom_call" | custom-call | flops 9663676416 | bytes 47185920 | tf_op jit(solution)/shard_map/mix/pallas_call | solution.py:340
  (40 shorter events, 13.2 us)
Async XLA Ops:
  6.7 26.9 %collective-permute-start.1 = (bf16[1024,2304]{1,0:T(8,128)(2,1)}, bf16[1024,2304]{1,0:T(8,128)(2,1)}, u32[]{:S(2)}, u32[]{:S(2)}) collective-permute-start(bf16[1024,2304]{1,0:T(8,128)(2,1)} %norm.2.u_ref.low_ref), channel_id=1, source_target_pairs={{0,1},{1,0},{2,3},{3,2},{4,5},{5,4},{6,7},{7,6},{8,9},{9,8},{10,11... | collective-permute-start | bytes 14155784 | tf_op jit(solution)/shard_map/ppermute | solution.py:362
  7.5 105.5 %collective-permute-start.6 = (bf16[1024,2304]{1,0:T(8,128)(2,1)}, bf16[1024,2304]{1,0:T(8,128)(2,1)}, u32[]{:S(2)}, u32[]{:S(2)}) collective-permute-start(bf16[1024,2304]{1,0:T(8,128)(2,1)} %norm.2.u_ref.low_ref), channel_id=1, source_target_pairs={{0,2},{1,3},{2,0},{3,1},{4,6},{5,7},{6,4},{7,5},{8,10},{9,11},{10,... | collective-permute-start | bytes 14155784 | tf_op jit(solution)/shard_map/ppermute | solution.py:362
  16.6 197.4 %collective-permute-start.7 = (bf16[1024,2304]{1,0:T(8,128)(2,1)}, bf16[1024,2304]{1,0:T(8,128)(2,1)}, u32[]{:S(2)}, u32[]{:S(2)}) collective-permute-start(bf16[1024,2304]{1,0:T(8,128)(2,1)} %norm.3.u_ref.high_ref), channel_id=1, source_target_pairs={{0,2},{1,3},{2,0},{3,1},{4,6},{5,7},{6,4},{7,5},{8,10},{9,11},{10,... | collective-permute-start | bytes 14155784 | tf_op jit(solution)/shard_map/ppermute | solution.py:362
  16.6 197.4 %collective-permute-start.2 = (bf16[1024,2304]{1,0:T(8,128)(2,1)}, bf16[1024,2304]{1,0:T(8,128)(2,1)}, u32[]{:S(2)}, u32[]{:S(2)}) collective-permute-start(bf16[1024,2304]{1,0:T(8,128)(2,1)} %norm.3.u_ref.high_ref), channel_id=1, source_target_pairs={{0,1},{1,0},{2,3},{3,2},{4,5},{5,4},{6,7},{7,6},{8,9},{9,8},{10,11... | collective-permute-start | bytes 14155784 | tf_op jit(solution)/shard_map/ppermute | solution.py:362
  18.5 13.1 %collective-permute-start = (s32[2,2176]{1,0:T(2,128)}, s32[2,2176]{1,0:T(2,128)}, u32[]{:S(2)}, u32[]{:S(2)}) collective-permute-start(s32[2,2176]{1,0:T(2,128)} %get-tuple-element.28), channel_id=1, source_target_pairs={{0,1},{1,0},{2,3},{3,2},{4,5},{5,4},{6,7},{7,6},{8,9},{9,8},{10,11... | collective-permute-start | bytes 52232 | tf_op jit(solution)/shard_map/ppermute | solution.py:362
  31.6 385.4 %collective-permute-start.4 = (s32[2,2176]{1,0:T(2,128)}, s32[2,2176]{1,0:T(2,128)}, u32[]{:S(2)}, u32[]{:S(2)}) collective-permute-start(s32[2,2176]{1,0:T(2,128)} %get-tuple-element.31), channel_id=1, source_target_pairs={{0,2},{1,3},{2,0},{3,1},{4,6},{5,7},{6,4},{7,5},{8,10},{9,11},{10,... | collective-permute-start | bytes 52232 | tf_op jit(solution)/shard_map/ppermute | solution.py:362
  33.6 396.4 %collective-permute-start.5 = (s32[2,2176]{1,0:T(2,128)}, s32[2,2176]{1,0:T(2,128)}, u32[]{:S(2)}, u32[]{:S(2)}) collective-permute-start(s32[2,2176]{1,0:T(2,128)} %get-tuple-element.32), channel_id=1, source_target_pairs={{0,3},{1,2},{2,1},{3,0},{4,7},{5,6},{6,5},{7,4},{8,11},{9,10},{10,... | collective-permute-start | bytes 52232 | tf_op jit(solution)/shard_map/ppermute | solution.py:362
  112.9 317.1 %collective-permute-start.8 = (bf16[1024,2304]{1,0:T(8,128)(2,1)}, bf16[1024,2304]{1,0:T(8,128)(2,1)}, u32[]{:S(2)}, u32[]{:S(2)}) collective-permute-start(bf16[1024,2304]{1,0:T(8,128)(2,1)} %collective-permute-done.6.low_ref), channel_id=1, source_target_pairs={{0,1},{1,0},{2,3},{3,2},{4,5},{5,4},{6,7},{7,6},{8,9},{9,8},{10,11... | collective-permute-start | bytes 14155784 | tf_op jit(solution)/shard_map/ppermute | solution.py:362
  214.0 216.0 %collective-permute-start.9 = (bf16[1024,2304]{1,0:T(8,128)(2,1)}, bf16[1024,2304]{1,0:T(8,128)(2,1)}, u32[]{:S(2)}, u32[]{:S(2)}) collective-permute-start(bf16[1024,2304]{1,0:T(8,128)(2,1)} %collective-permute-done.7.high_ref), channel_id=1, source_target_pairs={{0,1},{1,0},{2,3},{3,2},{4,5},{5,4},{6,7},{7,6},{8,9},{9,8},{10,11... | collective-permute-start | bytes 14155784 | tf_op jit(solution)/shard_map/ppermute | solution.py:362
  416.5 229.9 %collective-permute-start.3 = (bf16[2,512,2304]{2,1,0:T(8,128)(2,1)}, bf16[2,512,2304]{2,1,0:T(8,128)(2,1)}, u32[]{:S(2)}, u32[]{:S(2)}) collective-permute-start(bf16[2,512,2304]{2,1,0:T(8,128)(2,1)} %get-tuple-element.30), channel_id=1, source_target_pairs={{0,1},{1,0},{2,3},{3,2},{4,5},{5,4},{6,7},{7,6},{8,9},{9,8},{10,11... | collective-permute-start | bytes 14155784 | tf_op jit(solution)/shard_map/ppermute | solution.py:362
  456.2 272.6 %collective-permute-start.10 = (bf16[2,128,2304]{2,1,0:T(8,128)(2,1)}, bf16[2,128,2304]{2,1,0:T(8,128)(2,1)}, u32[]{:S(2)}, u32[]{:S(2)}) collective-permute-start(bf16[2,128,2304]{2,1,0:T(8,128)(2,1)} %get-tuple-element.34), channel_id=1, source_target_pairs={{0,1},{1,0},{2,3},{3,2},{4,5},{5,4},{6,7},{7,6},{8,9},{9,8},{10,11... | collective-permute-start | bytes 3538952 | tf_op jit(solution)/shard_map/ppermute | solution.py:362
  456.2 274.0 %collective-permute-start.15 = (bf16[2,128,2304]{2,1,0:T(8,128)(2,1)}, bf16[2,128,2304]{2,1,0:T(8,128)(2,1)}, u32[]{:S(2)}, u32[]{:S(2)}) collective-permute-start(bf16[2,128,2304]{2,1,0:T(8,128)(2,1)} %get-tuple-element.39), channel_id=1, source_target_pairs={{0,2},{1,3},{2,0},{3,1},{4,6},{5,7},{6,4},{7,5},{8,10},{9,11},{10,... | collective-permute-start | bytes 3538952 | tf_op jit(solution)/shard_map/ppermute | solution.py:362
  534.7 112.7 %collective-permute-start.17 = (bf16[1,128,2304]{2,1,0:T(8,128)(2,1)}, bf16[1,128,2304]{2,1,0:T(8,128)(2,1)}, u32[]{:S(2)}, u32[]{:S(2)}) collective-permute-start(bf16[1,128,2304]{2,1,0:T(8,128)(2,1)} %get-tuple-element.41), channel_id=1, source_target_pairs={{0,2},{1,3},{2,0},{3,1},{4,6},{5,7},{6,4},{7,5},{8,10},{9,11},{10,... | collective-permute-start | bytes 1769480 | tf_op jit(solution)/shard_map/ppermute | solution.py:362
  534.7 192.0 %collective-permute-start.18 = (bf16[1,128,2304]{2,1,0:T(8,128)(2,1)}, bf16[1,128,2304]{2,1,0:T(8,128)(2,1)}, u32[]{:S(2)}, u32[]{:S(2)}) collective-permute-start(bf16[1,128,2304]{2,1,0:T(8,128)(2,1)} %get-tuple-element.42), channel_id=1, source_target_pairs={{0,3},{1,2},{2,1},{3,0},{4,7},{5,6},{6,5},{7,4},{8,11},{9,10},{10,... | collective-permute-start | bytes 1769480 | tf_op jit(solution)/shard_map/ppermute | solution.py:362
  646.5 80.5 %collective-permute-start.19 = (bf16[1,128,2304]{2,1,0:T(8,128)(2,1)}, bf16[1,128,2304]{2,1,0:T(8,128)(2,1)}, u32[]{:S(2)}, u32[]{:S(2)}) collective-permute-start(bf16[1,128,2304]{2,1,0:T(8,128)(2,1)} %get-tuple-element.43), channel_id=1, source_target_pairs={{0,2},{1,3},{2,0},{3,1},{4,6},{5,7},{6,4},{7,5},{8,10},{9,11},{10,... | collective-permute-start | bytes 1769480 | tf_op jit(solution)/shard_map/ppermute | solution.py:362
  647.4 80.5 %collective-permute-start.20 = (bf16[1,128,2304]{2,1,0:T(8,128)(2,1)}, bf16[1,128,2304]{2,1,0:T(8,128)(2,1)}, u32[]{:S(2)}, u32[]{:S(2)}) collective-permute-start(bf16[1,128,2304]{2,1,0:T(8,128)(2,1)} %get-tuple-element.44), channel_id=1, source_target_pairs={{0,3},{1,2},{2,1},{3,0},{4,7},{5,6},{6,5},{7,4},{8,11},{9,10},{10,... | collective-permute-start | bytes 1769480 | tf_op jit(solution)/shard_map/ppermute | solution.py:362
  726.7 178.5 %collective-permute-start.11 = (bf16[2,192,2304]{2,1,0:T(8,128)(2,1)}, bf16[2,192,2304]{2,1,0:T(8,128)(2,1)}, u32[]{:S(2)}, u32[]{:S(2)}) collective-permute-start(bf16[2,192,2304]{2,1,0:T(8,128)(2,1)} %get-tuple-element.35), channel_id=1, source_target_pairs={{0,2},{1,3},{2,0},{3,1},{4,6},{5,7},{6,4},{7,5},{8,10},{9,11},{10,... | collective-permute-start | bytes 5308424 | tf_op jit(solution)/shard_map/ppermute | solution.py:362
  727.0 178.1 %collective-permute-start.12 = (bf16[2,192,2304]{2,1,0:T(8,128)(2,1)}, bf16[2,192,2304]{2,1,0:T(8,128)(2,1)}, u32[]{:S(2)}, u32[]{:S(2)}) collective-permute-start(bf16[2,192,2304]{2,1,0:T(8,128)(2,1)} %get-tuple-element.36), channel_id=1, source_target_pairs={{0,3},{1,2},{2,1},{3,0},{4,7},{5,6},{6,5},{7,4},{8,11},{9,10},{10,... | collective-permute-start | bytes 5308424 | tf_op jit(solution)/shard_map/ppermute | solution.py:362
  727.8 177.3 %collective-permute-start.13 = (bf16[2,192,2304]{2,1,0:T(8,128)(2,1)}, bf16[2,192,2304]{2,1,0:T(8,128)(2,1)}, u32[]{:S(2)}, u32[]{:S(2)}) collective-permute-start(bf16[2,192,2304]{2,1,0:T(8,128)(2,1)} %get-tuple-element.37), channel_id=1, source_target_pairs={{0,2},{1,3},{2,0},{3,1},{4,6},{5,7},{6,4},{7,5},{8,10},{9,11},{10,... | collective-permute-start | bytes 5308424 | tf_op jit(solution)/shard_map/ppermute | solution.py:362
  728.8 176.4 %collective-permute-start.14 = (bf16[2,192,2304]{2,1,0:T(8,128)(2,1)}, bf16[2,192,2304]{2,1,0:T(8,128)(2,1)}, u32[]{:S(2)}, u32[]{:S(2)}) collective-permute-start(bf16[2,192,2304]{2,1,0:T(8,128)(2,1)} %get-tuple-element.38), channel_id=1, source_target_pairs={{0,3},{1,2},{2,1},{3,0},{4,7},{5,6},{6,5},{7,4},{8,11},{9,10},{10,... | collective-permute-start | bytes 5308424 | tf_op jit(solution)/shard_map/ppermute | solution.py:362
  730.2 175.0 %collective-permute-start.16 = (bf16[2,128,2304]{2,1,0:T(8,128)(2,1)}, bf16[2,128,2304]{2,1,0:T(8,128)(2,1)}, u32[]{:S(2)}, u32[]{:S(2)}) collective-permute-start(bf16[2,128,2304]{2,1,0:T(8,128)(2,1)} %get-tuple-element.40), channel_id=1, source_target_pairs={{0,3},{1,2},{2,1},{3,0},{4,7},{5,6},{6,5},{7,4},{8,11},{9,10},{10,... | collective-permute-start | bytes 3538952 | tf_op jit(solution)/shard_map/ppermute | solution.py:362

commit v6 on v5

--- a/solution.py
+++ b/solution.py
@@ -131,46 +131,50 @@
     return tokens + block * (rows // LANES)
 
 
-def pack_kernel(half_steps, meta_ref, pos_ref, low_ref, high_ref, rows_ref):
+def pack_kernel(half_steps, meta_ref, pos_ref, low_ref, high_ref, rows_ref, block_ref, sem):
     step = pl.program_id(0)
     experts = rows_ref.shape[0]
     tokens = 2 * half_steps * PACK_ROWS
 
+    def fetch(half_ref, n, slot):
+        return pltpu.make_async_copy(half_ref.at[pl.ds(n * PACK_ROWS, PACK_ROWS), :], block_ref.at[slot], sem.at[slot])
+
     @pl.when(step == 0)
     def _():
+        for h, half_ref in enumerate((low_ref, high_ref)):
+            for n in range(half_steps):
+                fetch(half_ref, n, h * half_steps + n).start()
         rows_ref[...] = jnp.zeros_like(rows_ref)
 
-    def pack(block_ref):
-        sublane = lax.broadcasted_iota(I32, (PACK_WIN, PACK_ROWS), 0)
-        spans, slots = [], []
-        for e in range(experts):
-            begin = meta_ref[e, mark(tokens, PACK_ROWS, step)]
-            base = (begin // 16) * 16
-            spans.append((base, meta_ref[e, mark(tokens, PACK_ROWS, step + 1)] - base))
-            slots.append(jnp.broadcast_to(pos_ref[e:e + 1, :], (PACK_WIN, PACK_ROWS)))
-
-        def onehot(e, at):
-            return (slots[e] - at == sublane).astype(F32)
-
-        def put(e, at, picked):
-            head, body = pl.ds(pl.multiple_of(at, 16), 16), pl.ds(pl.multiple_of(at + 16, 16), PACK_WIN - 16)
-            rows_ref[e, head, :] = (rows_ref[e, head, :].astype(F32) + picked[:16]).astype(BF16)
-            rows_ref[e, body, :] = picked[16:].astype(BF16)
-
-        joined = jnp.concatenate([onehot(e, spans[e][0]) for e in range(experts)], axis=0).astype(BF16)
-        picked = jnp.dot(joined, block_ref[...], preferred_element_type=F32)
-        for e in range(experts):
-            put(e, spans[e][0], picked[e * PACK_WIN:(e + 1) * PACK_WIN])
-
-            def window(w, carry):
-                at = spans[e][0] + w * PACK_WIN
-                put(e, at, jnp.dot(onehot(e, at).astype(BF16), block_ref[...], preferred_element_type=F32))
-                return carry
-
-            lax.fori_loop(1, (spans[e][1] + PACK_WIN - 1) // PACK_WIN, window, 0)
-
-    pl.when(step < half_steps)(lambda: pack(low_ref))
-    pl.when(step >= half_steps)(lambda: pack(high_ref))
+    fetch(low_ref, 0, step).wait()
+    taken_ref = block_ref.at[step]
+    sublane = lax.broadcasted_iota(I32, (PACK_WIN, PACK_ROWS), 0)
+    spans, slots = [], []
+    for e in range(experts):
+        begin = meta_ref[e, mark(tokens, PACK_ROWS, step)]
+        base = (begin // 16) * 16
+        spans.append((base, meta_ref[e, mark(tokens, PACK_ROWS, step + 1)] - base))
+        slots.append(jnp.broadcast_to(pos_ref[e:e + 1, :], (PACK_WIN, PACK_ROWS)))
+
+    def onehot(e, at):
+        return (slots[e] - at == sublane).astype(F32)
+
+    def put(e, at, picked):
+        head, body = pl.ds(pl.multiple_of(at, 16), 16), pl.ds(pl.multiple_of(at + 16, 16), PACK_WIN - 16)
+        rows_ref[e, head, :] = (rows_ref[e, head, :].astype(F32) + picked[:16]).astype(BF16)
+        rows_ref[e, body, :] = picked[16:].astype(BF16)
+
+    joined = jnp.concatenate([onehot(e, spans[e][0]) for e in range(experts)], axis=0).astype(BF16)
+    picked = jnp.dot(joined, taken_ref[...], preferred_element_type=F32)
+    for e in range(experts):
+        put(e, spans[e][0], picked[e * PACK_WIN:(e + 1) * PACK_WIN])
+
+        def window(w, carry):
+            at = spans[e][0] + w * PACK_WIN
+            put(e, at, jnp.dot(onehot(e, at).astype(BF16), taken_ref[...], preferred_element_type=F32))
+            return carry
+
+        lax.fori_loop(1, (spans[e][1] + PACK_WIN - 1) // PACK_WIN, window, 0)
 
 
 def pack_call(meta, low, high, capacity):
@@ -184,9 +188,10 @@
             num_scalar_prefetch=1,
             grid=(2 * half_steps,),
             in_specs=[pl.BlockSpec((experts, PACK_ROWS), lambda i, s: (0, i)),
-                      pl.BlockSpec((PACK_ROWS, width), lambda i, s: (jnp.minimum(i, half_steps - 1), 0)),
-                      pl.BlockSpec((PACK_ROWS, width), lambda i, s: (jnp.maximum(i - half_steps, 0), 0))],
+                      pl.BlockSpec(memory_space=pl.ANY), pl.BlockSpec(memory_space=pl.ANY)],
             out_specs=pl.BlockSpec((experts, padded, width), lambda i, s: (0, 0, 0)),
+            scratch_shapes=[pltpu.VMEM((2 * half_steps, PACK_ROWS, width), BF16),
+                            pltpu.SemaphoreType.DMA((2 * half_steps,))],
         ),
         out_shape=jax.ShapeDtypeStruct((experts, padded, width), BF16),
         compiler_params=pltpu.CompilerParams(vmem_limit_bytes=VMEM_LIMIT),

time: 936 us -> 932 us (level)
  no operation moved by 1% of the time
where the time goes in v6:
time: 932 us; the launch traced here: 925 us
  Pallas kernels  539 us (58%)
  waiting for transfers between devices  321 us (34%)
  starting transfers between devices  59.5 us (6%)
    pallas_call x6, Pallas kernels, mlp_call(): pl.pallas_call(functools.partial(mlp_kernel, begin, tile_rows, tokens, fi...  425 us
    ppermute x21, waiting for transfers between devices, swap(): lax.ppermute(array, 'ep', [(i, i ^ distance) for i in range(group_size)])  321 us
    ppermute x21, starting transfers between devices, swap(): lax.ppermute(array, 'ep', [(i, i ^ distance) for i in range(group_size)])  59.5 us
    pallas_call x4, Pallas kernels, pack_call(): pl.pallas_call(functools.partial(pack_kernel, half_steps), grid_spec=pltp...  47.2 us
    pallas_call x2, Pallas kernels, mix_call(): pl.pallas_call(functools.partial(mix_kernel, columns, starts_at, capacity...  44.2 us
  transfers between devices with their start and end apart: 21, of which 3 were waited for; matrix products, arithmetic and copies ran while one was open for 1% of the time, Pallas kernels for 55%

profile of v6, /device:TPU:0, one launch (start us, length us, event | category | flops | bytes accessed | tf_op | source)
XLA Modules:
  0.0 925.1 jit_solution(18270863138916523734)
XLA Ops:
  0.0 6.7 norm.2.u_ref.low_ref
  7.5 2.5 collective-permute-start.6
  9.9 6.7 norm.3.u_ref.high_ref
  16.8 1.6 route.1
  18.8 11.8 %pack.4.refs_2_.refs_4_ = bf16[2,768,2304]{2,1,0:T(8,128)(2,1)} custom-call(s32[2,2176]{1,0:T(2,128)} %get-tuple-element.27.meta_ref.pos_ref.refs_0_, s32[2,2176]{1,0:T(2,128)} %get-tuple-element.27.meta_ref.pos_ref.refs_0_, bf16[1024,2304]{1,0:T(8,128)(2,1)} %norm.2.u_ref.low_ref, bf16[1024,2304]{1,0:T(8,128)(2,1)} %norm.3.u_ref.high_ref), custom_call_target="tpu_custom_call" | custom-call | flops 2415919104 | bytes 28311552 | tf_op jit(solution)/shard_map/pack/pallas_call | solution.py:185
  30.6 2.0 collective-permute-start.4
  32.7 80.2 %collective-permute-done.6.low_ref = bf16[1024,2304]{1,0:T(8,128)(2,1)} collective-permute-done((bf16[1024,2304]{1,0:T(8,128)(2,1)}, bf16[1024,2304]{1,0:T(8,128)(2,1)}, u32[]{:S(2)}, u32[]{:S(2)}) %collective-permute-start.6) | collective-permute-done | bytes 4718624 | tf_op jit(solution)/shard_map/ppermute | solution.py:367
  112.9 101.1 %collective-permute-done.7.high_ref = bf16[1024,2304]{1,0:T(8,128)(2,1)} collective-permute-done((bf16[1024,2304]{1,0:T(8,128)(2,1)}, bf16[1024,2304]{1,0:T(8,128)(2,1)}, u32[]{:S(2)}, u32[]{:S(2)}) %collective-permute-start.7) | collective-permute-done | bytes 4718624 | tf_op jit(solution)/shard_map/ppermute | solution.py:367
  214.0 11.7 %pack.5.refs_3_.refs_5_ = bf16[2,768,2304]{2,1,0:T(8,128)(2,1)} custom-call(s32[2,2176]{1,0:T(2,128)} %collective-permute-done.meta_ref.pos_ref.refs_1_, s32[2,2176]{1,0:T(2,128)} %collective-permute-done.meta_ref.pos_ref.refs_1_, bf16[1024,2304]{1,0:T(8,128)(2,1)} %collective-permute-done.1.low_ref, bf16[1024,2304]{1,0:T(8,128)(2,1)} %collective-permute-done.2.high_ref), custom_call_target="tpu_custom_call" | custom-call | flops 2415919104 | bytes 28311552 | tf_op jit(solution)/shard_map/pack/pallas_call | solution.py:185
  225.8 190.1 %mlp.6 = (bf16[2,512,2304]{2,1,0:T(8,128)(2,1)}, bf16[2,512,2304]{2,1,0:T(8,128)(2,1)}) custom-call(s32[2,2176]{1,0:T(2,128)} %get-tuple-element.27.meta_ref.pos_ref.refs_0_, s32[2,2176]{1,0:T(2,128)} %collective-permute-done.meta_ref.pos_ref.refs_1_, bf16[2,768,2304]{2,1,0:T(8,128)(2,1)} %pack.4.refs_2_.refs_4_, bf16[2,768,2304]{2,1,0:T(8,128)(2,1)} %pack.5.refs_3_.refs_5_, ...), custom_call_target="tpu_custom_call" | custom-call | flops 163074539520 | bytes 159252480 | tf_op jit(solution)/shard_map/mlp/pallas_call | solution.py:279
  416.4 11.9 %pack.6.refs_6_.refs_2_ = bf16[2,768,2304]{2,1,0:T(8,128)(2,1)} custom-call(s32[2,2176]{1,0:T(2,128)} %collective-permute-done.4.meta_ref.pos_ref.refs_2_.refs_0_, s32[2,2176]{1,0:T(2,128)} %collective-permute-done.4.meta_ref.pos_ref.refs_2_.refs_0_, bf16[1024,2304]{1,0:T(8,128)(2,1)} %collective-permute-done.6.low_ref, ...), custom_call_target="tpu_custom_call" | custom-call | flops 2415919104 | bytes 28311552 | tf_op jit(solution)/shard_map/pack/pallas_call | solution.py:185
  428.3 11.7 %pack.7.refs_7_.refs_3_ = bf16[2,768,2304]{2,1,0:T(8,128)(2,1)} custom-call(s32[2,2176]{1,0:T(2,128)} %collective-permute-done.5.meta_ref.pos_ref.refs_3_.refs_1_, s32[2,2176]{1,0:T(2,128)} %collective-permute-done.5.meta_ref.pos_ref.refs_3_.refs_1_, bf16[1024,2304]{1,0:T(8,128)(2,1)} %collective-permute-done.8.low_ref, ...), custom_call_target="tpu_custom_call" | custom-call | flops 2415919104 | bytes 28311552 | tf_op jit(solution)/shard_map/pack/pallas_call | solution.py:185
  440.1 13.0 %mlp.7 = (bf16[2,128,2304]{2,1,0:T(8,128)(2,1)}, bf16[2,128,2304]{2,1,0:T(8,128)(2,1)}, bf16[2,128,2304]{2,1,0:T(8,128)(2,1)}, bf16[2,128,2304]{2,1,0:T(8,128)(2,1)}) custom-call(s32[2,2176]{1,0:T(2,128)} %get-tuple-element.27.meta_ref.pos_ref.refs_0_, s32[2,2176]{1,0:T(2,128)} %collective-permute-done.meta_ref.pos_ref.refs_1_, ...), custom_call_target="tpu_custom_call" | custom-call | flops 81537269760 | bytes 159252480 | tf_op jit(solution)/shard_map/mlp/pallas_call | solution.py:279
  453.1 45.9 %collective-permute-start.15 = (bf16[2,128,2304]{2,1,0:T(8,128)(2,1)}, bf16[2,128,2304]{2,1,0:T(8,128)(2,1)}, u32[]{:S(2)}, u32[]{:S(2)}) collective-permute-start(bf16[2,128,2304]{2,1,0:T(8,128)(2,1)} %get-tuple-element.39), channel_id=1, source_target_pairs={{0,2},{1,3},{2,0},{3,1},{4,6},{5,7},{6,4},{7,5},{8,10},{9,11},{10,... | collective-permute-start | bytes 3538952 | tf_op jit(solution)/shard_map/ppermute | solution.py:367
  499.0 32.8 %mlp.10 = (bf16[1,128,2304]{2,1,0:T(8,128)(2,1)}, bf16[1,128,2304]{2,1,0:T(8,128)(2,1)}) custom-call(s32[2,2176]{1,0:T(2,128)} %collective-permute-done.4.meta_ref.pos_ref.refs_2_.refs_0_, s32[2,2176]{1,0:T(2,128)} %collective-permute-done.5.meta_ref.pos_ref.refs_3_.refs_1_, bf16[2,768,2304]{2,1,0:T(8,128)(2,1)} %pack.6.refs_6_.refs_2_, ...), custom_call_target="tpu_custom_call" | custom-call | flops 20384317440 | bytes 79626240 | tf_op jit(solution)/shard_map/mlp/pallas_call | solution.py:279
  532.9 77.9 %mlp.8 = (bf16[2,192,2304]{2,1,0:T(8,128)(2,1)}, bf16[2,192,2304]{2,1,0:T(8,128)(2,1)}) custom-call(s32[2,2176]{1,0:T(2,128)} %collective-permute-done.4.meta_ref.pos_ref.refs_2_.refs_0_, s32[2,2176]{1,0:T(2,128)} %collective-permute-done.5.meta_ref.pos_ref.refs_3_.refs_1_, bf16[2,768,2304]{2,1,0:T(8,128)(2,1)} %pack.6.refs_6_.refs_2_, ...), custom_call_target="tpu_custom_call" | custom-call | flops 61152952320 | bytes 159252480 | tf_op jit(solution)/shard_map/mlp/pallas_call | solution.py:279
  610.8 33.1 %mlp.11 = (bf16[1,128,2304]{2,1,0:T(8,128)(2,1)}, bf16[1,128,2304]{2,1,0:T(8,128)(2,1)}) custom-call(s32[2,2176]{1,0:T(2,128)} %collective-permute-done.4.meta_ref.pos_ref.refs_2_.refs_0_, s32[2,2176]{1,0:T(2,128)} %collective-permute-done.5.meta_ref.pos_ref.refs_3_.refs_1_, bf16[2,768,2304]{2,1,0:T(8,128)(2,1)} %pack.6.refs_6_.refs_2_, ...), custom_call_target="tpu_custom_call" | custom-call | flops 20384317440 | bytes 79626240 | tf_op jit(solution)/shard_map/mlp/pallas_call | solution.py:279
  644.9 1.5 collective-permute-start.20
  646.3 77.8 %mlp.9 = (bf16[2,192,2304]{2,1,0:T(8,128)(2,1)}, bf16[2,192,2304]{2,1,0:T(8,128)(2,1)}) custom-call(s32[2,2176]{1,0:T(2,128)} %collective-permute-done.4.meta_ref.pos_ref.refs_2_.refs_0_, s32[2,2176]{1,0:T(2,128)} %collective-permute-done.5.meta_ref.pos_ref.refs_3_.refs_1_, bf16[2,768,2304]{2,1,0:T(8,128)(2,1)} %pack.6.refs_6_.refs_2_, ...), custom_call_target="tpu_custom_call" | custom-call | flops 61152952320 | bytes 159252480 | tf_op jit(solution)/shard_map/mlp/pallas_call | solution.py:279
  731.3 3.9 gate.3
  735.2 3.9 gate.2
  741.1 21.9 %mix.2.base_ref = f32[2048,2304]{1,0:T(8,128)} custom-call(s32[8,128]{1,0:T(8,128)} %slice.6.start_ref, bf16[2048,2304]{1,0:T(8,128)(2,1)} %base_ref.1, s32[2048,8]{1,0:T(8,128)} %bitcast.7, f32[2048,8]{1,0:T(8,128)} %bitcast.9, bf16[2,512,2304]{2,1,0:T(8,128)(2,1)} %get-tuple-element.29.rest_0_, bf16[2,512,2304]{2,1,0:T(8,128)(2,1)} %collective-permute-done.3.rest_1_, ...), custom_call_target="tpu_custom_call" | custom-call | flops 9663676416 | bytes 47185920 | tf_op jit(solution)/shard_map/mix/pallas_call | solution.py:345
  763.1 139.4 %collective-permute-done.16.rest_5_ = bf16[2,128,2304]{2,1,0:T(8,128)(2,1)} collective-permute-done((bf16[2,128,2304]{2,1,0:T(8,128)(2,1)}, bf16[2,128,2304]{2,1,0:T(8,128)(2,1)}, u32[]{:S(2)}, u32[]{:S(2)}) %collective-permute-start.16) | collective-permute-done | bytes 1179680 | tf_op jit(solution)/shard_map/ppermute | solution.py:367
  902.5 22.3 %mix.3 = bf16[2048,2304]{1,0:T(8,128)(2,1)} custom-call(s32[8,128]{1,0:T(8,128)} %slice.6.start_ref, f32[2048,2304]{1,0:T(8,128)} %mix.2.base_ref, s32[2048,8]{1,0:T(8,128)} %bitcast.8, f32[2048,8]{1,0:T(8,128)} %bitcast.10, bf16[2,192,2304]{2,1,0:T(8,128)(2,1)} %collective-permute-done.11.rest_0_, bf16[2,192,2304]{2,1,0:T(8,128)(2,1)} %collective-permute-done.12.rest_1_, ...), custom_call_target="tpu_custom_call" | custom-call | flops 9663676416 | bytes 47185920 | tf_op jit(solution)/shard_map/mix/pallas_call | solution.py:345
  (40 shorter events, 13.2 us)
Async XLA Ops:
  6.7 25.9 %collective-permute-start.1 = (bf16[1024,2304]{1,0:T(8,128)(2,1)}, bf16[1024,2304]{1,0:T(8,128)(2,1)}, u32[]{:S(2)}, u32[]{:S(2)}) collective-permute-start(bf16[1024,2304]{1,0:T(8,128)(2,1)} %norm.2.u_ref.low_ref), channel_id=1, source_target_pairs={{0,1},{1,0},{2,3},{3,2},{4,5},{5,4},{6,7},{7,6},{8,9},{9,8},{10,11... | collective-permute-start | bytes 14155784 | tf_op jit(solution)/shard_map/ppermute | solution.py:367
  7.5 105.5 %collective-permute-start.6 = (bf16[1024,2304]{1,0:T(8,128)(2,1)}, bf16[1024,2304]{1,0:T(8,128)(2,1)}, u32[]{:S(2)}, u32[]{:S(2)}) collective-permute-start(bf16[1024,2304]{1,0:T(8,128)(2,1)} %norm.2.u_ref.low_ref), channel_id=1, source_target_pairs={{0,2},{1,3},{2,0},{3,1},{4,6},{5,7},{6,4},{7,5},{8,10},{9,11},{10,... | collective-permute-start | bytes 14155784 | tf_op jit(solution)/shard_map/ppermute | solution.py:367
  16.6 197.4 %collective-permute-start.7 = (bf16[1024,2304]{1,0:T(8,128)(2,1)}, bf16[1024,2304]{1,0:T(8,128)(2,1)}, u32[]{:S(2)}, u32[]{:S(2)}) collective-permute-start(bf16[1024,2304]{1,0:T(8,128)(2,1)} %norm.3.u_ref.high_ref), channel_id=1, source_target_pairs={{0,2},{1,3},{2,0},{3,1},{4,6},{5,7},{6,4},{7,5},{8,10},{9,11},{10,... | collective-permute-start | bytes 14155784 | tf_op jit(solution)/shard_map/ppermute | solution.py:367
  16.6 197.4 %collective-permute-start.2 = (bf16[1024,2304]{1,0:T(8,128)(2,1)}, bf16[1024,2304]{1,0:T(8,128)(2,1)}, u32[]{:S(2)}, u32[]{:S(2)}) collective-permute-start(bf16[1024,2304]{1,0:T(8,128)(2,1)} %norm.3.u_ref.high_ref), channel_id=1, source_target_pairs={{0,1},{1,0},{2,3},{3,2},{4,5},{5,4},{6,7},{7,6},{8,9},{9,8},{10,11... | collective-permute-start | bytes 14155784 | tf_op jit(solution)/shard_map/ppermute | solution.py:367
  18.5 12.2 %collective-permute-start = (s32[2,2176]{1,0:T(2,128)}, s32[2,2176]{1,0:T(2,128)}, u32[]{:S(2)}, u32[]{:S(2)}) collective-permute-start(s32[2,2176]{1,0:T(2,128)} %get-tuple-element.28), channel_id=1, source_target_pairs={{0,1},{1,0},{2,3},{3,2},{4,5},{5,4},{6,7},{7,6},{8,9},{9,8},{10,11... | collective-permute-start | bytes 52232 | tf_op jit(solution)/shard_map/ppermute | solution.py:367
  30.6 385.7 %collective-permute-start.4 = (s32[2,2176]{1,0:T(2,128)}, s32[2,2176]{1,0:T(2,128)}, u32[]{:S(2)}, u32[]{:S(2)}) collective-permute-start(s32[2,2176]{1,0:T(2,128)} %get-tuple-element.31), channel_id=1, source_target_pairs={{0,2},{1,3},{2,0},{3,1},{4,6},{5,7},{6,4},{7,5},{8,10},{9,11},{10,... | collective-permute-start | bytes 52232 | tf_op jit(solution)/shard_map/ppermute | solution.py:367
  32.7 395.6 %collective-permute-start.5 = (s32[2,2176]{1,0:T(2,128)}, s32[2,2176]{1,0:T(2,128)}, u32[]{:S(2)}, u32[]{:S(2)}) collective-permute-start(s32[2,2176]{1,0:T(2,128)} %get-tuple-element.32), channel_id=1, source_target_pairs={{0,3},{1,2},{2,1},{3,0},{4,7},{5,6},{6,5},{7,4},{8,11},{9,10},{10,... | collective-permute-start | bytes 52232 | tf_op jit(solution)/shard_map/ppermute | solution.py:367
  112.9 315.4 %collective-permute-start.8 = (bf16[1024,2304]{1,0:T(8,128)(2,1)}, bf16[1024,2304]{1,0:T(8,128)(2,1)}, u32[]{:S(2)}, u32[]{:S(2)}) collective-permute-start(bf16[1024,2304]{1,0:T(8,128)(2,1)} %collective-permute-done.6.low_ref), channel_id=1, source_target_pairs={{0,1},{1,0},{2,3},{3,2},{4,5},{5,4},{6,7},{7,6},{8,9},{9,8},{10,11... | collective-permute-start | bytes 14155784 | tf_op jit(solution)/shard_map/ppermute | solution.py:367
  214.0 214.3 %collective-permute-start.9 = (bf16[1024,2304]{1,0:T(8,128)(2,1)}, bf16[1024,2304]{1,0:T(8,128)(2,1)}, u32[]{:S(2)}, u32[]{:S(2)}) collective-permute-start(bf16[1024,2304]{1,0:T(8,128)(2,1)} %collective-permute-done.7.high_ref), channel_id=1, source_target_pairs={{0,1},{1,0},{2,3},{3,2},{4,5},{5,4},{6,7},{7,6},{8,9},{9,8},{10,11... | collective-permute-start | bytes 14155784 | tf_op jit(solution)/shard_map/ppermute | solution.py:367
  415.9 228.1 %collective-permute-start.3 = (bf16[2,512,2304]{2,1,0:T(8,128)(2,1)}, bf16[2,512,2304]{2,1,0:T(8,128)(2,1)}, u32[]{:S(2)}, u32[]{:S(2)}) collective-permute-start(bf16[2,512,2304]{2,1,0:T(8,128)(2,1)} %get-tuple-element.30), channel_id=1, source_target_pairs={{0,1},{1,0},{2,3},{3,2},{4,5},{5,4},{6,7},{7,6},{8,9},{9,8},{10,11... | collective-permute-start | bytes 14155784 | tf_op jit(solution)/shard_map/ppermute | solution.py:367
  453.1 273.1 %collective-permute-start.10 = (bf16[2,128,2304]{2,1,0:T(8,128)(2,1)}, bf16[2,128,2304]{2,1,0:T(8,128)(2,1)}, u32[]{:S(2)}, u32[]{:S(2)}) collective-permute-start(bf16[2,128,2304]{2,1,0:T(8,128)(2,1)} %get-tuple-element.34), channel_id=1, source_target_pairs={{0,1},{1,0},{2,3},{3,2},{4,5},{5,4},{6,7},{7,6},{8,9},{9,8},{10,11... | collective-permute-start | bytes 3538952 | tf_op jit(solution)/shard_map/ppermute | solution.py:367
  453.1 274.5 %collective-permute-start.15 = (bf16[2,128,2304]{2,1,0:T(8,128)(2,1)}, bf16[2,128,2304]{2,1,0:T(8,128)(2,1)}, u32[]{:S(2)}, u32[]{:S(2)}) collective-permute-start(bf16[2,128,2304]{2,1,0:T(8,128)(2,1)} %get-tuple-element.39), channel_id=1, source_target_pairs={{0,2},{1,3},{2,0},{3,1},{4,6},{5,7},{6,4},{7,5},{8,10},{9,11},{10,... | collective-permute-start | bytes 3538952 | tf_op jit(solution)/shard_map/ppermute | solution.py:367
  531.8 113.0 %collective-permute-start.17 = (bf16[1,128,2304]{2,1,0:T(8,128)(2,1)}, bf16[1,128,2304]{2,1,0:T(8,128)(2,1)}, u32[]{:S(2)}, u32[]{:S(2)}) collective-permute-start(bf16[1,128,2304]{2,1,0:T(8,128)(2,1)} %get-tuple-element.41), channel_id=1, source_target_pairs={{0,2},{1,3},{2,0},{3,1},{4,6},{5,7},{6,4},{7,5},{8,10},{9,11},{10,... | collective-permute-start | bytes 1769480 | tf_op jit(solution)/shard_map/ppermute | solution.py:367
  531.8 192.3 %collective-permute-start.18 = (bf16[1,128,2304]{2,1,0:T(8,128)(2,1)}, bf16[1,128,2304]{2,1,0:T(8,128)(2,1)}, u32[]{:S(2)}, u32[]{:S(2)}) collective-permute-start(bf16[1,128,2304]{2,1,0:T(8,128)(2,1)} %get-tuple-element.42), channel_id=1, source_target_pairs={{0,3},{1,2},{2,1},{3,0},{4,7},{5,6},{6,5},{7,4},{8,11},{9,10},{10,... | collective-permute-start | bytes 1769480 | tf_op jit(solution)/shard_map/ppermute | solution.py:367
  643.9 80.5 %collective-permute-start.19 = (bf16[1,128,2304]{2,1,0:T(8,128)(2,1)}, bf16[1,128,2304]{2,1,0:T(8,128)(2,1)}, u32[]{:S(2)}, u32[]{:S(2)}) collective-permute-start(bf16[1,128,2304]{2,1,0:T(8,128)(2,1)} %get-tuple-element.43), channel_id=1, source_target_pairs={{0,2},{1,3},{2,0},{3,1},{4,6},{5,7},{6,4},{7,5},{8,10},{9,11},{10,... | collective-permute-start | bytes 1769480 | tf_op jit(solution)/shard_map/ppermute | solution.py:367
  644.9 80.4 %collective-permute-start.20 = (bf16[1,128,2304]{2,1,0:T(8,128)(2,1)}, bf16[1,128,2304]{2,1,0:T(8,128)(2,1)}, u32[]{:S(2)}, u32[]{:S(2)}) collective-permute-start(bf16[1,128,2304]{2,1,0:T(8,128)(2,1)} %get-tuple-element.44), channel_id=1, source_target_pairs={{0,3},{1,2},{2,1},{3,0},{4,7},{5,6},{6,5},{7,4},{8,11},{9,10},{10,... | collective-permute-start | bytes 1769480 | tf_op jit(solution)/shard_map/ppermute | solution.py:367
  724.1 178.4 %collective-permute-start.11 = (bf16[2,192,2304]{2,1,0:T(8,128)(2,1)}, bf16[2,192,2304]{2,1,0:T(8,128)(2,1)}, u32[]{:S(2)}, u32[]{:S(2)}) collective-permute-start(bf16[2,192,2304]{2,1,0:T(8,128)(2,1)} %get-tuple-element.35), channel_id=1, source_target_pairs={{0,2},{1,3},{2,0},{3,1},{4,6},{5,7},{6,4},{7,5},{8,10},{9,11},{10,... | collective-permute-start | bytes 5308424 | tf_op jit(solution)/shard_map/ppermute | solution.py:367
  724.4 178.1 %collective-permute-start.12 = (bf16[2,192,2304]{2,1,0:T(8,128)(2,1)}, bf16[2,192,2304]{2,1,0:T(8,128)(2,1)}, u32[]{:S(2)}, u32[]{:S(2)}) collective-permute-start(bf16[2,192,2304]{2,1,0:T(8,128)(2,1)} %get-tuple-element.36), channel_id=1, source_target_pairs={{0,3},{1,2},{2,1},{3,0},{4,7},{5,6},{6,5},{7,4},{8,11},{9,10},{10,... | collective-permute-start | bytes 5308424 | tf_op jit(solution)/shard_map/ppermute | solution.py:367
  725.2 177.3 %collective-permute-start.13 = (bf16[2,192,2304]{2,1,0:T(8,128)(2,1)}, bf16[2,192,2304]{2,1,0:T(8,128)(2,1)}, u32[]{:S(2)}, u32[]{:S(2)}) collective-permute-start(bf16[2,192,2304]{2,1,0:T(8,128)(2,1)} %get-tuple-element.37), channel_id=1, source_target_pairs={{0,2},{1,3},{2,0},{3,1},{4,6},{5,7},{6,4},{7,5},{8,10},{9,11},{10,... | collective-permute-start | bytes 5308424 | tf_op jit(solution)/shard_map/ppermute | solution.py:367
  726.2 176.4 %collective-permute-start.14 = (bf16[2,192,2304]{2,1,0:T(8,128)(2,1)}, bf16[2,192,2304]{2,1,0:T(8,128)(2,1)}, u32[]{:S(2)}, u32[]{:S(2)}) collective-permute-start(bf16[2,192,2304]{2,1,0:T(8,128)(2,1)} %get-tuple-element.38), channel_id=1, source_target_pairs={{0,3},{1,2},{2,1},{3,0},{4,7},{5,6},{6,5},{7,4},{8,11},{9,10},{10,... | collective-permute-start | bytes 5308424 | tf_op jit(solution)/shard_map/ppermute | solution.py:367
  727.6 174.9 %collective-permute-start.16 = (bf16[2,128,2304]{2,1,0:T(8,128)(2,1)}, bf16[2,128,2304]{2,1,0:T(8,128)(2,1)}, u32[]{:S(2)}, u32[]{:S(2)}) collective-permute-start(bf16[2,128,2304]{2,1,0:T(8,128)(2,1)} %get-tuple-element.40), channel_id=1, source_target_pairs={{0,3},{1,2},{2,1},{3,0},{4,7},{5,6},{6,5},{7,4},{8,11},{9,10},{10,... | collective-permute-start | bytes 3538952 | tf_op jit(solution)/shard_map/ppermute | solution.py:367
